TPU v7x, 512 devices: a whole 4x8x8 slice. The times are simulated.
512 devices in a mesh: replica: 32 (over z, x_hi, core), shard: 16 (over y, x_lo).
Axes of the slice: x: 4 (x_hi: 2, x_lo: 2; x = x_hi * 2 + x_lo), y: 8, z: 8, core: 2. Of those that a mesh axis runs over, the one named last changes fastest.
Arguments:
- local_weights: bfloat16 [32, 8192, 512], P('replica', 'shard'), may hold values from -1.3258252 to 1.3258252
- outer_base: bfloat16 [8192, 512], P('shard'), may hold values from -0.0625 to 0.0625
- momentum: bfloat16 [8192, 512], P('shard', 'replica'), may hold values from -0.06591797 to 0.06591797
- error_feedback: bfloat16 [32, 8192, 512], P('replica', 'shard'), may hold values from -0.032958984 to 0.032958984
- q_start: float32 [512, 32], replicated, may hold values from -6 to 6
- tokens: bfloat16 [32, 2048, 8192], P('replica', None, 'shard'), may hold values from -6 to 6
Outputs:
- new_base: bfloat16 [8192, 512], P('shard')
- new_momentum: bfloat16 [8192, 512], P('shard', 'replica')
- new_error: bfloat16 [32, 8192, 512], P('replica', 'shard')
- key_rows: bfloat16 [32, 2048, 512], P('replica', 'shard')
All inputs are finite; a program needn't handle non-finite values.
Results may differ from a plain program's by a relative error of at most 0.0065.
Values may be sent and summed in bfloat16 or wider, within the bound.
No kernel may reach another device: no remote copies, remote signals or barrier semaphores. Data moves between devices by JAX's collectives and lax.ppermute only.
A program may use at most 64 MiB of HBM per device.

v0:
```python
import jax
import jax.numpy as jnp
from jax import lax
from jax.sharding import PartitionSpec as P

outer_mu = 0.9
outer_rate = 0.7


def laid_out(tiles, dim):
    tiles = jnp.moveaxis(tiles, 0, dim)
    dims = tiles.shape
    return tiles.reshape(*dims[:dim], dims[dim] * dims[dim + 1], *dims[dim + 2 :])


def copy_for_each(x, axis):
    copies = jnp.broadcast_to(x, (lax.axis_size(axis), *x.shape))
    return lax.all_to_all(copies, axis, split_axis=0, concat_axis=0, tiled=True)


def collect(x, axis, dim):
    return laid_out(copy_for_each(x, axis), dim)


def taken_together(x, axis):
    everything = copy_for_each(x, axis)
    return jnp.sum(everything, axis=0)


def together(arrays, axis):
    ends = [0]
    for a in arrays:
        ends.append(ends[-1] + a.size)
    running = lax.psum(jnp.concatenate([a.ravel() for a in arrays]), axis)
    return tuple((running[b:e].reshape(a.shape) for a, b, e in zip(arrays, ends, ends[1:])))


def split_up(x, dim, peers):
    before, after = (x.shape[:dim], x.shape[dim + 1 :])
    return jnp.moveaxis(x.reshape(*before, peers, -1, *after), dim, 0)


def sum_at_owner(x, axis, dim):
    peers = lax.axis_size(axis)
    tiles = lax.all_to_all(split_up(x, dim, peers), axis, 0, 0, tiled=True)
    return jnp.sum(tiles.astype(jnp.float32), axis=0)


def on_device(local_weights, outer_base, momentum, error_feedback, q_start, tokens):
    highest = lax.Precision.HIGHEST
    replicas = lax.axis_size("replica")
    own_columns = momentum.shape[1]
    full_momentum = collect(momentum, "replica", 1)
    pseudo = (
        outer_base.astype(jnp.float32)
        - local_weights[0].astype(jnp.float32)
        + error_feedback[0].astype(jnp.float32)
    )
    p_local = jnp.dot(pseudo, q_start, precision=highest)
    p_mean = taken_together(p_local, "replica") / replicas
    own_gram = jnp.dot(p_mean.T, p_mean, precision=highest)
    q_raw = jnp.dot(pseudo.T, p_mean, precision=highest)
    q_sum, gram_sum = together((q_raw, own_gram / replicas), ("replica", "shard"))
    factor_low = jnp.linalg.cholesky(gram_sum)
    basis = jax.scipy.linalg.solve_triangular(factor_low, p_mean.T, lower=True).T
    q_mean = jax.scipy.linalg.solve_triangular(factor_low, q_sum.T, lower=True).T / replicas
    update = jnp.dot(basis, q_mean.T, precision=highest)
    new_error = (pseudo - update).astype(jnp.bfloat16)[None]
    moment = outer_mu * full_momentum.astype(jnp.float32) + update
    new_base = (outer_base.astype(jnp.float32) - outer_rate * (outer_mu * moment + update)).astype(
        jnp.bfloat16
    )
    first_column = lax.axis_index("replica") * own_columns
    new_momentum = lax.dynamic_slice_in_dim(moment, first_column, own_columns, 1).astype(
        jnp.bfloat16
    )
    own_tokens = tokens[0]
    key_sum = sum_at_owner(
        jnp.dot(own_tokens, new_base, preferred_element_type=jnp.float32).astype(jnp.bfloat16),
        "shard",
        0,
    )
    key_rows = key_sum.astype(jnp.bfloat16)[None]
    return (new_base, new_momentum, new_error, key_rows)


def solution(mesh):
    in_specs = (
        P("replica", "shard", None),
        P("shard", None),
        P("shard", "replica"),
        P("replica", "shard", None),
        P(),
        P("replica", None, "shard"),
    )
    out_specs = (
        P("shard", None),
        P("shard", "replica"),
        P("replica", "shard", None),
        P("replica", "shard", None),
    )
    return jax.shard_map(
        on_device, mesh=mesh, in_specs=in_specs, out_specs=out_specs, check_vma=False
    )
```

profile of v0, /device:TPU:1, one launch (start us, length us, event | category | flops | bytes accessed | tf_op | source)
XLA Modules:
  0.0 438.2 jit_solution(4397631997838453536)
XLA Ops:
  7.2 1.4 copy.35
  8.6 1.3 copy.36
  9.9 2.0 copy.37
  11.9 1.9 fusion.9
  14.1 64.9 %all_to_all.15 = f32[32,512,32]{1,2,0:T(8,128)} all-to-all(f32[32,512,32]{1,2,0:T(8,128)S(1)} %broadcast_in_dim.15), channel_id=1, replica_groups=mesh['replica'=32,'shard'=16] {'replica'}, dimensions={0} | all-to-all | bytes 4194304 | tf_op jit(solution)/shard_map/all_to_all | solution.py:18
  79.0 0.9 broadcast_in_dim.14
  79.9 5.9 %all-to-all-start = ((bf16[32,512,16]{1,2,0:T(8,128)(2,1)}), bf16[32,512,16]{1,2,0:T(8,128)(2,1)}, u32[]{:S(2)}, u32[]{:S(2)}) async-start(bf16[32,512,16]{1,2,0:T(8,128)(2,1)} %broadcast_in_dim.14), calls=%async_computation | async-start | bytes 1048576 | tf_op jit(solution)/shard_map/all_to_all | solution.py:18
  85.8 1.7 reduce_sum.21
  87.6 2.1 fusion.7
  90.7 12.0 %all-to-all-done = bf16[32,512,16]{1,2,0:T(8,128)(2,1)} async-done(((bf16[32,512,16]{1,2,0:T(8,128)(2,1)}), bf16[32,512,16]{1,2,0:T(8,128)(2,1)}, u32[]{:S(2)}, u32[]{:S(2)}) %all-to-all-start) | async-done | bytes 524320 | tf_op jit(solution)/shard_map/all_to_all | solution.py:18
  102.7 2.2 convert_multiply_fusion
  104.8 251.7 %all-reduce.2.cloned.1.call-done = f32[17408]{0:T(1024)} async-done(((f32[17408]{0:T(1024)}), f32[17408]{0:T(1024)}) %all-reduce.2.cloned.1.call-update) | async-done | bytes 69648 | tf_op jit(solution)/shard_map/psum | solution.py:34
  357.4 2.9 cholesky.18
  361.7 2.4 custom-call.7
  364.1 0.9 slice.35
  365.8 3.7 fusion.5
  369.5 1.3 fusion.1
  370.8 1.8 copy.49
  372.6 4.6 %all-to-all-start.2 = ((bf16[16,128,512]{1,2,0:T(8,128)(2,1)}), bf16[16,128,512]{1,2,0:T(8,128)(2,1)}, u32[]{:S(2)}, u32[]{:S(2)}) async-start(bf16[16,128,512]{1,2,0:T(8,128)(2,1)} %bitcast.56), calls=%async_computation.2 | async-start | bytes 4194304 | tf_op jit(solution)/shard_map/all_to_all | solution.py:45
  377.2 1.0 copy.42
  378.2 1.0 copy.43
  379.2 1.3 dynamic-slice_convert_fusion
  380.5 48.2 %all-to-all-done.2 = bf16[16,128,512]{1,2,0:T(8,128)(2,1)} async-done(((bf16[16,128,512]{1,2,0:T(8,128)(2,1)}), bf16[16,128,512]{1,2,0:T(8,128)(2,1)}, u32[]{:S(2)}, u32[]{:S(2)}) %all-to-all-start.2) | async-done | bytes 2097184 | tf_op jit(solution)/shard_map/all_to_all | solution.py:45
  428.7 1.9 reduce_sum.22
  (30 shorter events, 5.0 us)
Async XLA Ops:
  7.2 362.3 %copy-start = (bf16[1,2048,512]{2,1,0:T(8,128)(2,1)S(1)}, bf16[1,2048,512]{2,1,0:T(8,128)(2,1)}, u32[]{:S(2)}) copy-start(bf16[1,2048,512]{2,1,0:T(8,128)(2,1)} %param.13) | copy-start | bytes 6291460
  7.2 4.7 %copy-start.4 = (f32[512,32]{0,1:T(8,128)S(1)}, f32[512,32]{0,1:T(8,128)}, u32[]{:S(2)}) copy-start(f32[512,32]{0,1:T(8,128)} %param.12) | copy-start | bytes 196612
  14.1 64.9 %copy-start.5 = (bf16[512,16]{0,1:T(8,128)(2,1)S(1)}, bf16[512,16]{0,1:T(8,128)(2,1)}, u32[]{:S(2)}) copy-start(bf16[512,16]{0,1:T(8,128)(2,1)} %param.10) | copy-start | bytes 49156
  79.9 22.8 %all-to-all-start = ((bf16[32,512,16]{1,2,0:T(8,128)(2,1)}), bf16[32,512,16]{1,2,0:T(8,128)(2,1)}, u32[]{:S(2)}, u32[]{:S(2)}) async-start(bf16[32,512,16]{1,2,0:T(8,128)(2,1)} %broadcast_in_dim.14), calls=%async_computation | async-start | bytes 1048576 | tf_op jit(solution)/shard_map/all_to_all | solution.py:18
  85.8 270.8 %all-reduce.2.cloned.1.call-start = ((), (), s32[]{:S(2)}) async-start(), calls=%async_computation.3 | async-start | bytes 139264 | tf_op jit(solution)/shard_map/psum | solution.py:34
  369.5 1.3 copy-start.2
  372.6 4.6 %copy-start.3 = (bf16[512,512]{0,1:T(8,128)(2,1)S(1)}, bf16[512,512]{0,1:T(8,128)(2,1)}, u32[]{:S(2)}) copy-start(bf16[512,512]{0,1:T(8,128)(2,1)} %copy-done.2) | copy-start | bytes 1572868
  372.6 5.6 %copy-start.1 = (bf16[1,512,512]{1,2,0:T(8,128)(2,1)S(1)}, bf16[1,512,512]{1,2,0:T(8,128)(2,1)}, u32[]{:S(2)}) copy-start(bf16[1,512,512]{1,2,0:T(8,128)(2,1)} %get-tuple-element.23) | copy-start | bytes 1572868
  372.6 56.1 %all-to-all-start.2 = ((bf16[16,128,512]{1,2,0:T(8,128)(2,1)}), bf16[16,128,512]{1,2,0:T(8,128)(2,1)}, u32[]{:S(2)}, u32[]{:S(2)}) async-start(bf16[16,128,512]{1,2,0:T(8,128)(2,1)} %bitcast.56), calls=%async_computation.2 | async-start | bytes 4194304 | tf_op jit(solution)/shard_map/all_to_all | solution.py:45
Sparse Core Ops, SparseCore 0:
  92.1 264.4 all-reduce.1
where the time goes:
time: 439 us; the launch traced here: 438 us
  waiting for transfers between devices  312 us (71%)
  blocking collectives  64.9 us (15%)
  between operations  14.2 us (3%)
  local copies, waits for them, and re-layouts  13.8 us (3%)
  other arithmetic  13.1 us (3%)
  starting transfers between devices  10.5 us (2%)
  matrix products  9.83 us (2%)
    psum x1, waiting for transfers between devices, together(): running = lax.psum(jnp.concatenate([a.ravel() for a in arrays]), axis)  252 us
    all_to_all x1, blocking collectives, copy_for_each(): return lax.all_to_all(copies, axis, split_axis=0, concat_axis=0, tiled=True)  64.9 us
    all_to_all x1, waiting for transfers between devices, sum_at_owner(): tiles = lax.all_to_all(split_up(x, dim, peers), axis, 0, 0, tiled=True)  48.2 us
    all_to_all x1, waiting for transfers between devices, copy_for_each(): return lax.all_to_all(copies, axis, split_axis=0, concat_axis=0, tiled=True)  12 us
  transfers between devices with their start and end apart: 3, of which 3 were waited for; matrix products, arithmetic and copies ran while one was open for 2% of the time, Pallas kernels for 0%

commit v1 on v0

v1 whole, which is shorter than its diff:
```python
import functools

import jax
import jax.numpy as jnp
from jax import lax
from jax.experimental import pallas as pl
from jax.experimental.pallas import tpu as pltpu
from jax.sharding import Mesh, PartitionSpec as P

outer_mu = 0.9
outer_rate = 0.7
own_mom = outer_rate * outer_mu * outer_mu
own_upd = outer_rate * (outer_mu + 1.0)

chips = ("z", "xh")
peers = ("core", "z", "xh")
shard = ("y2", "y1", "y0", "xl")
f32, bf16 = jnp.float32, jnp.bfloat16
highest = lax.Precision.HIGHEST


def swap(x, axis):
    return lax.ppermute(x, axis, [(0, 1), (1, 0)])


def exchange(x, axis):
    return lax.all_to_all(x, axis, 0, 0, tiled=True)


def copy_for_each(x, axis):
    return exchange(jnp.broadcast_to(x, (lax.axis_size(axis), *x.shape)), axis)


def pick(x, at, dim):
    return lax.dynamic_index_in_dim(x, at, dim, keepdims=False)


def halve(x, axis, dim):
    me = lax.axis_index(axis)
    other = swap(pick(x, 1 - me, dim).astype(bf16), axis)
    return pick(x, me, dim) + other.astype(f32)


def dot(a, b, dims, precision=None):
    return lax.dot_general(
        a, b, (dims, ((), ())), precision=precision, preferred_element_type=f32
    )


def lane_group(shape, rank):
    return lax.broadcasted_iota(jnp.int32, shape, 1) // rank


def moments(first_ref, q_ref, out_ref, *, own, rank, replicas):
    mean = jnp.sum(first_ref[:, :own].astype(f32), axis=0) * (1.0 / replicas)
    p = dot(mean, q_ref[...], ((1,), (0,)), highest)
    group = lane_group(p.shape, rank)
    p_at = [jnp.where(group == i, p, 0.0) for i in range(4)]
    upper = dot(p_at[0], p_at[1], ((0,), (0,)), highest)
    lower = dot(p_at[0], p_at[2], ((0,), (0,)), highest)
    same = p_at[0] + upper[:own] + lower[own : 2 * own]
    q_rows = dot(mean, p_at[3], ((0,), (0,)), highest)
    out_ref[...] = q_rows.reshape(out_ref.shape) + same[None]


def token_products(second_ref, tokens_ref, out_ref, *, own, rank):
    peers_, rows_, lanes = second_ref.shape
    shards = out_ref.shape[0]
    block = tokens_ref.shape[0] // shards
    step = block // 4
    second = second_ref[...]
    sums = jnp.sum(second, axis=0)
    flat = second.reshape(peers_ * rows_, lanes)
    p = jnp.where(lane_group(flat.shape, rank) == 0, flat, 0.0)
    total = jnp.zeros((shards * step, lanes), f32)
    tokens = tokens_ref[...].reshape(shards, 4, step, -1)
    for i in range(4):
        at = pltpu.roll(p, i * rank, 1) if i else p
        high = at.astype(bf16)
        low = (at - high.astype(f32)).astype(bf16)
        part = tokens[:, i].reshape(shards * step, -1)
        total = total + dot(part, high, ((1,), (0,))) + dot(part, low, ((1,), (0,)))
    out_ref[:, :own] = jnp.broadcast_to(sums[None], (shards, own, lanes))
    out_ref[:, own:] = total.reshape(shards, step, lanes)


def key_products(
    at_ref, tokens_ref, base_ref, momentum_ref, sa_ref, ka_ref, sb_ref, kb_ref
):
    xl, y0 = at_ref[0], at_ref[1]
    block, half = sa_ref.shape[1:]
    settled = base_ref[...].astype(f32) - own_mom * momentum_ref[...].astype(f32)
    settled = settled.astype(bf16)
    left, right = settled[:, :half], settled[:, half:]

    def rows(i):
        return tokens_ref[pl.ds(pl.multiple_of(i * block, block), block)]

    for j in range(sa_ref.shape[0]):
        sa_ref[j] = dot(rows(2 * j + 1 - xl), left, ((1,), (0,))).astype(bf16)
        sb_ref[j] = dot(
            rows((j // 2) * 4 + (1 - y0) * 2 + j % 2), right, ((1,), (0,))
        ).astype(bf16)
    for j in range(sa_ref.shape[0]):
        ka_ref[j] = dot(rows(2 * j + xl), left, ((1,), (0,)))
        kb_ref[j] = dot(rows((j // 2) * 4 + y0 * 2 + j % 2), right, ((1,), (0,)))


def in_vmem(kernel, out_shape, n, scalars=0, **cost):
    whole = pl.BlockSpec(memory_space=pltpu.VMEM)
    small = pl.BlockSpec(memory_space=pltpu.SMEM)
    return pl.pallas_call(
        kernel,
        out_shape=out_shape,
        in_specs=[small] * scalars + [whole] * (n - scalars),
        out_specs=jax.tree.map(lambda _: whole, out_shape),
        cost_estimate=pl.CostEstimate(**cost),
    )


def on_device(local_weights, outer_base, momentum, error_feedback, q_start, tokens):
    replicas, shards = lax.axis_size(peers), lax.axis_size(shard)
    rows, kv = outer_base.shape
    rank = q_start.shape[1]
    own = rows // replicas
    cols = kv // replicas
    core = lax.axis_index("core")
    base = outer_base.astype(f32)
    own_tokens = tokens[0]
    block = own_tokens.shape[0] // shards
    shape = jax.ShapeDtypeStruct

    pseudo = base - local_weights[0].astype(f32) + error_feedback[0].astype(f32)
    halves = pseudo.reshape(2, rows // 2, kv)
    pair = pick(halves, core, 0) + swap(pick(halves, 1 - core, 0), "core")
    first = exchange(
        jnp.concatenate(
            [
                pair.astype(bf16).reshape(replicas // 2, own, kv),
                jnp.broadcast_to(momentum.T, (replicas // 2, cols, rows)),
            ],
            axis=1,
        ),
        chips,
    )
    second = in_vmem(
        functools.partial(moments, own=own, rank=rank, replicas=replicas),
        shape((replicas, own, 4 * rank), f32),
        2,
        flops=20000000,
        bytes_accessed=1000000,
        transcendentals=0,
    )(first, jnp.tile(q_start, (1, 4)))
    second = exchange(second, peers)

    my_momentum = first[:, own:]
    its_momentum = swap(my_momentum, "core")
    full_momentum = jnp.stack(
        [
            jnp.where(core == 0, my_momentum, its_momentum),
            jnp.where(core == 0, its_momentum, my_momentum),
        ],
        axis=1,
    ).reshape(kv, rows)
    full_momentum = full_momentum.T

    part = (shards // 2, block, kv // 2)
    send_a, keep_a, send_b, keep_b = in_vmem(
        key_products,
        (shape(part, bf16), shape(part, f32), shape(part, bf16), shape(part, f32)),
        4,
        1,
        flops=2 * 2048 * 512 * 512,
        bytes_accessed=9000000,
        transcendentals=0,
    )(
        jnp.stack([lax.axis_index("xl"), lax.axis_index("y0")]).astype(jnp.int32),
        own_tokens,
        outer_base,
        full_momentum,
    )
    key_a = keep_a + swap(send_a, "xl").astype(f32)
    key_b = keep_b + swap(send_b, "y0").astype(f32)
    quarter = (shards // 4, 2, block, kv // 2)
    key_a = halve(key_a.reshape(quarter), "y0", 1)
    key_b = halve(key_b.reshape(quarter), "xl", 1)
    key_part = jnp.concatenate([key_a, key_b], axis=-1)
    place = lax.axis_index(("y2", "y1"))
    key_sum = pick(key_part, place, 0)
    for d in (1, 2, 3):
        away = pick(key_part, place ^ d, 0).astype(bf16)
        key_sum = key_sum + lax.ppermute(
            away, ("y2", "y1"), [(i, i ^ d) for i in range(4)]
        ).astype(f32)

    third = in_vmem(
        functools.partial(token_products, own=own, rank=rank),
        shape((shards, own + block // 4, 4 * rank), f32),
        2,
        flops=500000000,
        bytes_accessed=3000000,
        transcendentals=0,
    )(second, own_tokens)
    third = jnp.sum(exchange(third, shard), axis=0)
    sums, token_sum = third[:own], third[own:]
    fourth = copy_for_each(sums, peers)

    token_sum = jnp.concatenate(
        [token_sum[:, i * rank : (i + 1) * rank] for i in range(4)], axis=0
    )
    gram = jnp.concatenate([sums[:, rank : 2 * rank], sums[:, 2 * rank : 3 * rank]], axis=0)
    p_mean = second[:, :, :rank].reshape(rows, rank)
    factor_low = jnp.linalg.cholesky(gram)
    inverse = jax.scipy.linalg.solve_triangular(
        factor_low, jnp.eye(rank, dtype=f32), lower=True
    )
    basis = jnp.dot(p_mean, inverse.T, precision=highest)
    token_basis = jnp.dot(token_sum, inverse.T, precision=highest)

    q_sum = fourth[:, :, 3 * rank :].reshape(kv, rank)
    q_mean = jnp.dot(q_sum, inverse.T, precision=highest)
    update = jnp.dot(basis, q_mean.T, precision=highest)
    new_error = (pseudo - update).astype(bf16)[None]
    moment = outer_mu * full_momentum.astype(f32) + update
    new_base = (base - outer_rate * (outer_mu * moment + update)).astype(bf16)
    at = lax.axis_index(chips + ("core",)) * cols
    own_q = lax.dynamic_slice_in_dim(q_mean, at, cols, 0)
    new_momentum = outer_mu * momentum.astype(f32) + jnp.dot(
        basis, own_q.T, precision=highest
    )
    key_rows = key_sum - own_upd * jnp.dot(token_basis, q_mean.T, precision=highest)
    return (
        new_base,
        new_momentum.astype(bf16),
        new_error,
        key_rows.astype(bf16)[None],
    )


def solution(mesh):
    fine = Mesh(
        mesh.devices.reshape(8, 2, 2, 2, 2, 2, 2), chips + ("core",) + shard
    )
    replica = chips + ("core",)
    in_specs = (
        P(replica, shard, None),
        P(shard, None),
        P(shard, replica),
        P(replica, shard, None),
        P(),
        P(replica, None, shard),
    )
    out_specs = (
        P(shard, None),
        P(shard, replica),
        P(replica, shard, None),
        P(replica, shard, None),
    )
    return jax.shard_map(
        on_device, mesh=fine, in_specs=in_specs, out_specs=out_specs, check_vma=False
    )
```

time: 439 us -> 146 us (0.33)
  waiting for transfers between devices: 312 us -> 16.7 us
  starting transfers between devices: 10.5 us -> 60.1 us
  blocking collectives: 64.9 us -> 24.5 us
  between operations: 14.2 us -> 1.08 us
  Pallas kernels: 0 us -> 11 us
  matrix products: 9.83 us -> 4.8 us
  local copies, waits for them, and re-layouts: 13.8 us -> 9.1 us
  other arithmetic: 13.1 us -> 17.5 us
    psum x1 -> x0, waiting for transfers between devices: 252 us -> none  [together(): running = lax.psum(jnp.concatenate([a.ravel() for a in arrays]), axis)]
    all_to_all x2 -> x3, waiting for transfers between devices: 60.2 us -> 10.5 us  [exchange(): return lax.all_to_all(x, axis, 0, 0, tiled=True)]
    all_to_all x1, blocking collectives: 64.9 us -> 24.5 us  [exchange(): return lax.all_to_all(x, axis, 0, 0, tiled=True)]
    ppermute x0 -> x9, starting transfers between devices: none -> 36.4 us  [the longest x6 25 us: swap(): return lax.ppermute(x, axis, [(0, 1), (1, 0)])]
    all_to_all x2 -> x3, starting transfers between devices: 10.5 us -> 23.7 us  [exchange(): return lax.all_to_all(x, axis, 0, 0, tiled=True)]
    pallas_call x0 -> x3, Pallas kernels: none -> 11 us  [the longest x1 4.69 us: on_device(): in_vmem(key_products, (shape(part, bf16), shape(part, f32), shape(part, b...]
    ppermute x0 -> x9, waiting for transfers between devices: none -> 6.27 us  [the longest x6 6.26 us: swap(): return lax.ppermute(x, axis, [(0, 1), (1, 0)])]
    add x0 -> x5, other arithmetic: none -> 5.33 us  [the longest x1 1.55 us: on_device(): pseudo = base - local_weights[0].astype(f32) + error_feedback[0].astype(f32)]
  transfers between devices with their start and end apart: 3 -> 12, of which waited for: 3 -> 4; matrix products, arithmetic and copies ran while one was open for 2% -> 17% of each run, Pallas kernels for 0% -> 8%
where the time goes in v1:
time: 146 us; the launch traced here: 145 us
  starting transfers between devices  60.1 us (41%)
  blocking collectives  24.5 us (17%)
  other arithmetic  17.5 us (12%)
  waiting for transfers between devices  16.7 us (11%)
  Pallas kernels  11 us (8%)
  local copies, waits for them, and re-layouts  9.1 us (6%)
  matrix products  4.8 us (3%)
    ppermute x6, starting transfers between devices, swap(): return lax.ppermute(x, axis, [(0, 1), (1, 0)])  25 us
    all_to_all x1, blocking collectives, exchange(): return lax.all_to_all(x, axis, 0, 0, tiled=True)  24.5 us
    all_to_all x3, starting transfers between devices, exchange(): return lax.all_to_all(x, axis, 0, 0, tiled=True)  23.7 us
    ppermute x3, starting transfers between devices, on_device(): lax.ppermute(away, ('y2', 'y1'), [(i, i ^ d) for i in range(4)]).astype(f32)  11.4 us
    all_to_all x3, waiting for transfers between devices, exchange(): return lax.all_to_all(x, axis, 0, 0, tiled=True)  10.5 us
    ppermute x6, waiting for transfers between devices, swap(): return lax.ppermute(x, axis, [(0, 1), (1, 0)])  6.26 us
    pallas_call x1, Pallas kernels, on_device(): in_vmem(key_products, (shape(part, bf16), shape(part, f32), shape(part, b...  4.69 us
    pallas_call x1, Pallas kernels, on_device(): in_vmem(functools.partial(token_products, own=own, rank=rank), shape((sha...  3.75 us
  transfers between devices with their start and end apart: 12, of which 4 were waited for; matrix products, arithmetic and copies ran while one was open for 17% of the time, Pallas kernels for 8%

profile of v1, /device:TPU:1, one launch (start us, length us, event | category | flops | bytes accessed | tf_op | source)
XLA Modules:
  0.0 144.9 jit_solution(14466484364942721718)
XLA Ops:
  0.6 1.6 %fusion.1 = f32[512,512]{1,0:T(8,128)S(1)} fusion(bf16[512,512]{1,0:T(8,128)(2,1)} %base_ref.1, bf16[1,512,512]{2,1,0:T(8,128)(2,1)} %param.9, bf16[1,512,512]{2,1,0:T(8,128)(2,1)} %param.6), kind=kLoop, calls=%fused_computation.13 | loop fusion | flops 1310720 | bytes 2621440 | tf_op jit(solution)/shard_map/add | solution.py:133
  2.3 8.7 %collective-permute-start = (f32[256,512]{1,0:T(8,128)S(1)}, f32[256,512]{1,0:T(8,128)S(1)}, u32[]{:S(2)}, u32[]{:S(2)}) collective-permute-start(f32[256,512]{1,0:T(8,128)S(1)} %dynamic-slice_bitcast_fusion), channel_id=1, source_target_pairs={{0,16},{16,0},{1,17},{17,1},{2,18},{18,2},{3,19},{19,3},{4,20},{20... | collective-permute-start | bytes 1572872 | tf_op jit(solution)/shard_map/ppermute | solution.py:23
  11.0 1.5 %collective-permute-done = f32[256,512]{1,0:T(8,128)S(1)} collective-permute-done((f32[256,512]{1,0:T(8,128)S(1)}, f32[256,512]{1,0:T(8,128)S(1)}, u32[]{:S(2)}, u32[]{:S(2)}) %collective-permute-start) | collective-permute-done | bytes 524320 | tf_op jit(solution)/shard_map/ppermute | solution.py:23
  12.7 24.5 %all_to_all.20.first_ref = bf16[16,32,512]{2,1,0:T(8,128)(2,1)S(1)} all-to-all(bf16[16,32,512]{2,1,0:T(8,128)(2,1)S(1)} %pad_maximum_fusion), channel_id=1, replica_groups=mesh['z'=8,'xh'=2,'core'=2,'y2'=2,'y1'=2,'y0'=2,'xl'=2] {'z','xh'}, dimensions={0} | all-to-all | bytes 1048576 | tf_op jit(solution)/shard_map/all_to_all | solution.py:27
  37.3 4.5 %collective-permute-start.1 = (bf16[16,16,512]{2,1,0:T(8,128)(2,1)S(1)}, bf16[16,16,512]{2,1,0:T(8,128)(2,1)S(1)}, u32[]{:S(2)}, u32[]{:S(2)}) collective-permute-start(bf16[16,16,512]{2,1,0:T(8,128)(2,1)S(1)} %slice.59), channel_id=1, source_target_pairs={{0,16},{16,0},{1,17},{17,1},{2,18},{18,2},{3,19},{19,3},{4,20},{20... | collective-permute-start | bytes 786440 | tf_op jit(solution)/shard_map/ppermute | solution.py:23
  43.3 2.6 %shard_map.93 = f32[32,16,128]{2,1,0:T(8,128)} custom-call(bf16[16,32,512]{2,1,0:T(8,128)(2,1)} %copy-done, f32[512,128]{1,0:T(8,128)} %copy.33.q_ref), custom_call_target="tpu_custom_call" | custom-call | flops 20000000 | bytes 1000000 | tf_op jit(solution)/shard_map/pallas_call | solution.py:146
  45.9 3.7 %all-to-all-start.1 = ((f32[32,16,128]{2,1,0:T(8,128)}), f32[32,16,128]{2,1,0:T(8,128)S(1)}, u32[]{:S(2)}, u32[]{:S(2)}) async-start(f32[32,16,128]{2,1,0:T(8,128)} %shard_map.93), calls=%async_computation.1 | async-start | bytes 524288 | tf_op jit(solution)/shard_map/all_to_all | solution.py:27
  51.7 4.7 %shard_map.95 = (bf16[8,128,256]{2,1,0:T(8,128)(2,1)}, f32[8,128,256]{2,1,0:T(8,128)}, bf16[8,128,256]{2,1,0:T(8,128)(2,1)}, f32[8,128,256]{2,1,0:T(8,128)}) custom-call(s32[2]{0:T(128)} %pad_add_fusion.at_ref, bf16[2048,512]{1,0:T(8,128)(2,1)} %bitcast.98, bf16[512,512]{1,0:T(8,128)(2,1)} %base_ref.1, bf16[512,512]{1,0:T(8,128)(2,1)} %bitcast.97), custom_call_target="tpu_custom_call" | custom-call | flops 1073741824 | bytes 9000000 | tf_op jit(solution)/shard_map/pallas_call | solution.py:168
  56.4 3.2 %collective-permute-start.4 = (bf16[8,128,256]{2,1,0:T(8,128)(2,1)}, bf16[8,128,256]{2,1,0:T(8,128)(2,1)S(1)}, u32[]{:S(2)}, u32[]{:S(2)}) collective-permute-start(bf16[8,128,256]{2,1,0:T(8,128)(2,1)} %get-tuple-element.11), channel_id=1, source_target_pairs={{0,2},{2,0},{1,3},{3,1},{4,6},{6,4},{5,7},{7,5},{8,10},{10,8},{9,1... | collective-permute-start | bytes 1572872 | tf_op jit(solution)/shard_map/ppermute | solution.py:23
  59.6 2.2 %collective-permute-start.2 = (bf16[8,128,256]{2,1,0:T(8,128)(2,1)}, bf16[8,128,256]{2,1,0:T(8,128)(2,1)}, u32[]{:S(2)}, u32[]{:S(2)}) collective-permute-start(bf16[8,128,256]{2,1,0:T(8,128)(2,1)} %get-tuple-element.9), channel_id=1, source_target_pairs={{0,1},{1,0},{2,3},{3,2},{4,5},{5,4},{6,7},{7,6},{8,9},{9,8},{10,11... | collective-permute-start | bytes 1572872 | tf_op jit(solution)/shard_map/ppermute | solution.py:23
  62.5 3.7 %shard_map.94 = f32[16,48,128]{2,1,0:T(8,128)} custom-call(f32[32,16,128]{2,1,0:T(8,128)} %copy-done.2, bf16[2048,512]{1,0:T(8,128)(2,1)} %bitcast.99), custom_call_target="tpu_custom_call" | custom-call | flops 500000000 | bytes 3000000 | tf_op jit(solution)/shard_map/pallas_call | solution.py:196
  66.3 7.1 %all-to-all-start.2 = ((f32[16,48,128]{2,1,0:T(8,128)}), f32[16,48,128]{2,1,0:T(8,128)}, u32[]{:S(2)}, u32[]{:S(2)}) async-start(f32[16,48,128]{2,1,0:T(8,128)} %shard_map.94), calls=%async_computation.2 | async-start | bytes 786432 | tf_op jit(solution)/shard_map/all_to_all | solution.py:27
  76.5 3.2 %collective-permute-start.5 = (bf16[4,128,256]{2,1,0:T(8,128)(2,1)}, bf16[4,128,256]{2,1,0:T(8,128)(2,1)S(1)}, u32[]{:S(2)}, u32[]{:S(2)}) collective-permute-start(bf16[4,128,256]{2,1,0:T(8,128)(2,1)} %fusion.6), channel_id=1, source_target_pairs={{0,1},{1,0},{2,3},{3,2},{4,5},{5,4},{6,7},{7,6},{8,9},{9,8},{10,11... | collective-permute-start | bytes 786440 | tf_op jit(solution)/shard_map/ppermute | solution.py:23
  81.9 3.1 %collective-permute-start.3 = (bf16[4,128,256]{2,1,0:T(8,128)(2,1)S(1)}, bf16[4,128,256]{2,1,0:T(8,128)(2,1)S(1)}, u32[]{:S(2)}, u32[]{:S(2)}) collective-permute-start(bf16[4,128,256]{2,1,0:T(8,128)(2,1)S(1)} %fusion.5), channel_id=1, source_target_pairs={{0,2},{2,0},{1,3},{3,1},{4,6},{6,4},{5,7},{7,5},{8,10},{10,8},{9,1... | collective-permute-start | bytes 786440 | tf_op jit(solution)/shard_map/ppermute | solution.py:23
  85.0 3.7 %collective-permute-done.5 = bf16[4,128,256]{2,1,0:T(8,128)(2,1)S(1)} collective-permute-done((bf16[4,128,256]{2,1,0:T(8,128)(2,1)}, bf16[4,128,256]{2,1,0:T(8,128)(2,1)S(1)}, u32[]{:S(2)}, u32[]{:S(2)}) %collective-permute-start.5) | collective-permute-done | bytes 262176 | tf_op jit(solution)/shard_map/ppermute | solution.py:23
  91.7 5.2 %collective-permute-start.8 = (bf16[128,512]{1,0:T(8,128)(2,1)}, bf16[128,512]{1,0:T(8,128)(2,1)}, u32[]{:S(2)}, u32[]{:S(2)}) collective-permute-start(bf16[128,512]{1,0:T(8,128)(2,1)} %get-tuple-element.14), channel_id=1, source_target_pairs={{0,12},{4,8},{8,4},{12,0},{1,13},{5,9},{9,5},{13,1},{2,14},{6,10},... | collective-permute-start | bytes 393224 | tf_op jit(solution)/shard_map/ppermute | solution.py:192
  96.9 4.0 %collective-permute-start.7 = (bf16[128,512]{1,0:T(8,128)(2,1)}, bf16[128,512]{1,0:T(8,128)(2,1)}, u32[]{:S(2)}, u32[]{:S(2)}) collective-permute-start(bf16[128,512]{1,0:T(8,128)(2,1)} %get-tuple-element.13), channel_id=1, source_target_pairs={{0,8},{4,12},{8,0},{12,4},{1,9},{5,13},{9,1},{13,5},{2,10},{6,14},... | collective-permute-start | bytes 393224 | tf_op jit(solution)/shard_map/ppermute | solution.py:192
  100.9 2.2 %collective-permute-start.6 = (bf16[128,512]{1,0:T(8,128)(2,1)}, bf16[128,512]{1,0:T(8,128)(2,1)}, u32[]{:S(2)}, u32[]{:S(2)}) collective-permute-start(bf16[128,512]{1,0:T(8,128)(2,1)} %get-tuple-element.12), channel_id=1, source_target_pairs={{0,4},{4,0},{8,12},{12,8},{1,5},{5,1},{9,13},{13,9},{2,6},{6,2},{1... | collective-permute-start | bytes 393224 | tf_op jit(solution)/shard_map/ppermute | solution.py:192
  105.3 2.9 %cholesky.17 = f32[32,32]{1,0:T(8,128)S(1)} custom-call(f32[32,32]{1,0:T(8,128)S(1)} %fusion.35), custom_call_target="Cholesky" | custom-call | tf_op jit(solution)/shard_map/jit(cholesky)/cholesky | solution.py:213
  109.6 2.4 %custom-call.7 = f32[1,32,32]{1,2,0:T(8,128)S(1)} custom-call(f32[1,32,32]{2,1,0:T(8,128)S(1)} %fusion.24), custom_call_target="InvertDiagBlocksLowerTriangular" | custom-call | tf_op jit(solution)/shard_map/jit(_solve_triangular)/triangular_solve | solution.py:214
  112.7 12.9 %all-to-all-start.3 = ((f32[32,16,128]{2,1,0:T(8,128)}), f32[32,16,128]{2,1,0:T(8,128)}, u32[]{:S(2)}, u32[]{:S(2)}) async-start(f32[32,16,128]{2,1,0:T(8,128)} %broadcast_in_dim.15), calls=%async_computation.3 | async-start | bytes 524288 | tf_op jit(solution)/shard_map/all_to_all | solution.py:27
  127.5 10.5 %all-to-all-done.3 = f32[32,16,128]{2,1,0:T(8,128)} async-done(((f32[32,16,128]{2,1,0:T(8,128)}), f32[32,16,128]{2,1,0:T(8,128)}, u32[]{:S(2)}, u32[]{:S(2)}) %all-to-all-start.3) | async-done | bytes 262176 | tf_op jit(solution)/shard_map/all_to_all | solution.py:27
  139.5 2.3 %fusion.3 = (bf16[1,512,512]{2,1,0:T(8,128)(2,1)}, bf16[512,512]{1,0:T(8,128)(2,1)}) fusion(f32[512,512]{1,0:T(8,128)S(1)} %fusion.1, bf16[512,512]{0,1:T(8,128)(2,1)S(1)} %copy-done.5, bf16[512,512]{1,0:T(8,128)(2,1)S(1)} %copy-done.4, f32[512,32]{0,1:T(8,128)S(1)} %fusion.41, f32[512,32]{0,1:T(8,128)S(1)} %fusion.42), kind=kOutput, calls=%fused_computation.18 | convolution fusion | flops 103546880 | bytes 3276800 | tf_op jit(solution)/shard_map/dot_general | solution.py:222
  143.1 1.8 %fusion.23 = bf16[1,128,512]{2,1,0:T(8,128)(2,1)} fusion(f32[128,512]{1,0:T(8,128)S(1)} %convolution_multiply_fusion, bf16[128,512]{1,0:T(8,128)(2,1)} %collective-permute-done.8, bf16[128,512]{1,0:T(8,128)(2,1)} %collective-permute-done.7, bf16[128,512]{1,0:T(8,128)(2,1)} %collective-permute-done.6, s32[]{:T(128)S(6)} %select_n.63, ...), kind=kLoop, calls=%fused_computation.48 | loop fusion | flops 589824 | bytes 1835012 | tf_op jit(solution)/shard_map/broadcast_in_dim | solution.py:236
  (72 shorter events, 21.5 us)
Async XLA Ops:
  0.6 12.0 %copy-start.9 = (bf16[512,16]{0,1:T(8,128)(2,1)S(1)}, bf16[512,16]{0,1:T(8,128)(2,1)}, u32[]{:S(2)}) copy-start(bf16[512,16]{0,1:T(8,128)(2,1)} %param.8) | copy-start | bytes 49156
  2.3 10.3 %collective-permute-start = (f32[256,512]{1,0:T(8,128)S(1)}, f32[256,512]{1,0:T(8,128)S(1)}, u32[]{:S(2)}, u32[]{:S(2)}) collective-permute-start(f32[256,512]{1,0:T(8,128)S(1)} %dynamic-slice_bitcast_fusion), channel_id=1, source_target_pairs={{0,16},{16,0},{1,17},{17,1},{2,18},{18,2},{3,19},{19,3},{4,20},{20... | collective-permute-start | bytes 1572872 | tf_op jit(solution)/shard_map/ppermute | solution.py:23
  11.0 30.8 %copy-start.8 = (f32[512,32]{0,1:T(8,128)S(1)}, f32[512,32]{0,1:T(8,128)}, u32[]{:S(2)}) copy-start(f32[512,32]{0,1:T(8,128)} %param.10) | copy-start | bytes 196612
  37.3 6.0 %copy-start = (bf16[16,32,512]{2,1,0:T(8,128)(2,1)}, bf16[16,32,512]{2,1,0:T(8,128)(2,1)S(1)}, u32[]{:S(2)}) copy-start(bf16[16,32,512]{2,1,0:T(8,128)(2,1)S(1)} %all_to_all.20.first_ref) | copy-start | bytes 1572868
  37.3 12.3 %collective-permute-start.1 = (bf16[16,16,512]{2,1,0:T(8,128)(2,1)S(1)}, bf16[16,16,512]{2,1,0:T(8,128)(2,1)S(1)}, u32[]{:S(2)}, u32[]{:S(2)}) collective-permute-start(bf16[16,16,512]{2,1,0:T(8,128)(2,1)S(1)} %slice.59), channel_id=1, source_target_pairs={{0,16},{16,0},{1,17},{17,1},{2,18},{18,2},{3,19},{19,3},{4,20},{20... | collective-permute-start | bytes 786440 | tf_op jit(solution)/shard_map/ppermute | solution.py:23
  45.9 15.9 %all-to-all-start.1 = ((f32[32,16,128]{2,1,0:T(8,128)}), f32[32,16,128]{2,1,0:T(8,128)S(1)}, u32[]{:S(2)}, u32[]{:S(2)}) async-start(f32[32,16,128]{2,1,0:T(8,128)} %shard_map.93), calls=%async_computation.1 | async-start | bytes 524288 | tf_op jit(solution)/shard_map/all_to_all | solution.py:27
  56.4 17.0 %collective-permute-start.4 = (bf16[8,128,256]{2,1,0:T(8,128)(2,1)}, bf16[8,128,256]{2,1,0:T(8,128)(2,1)S(1)}, u32[]{:S(2)}, u32[]{:S(2)}) collective-permute-start(bf16[8,128,256]{2,1,0:T(8,128)(2,1)} %get-tuple-element.11), channel_id=1, source_target_pairs={{0,2},{2,0},{1,3},{3,1},{4,6},{6,4},{5,7},{7,5},{8,10},{10,8},{9,1... | collective-permute-start | bytes 1572872 | tf_op jit(solution)/shard_map/ppermute | solution.py:23
  59.6 20.1 %collective-permute-start.2 = (bf16[8,128,256]{2,1,0:T(8,128)(2,1)}, bf16[8,128,256]{2,1,0:T(8,128)(2,1)}, u32[]{:S(2)}, u32[]{:S(2)}) collective-permute-start(bf16[8,128,256]{2,1,0:T(8,128)(2,1)} %get-tuple-element.9), channel_id=1, source_target_pairs={{0,1},{1,0},{2,3},{3,2},{4,5},{5,4},{6,7},{7,6},{8,9},{9,8},{10,11... | collective-permute-start | bytes 1572872 | tf_op jit(solution)/shard_map/ppermute | solution.py:23
  61.8 0.7 copy-start.2
  66.3 13.4 %copy-start.6 = (f32[8,128,256]{2,1,0:T(8,128)S(1)}, f32[8,128,256]{2,1,0:T(8,128)}, u32[]{:S(2)}) copy-start(f32[8,128,256]{2,1,0:T(8,128)} %get-tuple-element.8) | copy-start | bytes 3145732
  66.3 36.9 %all-to-all-start.2 = ((f32[16,48,128]{2,1,0:T(8,128)}), f32[16,48,128]{2,1,0:T(8,128)}, u32[]{:S(2)}, u32[]{:S(2)}) async-start(f32[16,48,128]{2,1,0:T(8,128)} %shard_map.94), calls=%async_computation.2 | async-start | bytes 786432 | tf_op jit(solution)/shard_map/all_to_all | solution.py:27
  73.4 0.8 copy-start.7
  76.5 12.3 %collective-permute-start.5 = (bf16[4,128,256]{2,1,0:T(8,128)(2,1)}, bf16[4,128,256]{2,1,0:T(8,128)(2,1)S(1)}, u32[]{:S(2)}, u32[]{:S(2)}) collective-permute-start(bf16[4,128,256]{2,1,0:T(8,128)(2,1)} %fusion.6), channel_id=1, source_target_pairs={{0,1},{1,0},{2,3},{3,2},{4,5},{5,4},{6,7},{7,6},{8,9},{9,8},{10,11... | collective-permute-start | bytes 786440 | tf_op jit(solution)/shard_map/ppermute | solution.py:23
  80.9 1.0 copy-start.1
  81.9 7.9 %collective-permute-start.3 = (bf16[4,128,256]{2,1,0:T(8,128)(2,1)S(1)}, bf16[4,128,256]{2,1,0:T(8,128)(2,1)S(1)}, u32[]{:S(2)}, u32[]{:S(2)}) collective-permute-start(bf16[4,128,256]{2,1,0:T(8,128)(2,1)S(1)} %fusion.5), channel_id=1, source_target_pairs={{0,2},{2,0},{1,3},{3,1},{4,6},{6,4},{5,7},{7,5},{8,10},{10,8},{9,1... | collective-permute-start | bytes 786440 | tf_op jit(solution)/shard_map/ppermute | solution.py:23
  88.8 38.3 %copy-start.3 = (f32[32,16,128]{2,1,0:T(8,128)S(1)}, f32[32,16,128]{2,1,0:T(8,128)}, u32[]{:S(2)}) copy-start(f32[32,16,128]{2,1,0:T(8,128)} %copy-done.2) | copy-start | bytes 786436
  90.9 48.5 %copy-start.4 = (bf16[512,512]{1,0:T(8,128)(2,1)S(1)}, bf16[512,512]{1,0:T(8,128)(2,1)}, u32[]{:S(2)}) copy-start(bf16[512,512]{1,0:T(8,128)(2,1)} %base_ref.1) | copy-start | bytes 1572868
  90.9 48.5 %copy-start.5 = (bf16[512,512]{0,1:T(8,128)(2,1)S(1)}, bf16[512,512]{0,1:T(8,128)(2,1)}, u32[]{:S(2)}) copy-start(bf16[512,512]{0,1:T(8,128)(2,1)} %copy.32) | copy-start | bytes 1572868
  91.7 51.4 %collective-permute-start.8 = (bf16[128,512]{1,0:T(8,128)(2,1)}, bf16[128,512]{1,0:T(8,128)(2,1)}, u32[]{:S(2)}, u32[]{:S(2)}) collective-permute-start(bf16[128,512]{1,0:T(8,128)(2,1)} %get-tuple-element.14), channel_id=1, source_target_pairs={{0,12},{4,8},{8,4},{12,0},{1,13},{5,9},{9,5},{13,1},{2,14},{6,10},... | collective-permute-start | bytes 393224 | tf_op jit(solution)/shard_map/ppermute | solution.py:192
  96.9 46.2 %collective-permute-start.7 = (bf16[128,512]{1,0:T(8,128)(2,1)}, bf16[128,512]{1,0:T(8,128)(2,1)}, u32[]{:S(2)}, u32[]{:S(2)}) collective-permute-start(bf16[128,512]{1,0:T(8,128)(2,1)} %get-tuple-element.13), channel_id=1, source_target_pairs={{0,8},{4,12},{8,0},{12,4},{1,9},{5,13},{9,1},{13,5},{2,10},{6,14},... | collective-permute-start | bytes 393224 | tf_op jit(solution)/shard_map/ppermute | solution.py:192
  100.9 42.2 %collective-permute-start.6 = (bf16[128,512]{1,0:T(8,128)(2,1)}, bf16[128,512]{1,0:T(8,128)(2,1)}, u32[]{:S(2)}, u32[]{:S(2)}) collective-permute-start(bf16[128,512]{1,0:T(8,128)(2,1)} %get-tuple-element.12), channel_id=1, source_target_pairs={{0,4},{4,0},{8,12},{12,8},{1,5},{5,1},{9,13},{13,9},{2,6},{6,2},{1... | collective-permute-start | bytes 393224 | tf_op jit(solution)/shard_map/ppermute | solution.py:192
  112.7 25.3 %all-to-all-start.3 = ((f32[32,16,128]{2,1,0:T(8,128)}), f32[32,16,128]{2,1,0:T(8,128)}, u32[]{:S(2)}, u32[]{:S(2)}) async-start(f32[32,16,128]{2,1,0:T(8,128)} %broadcast_in_dim.15), calls=%async_computation.3 | async-start | bytes 524288 | tf_op jit(solution)/shard_map/all_to_all | solution.py:27

commit v2 on v1

--- a/solution.py
+++ b/solution.py
@@ -7,10 +7,12 @@
 from jax.experimental.pallas import tpu as pltpu
 from jax.sharding import Mesh, PartitionSpec as P
 
+
 outer_mu = 0.9
 outer_rate = 0.7
 own_mom = outer_rate * outer_mu * outer_mu
 own_upd = outer_rate * (outer_mu + 1.0)
+
 
 chips = ("z", "xh")
 peers = ("core", "z", "xh")
@@ -52,8 +54,9 @@
 
 
 def moments(first_ref, q_ref, out_ref, *, own, rank, replicas):
-    mean = jnp.sum(first_ref[:, :own].astype(f32), axis=0) * (1.0 / replicas)
-    p = dot(mean, q_ref[...], ((1,), (0,)), highest)
+    mean = jnp.sum(first_ref[...].astype(f32), axis=0) * (1.0 / replicas)
+    q = jnp.concatenate([q_ref[...]] * 4, axis=0)
+    p = dot(mean, q, ((1,), (1,)), highest)
     group = lane_group(p.shape, rank)
     p_at = [jnp.where(group == i, p, 0.0) for i in range(4)]
     upper = dot(p_at[0], p_at[1], ((0,), (0,)), highest)
@@ -84,10 +87,8 @@
     out_ref[:, own:] = total.reshape(shards, step, lanes)
 
 
-def key_products(
-    at_ref, tokens_ref, base_ref, momentum_ref, sa_ref, ka_ref, sb_ref, kb_ref
-):
-    xl, y0 = at_ref[0], at_ref[1]
+def key_products(tokens_ref, base_ref, momentum_ref, sa_ref, ka_ref, sb_ref, kb_ref):
+    xl, y0 = lax.axis_index("xl"), lax.axis_index("y0")
     block, half = sa_ref.shape[1:]
     settled = base_ref[...].astype(f32) - own_mom * momentum_ref[...].astype(f32)
     settled = settled.astype(bf16)
@@ -106,15 +107,17 @@
         kb_ref[j] = dot(rows((j // 2) * 4 + y0 * 2 + j % 2), right, ((1,), (0,)))
 
 
-def in_vmem(kernel, out_shape, n, scalars=0, **cost):
+def in_vmem(kernel, out_shape, n, mib, flops):
     whole = pl.BlockSpec(memory_space=pltpu.VMEM)
-    small = pl.BlockSpec(memory_space=pltpu.SMEM)
     return pl.pallas_call(
         kernel,
         out_shape=out_shape,
-        in_specs=[small] * scalars + [whole] * (n - scalars),
+        in_specs=[whole] * n,
         out_specs=jax.tree.map(lambda _: whole, out_shape),
-        cost_estimate=pl.CostEstimate(**cost),
+        cost_estimate=pl.CostEstimate(
+            flops=flops, bytes_accessed=flops // 100, transcendentals=0
+        ),
+        compiler_params=pltpu.CompilerParams(vmem_limit_bytes=mib << 20) if mib else None,
     )
 
 
@@ -130,30 +133,23 @@
     block = own_tokens.shape[0] // shards
     shape = jax.ShapeDtypeStruct
 
+    my_momentum = copy_for_each(momentum.T, chips)
+
     pseudo = base - local_weights[0].astype(f32) + error_feedback[0].astype(f32)
     halves = pseudo.reshape(2, rows // 2, kv)
-    pair = pick(halves, core, 0) + swap(pick(halves, 1 - core, 0), "core")
-    first = exchange(
-        jnp.concatenate(
-            [
-                pair.astype(bf16).reshape(replicas // 2, own, kv),
-                jnp.broadcast_to(momentum.T, (replicas // 2, cols, rows)),
-            ],
-            axis=1,
-        ),
-        chips,
-    )
+    pair = swap(pick(halves, 1 - core, 0), "core")
+    pair = (pick(halves, core, 0) + pair).astype(bf16)
+    pair, my_momentum = lax.optimization_barrier((pair, my_momentum))
+    first = exchange(pair.reshape(replicas // 2, own, kv), chips)
     second = in_vmem(
         functools.partial(moments, own=own, rank=rank, replicas=replicas),
         shape((replicas, own, 4 * rank), f32),
         2,
-        flops=20000000,
-        bytes_accessed=1000000,
-        transcendentals=0,
-    )(first, jnp.tile(q_start, (1, 4)))
+        0,
+        40000000,
+    )(first, q_start.T)
     second = exchange(second, peers)
 
-    my_momentum = first[:, own:]
     its_momentum = swap(my_momentum, "core")
     full_momentum = jnp.stack(
         [
@@ -168,19 +164,14 @@
     send_a, keep_a, send_b, keep_b = in_vmem(
         key_products,
         (shape(part, bf16), shape(part, f32), shape(part, bf16), shape(part, f32)),
-        4,
-        1,
-        flops=2 * 2048 * 512 * 512,
-        bytes_accessed=9000000,
-        transcendentals=0,
-    )(
-        jnp.stack([lax.axis_index("xl"), lax.axis_index("y0")]).astype(jnp.int32),
-        own_tokens,
-        outer_base,
-        full_momentum,
-    )
-    key_a = keep_a + swap(send_a, "xl").astype(f32)
-    key_b = keep_b + swap(send_b, "y0").astype(f32)
+        3,
+        0,
+        2 * tokens.shape[1] * rows * kv,
+    )(own_tokens, outer_base, full_momentum)
+    key_a = swap(send_a, "xl")
+    key_b = swap(send_b, "y0")
+    key_a = keep_a + key_a.astype(f32)
+    key_b = keep_b + key_b.astype(f32)
     quarter = (shards // 4, 2, block, kv // 2)
     key_a = halve(key_a.reshape(quarter), "y0", 1)
     key_b = halve(key_b.reshape(quarter), "xl", 1)
@@ -189,19 +180,18 @@
     key_sum = pick(key_part, place, 0)
     for d in (1, 2, 3):
         away = pick(key_part, place ^ d, 0).astype(bf16)
-        key_sum = key_sum + lax.ppermute(
-            away, ("y2", "y1"), [(i, i ^ d) for i in range(4)]
-        ).astype(f32)
+        away = lax.ppermute(away, ("y2", "y1"), [(i, i ^ d) for i in range(4)])
+        key_sum = key_sum + away.astype(f32)
 
     third = in_vmem(
         functools.partial(token_products, own=own, rank=rank),
         shape((shards, own + block // 4, 4 * rank), f32),
         2,
-        flops=500000000,
-        bytes_accessed=3000000,
-        transcendentals=0,
+        0,
+        500000000,
     )(second, own_tokens)
-    third = jnp.sum(exchange(third, shard), axis=0)
+    third = exchange(third, shard)
+    third = jnp.sum(third, axis=0)
     sums, token_sum = third[:own], third[own:]
     fourth = copy_for_each(sums, peers)
 
@@ -256,6 +246,11 @@
         P(replica, shard, None),
         P(replica, shard, None),
     )
-    return jax.shard_map(
-        on_device, mesh=fine, in_specs=in_specs, out_specs=out_specs, check_vma=False
-    )
+
+    def step(*arrays):
+        return on_device(*arrays)
+
+    step = jax.shard_map(
+        step, mesh=fine, in_specs=in_specs, out_specs=out_specs, check_vma=False
+    )
+    return step

time: 146 us -> 161 us (1.10)
  waiting for transfers between devices: 16.7 us -> 50.4 us
  blocking collectives: 24.5 us -> 0 us
  starting transfers between devices: 60.1 us -> 65 us
    all_to_all x3 -> x5, waiting for transfers between devices: 10.5 us -> 38.5 us  [exchange(): return lax.all_to_all(x, axis, 0, 0, tiled=True)]
    all_to_all x1 -> x0, blocking collectives: 24.5 us -> none  [exchange(): return lax.all_to_all(x, axis, 0, 0, tiled=True)]
    all_to_all x3 -> x5, starting transfers between devices: 23.7 us -> 30.3 us  [exchange(): return lax.all_to_all(x, axis, 0, 0, tiled=True)]
    ppermute x6, waiting for transfers between devices: 6.26 us -> 11.9 us  [swap(): return lax.ppermute(x, axis, [(0, 1), (1, 0)])]
    ppermute x6, starting transfers between devices: 25 us -> 23.3 us  [swap(): return lax.ppermute(x, axis, [(0, 1), (1, 0)])]
  transfers between devices with their start and end apart: 12 -> 14, of which waited for: 4 -> 6; matrix products, arithmetic and copies ran while one was open for 17% -> 16% of each run, Pallas kernels for 8% -> 4%
where the time goes in v2:
time: 161 us; the launch traced here: 160 us
  starting transfers between devices  65 us (40%)
  waiting for transfers between devices  50.4 us (31%)
  other arithmetic  17.6 us (11%)
  Pallas kernels  11.3 us (7%)
  local copies, waits for them, and re-layouts  9.36 us (6%)
  matrix products  4.81 us (3%)
    all_to_all x5, waiting for transfers between devices, exchange(): return lax.all_to_all(x, axis, 0, 0, tiled=True)  38.5 us
    all_to_all x5, starting transfers between devices, exchange(): return lax.all_to_all(x, axis, 0, 0, tiled=True)  30.3 us
    ppermute x6, starting transfers between devices, swap(): return lax.ppermute(x, axis, [(0, 1), (1, 0)])  23.3 us
    ppermute x6, waiting for transfers between devices, swap(): return lax.ppermute(x, axis, [(0, 1), (1, 0)])  11.9 us
    ppermute x3, starting transfers between devices, on_device(): away = lax.ppermute(away, ('y2', 'y1'), [(i, i ^ d) for i in range(4)])  11.4 us
    pallas_call x1, Pallas kernels, on_device(): in_vmem(key_products, (shape(part, bf16), shape(part, f32), shape(part, b...  4.68 us
    pallas_call x1, Pallas kernels, on_device(): in_vmem(functools.partial(token_products, own=own, rank=rank), shape((sha...  3.74 us
    another operation x3, other arithmetic, on_device(): factor_low = jnp.linalg.cholesky(gram)  3.6 us
  transfers between devices with their start and end apart: 14, of which 6 were waited for; matrix products, arithmetic and copies ran while one was open for 16% of the time, Pallas kernels for 4%

profile of v2, /device:TPU:1, one launch (start us, length us, event | category | flops | bytes accessed | tf_op | source)
XLA Modules:
  0.0 159.6 jit_solution(1268748900594308487)
XLA Ops:
  2.3 8.7 %collective-permute-start = (f32[256,512]{1,0:T(8,128)S(1)}, f32[256,512]{1,0:T(8,128)S(1)}, u32[]{:S(2)}, u32[]{:S(2)}) collective-permute-start(f32[256,512]{1,0:T(8,128)S(1)} %dynamic-slice_bitcast_fusion), channel_id=1, source_target_pairs={{0,16},{16,0},{1,17},{17,1},{2,18},{18,2},{3,19},{19,3},{4,20},{20... | collective-permute-start | bytes 1572872 | tf_op jit(solution)/shard_map/ppermute | solution.py:25
  11.8 7.3 %all-to-all-start = ((bf16[16,16,512]{2,1,0:T(8,128)(2,1)}), bf16[16,16,512]{2,1,0:T(8,128)(2,1)S(1)}, u32[]{:S(2)}, u32[]{:S(2)}) async-start(bf16[16,16,512]{2,1,0:T(8,128)(2,1)} %broadcast_in_dim.14), calls=%async_computation | async-start | bytes 524288 | tf_op jit(solution)/shard_map/all_to_all | solution.py:29
  19.8 12.1 %all-to-all-done = bf16[16,16,512]{2,1,0:T(8,128)(2,1)S(1)} async-done(((bf16[16,16,512]{2,1,0:T(8,128)(2,1)}), bf16[16,16,512]{2,1,0:T(8,128)(2,1)S(1)}, u32[]{:S(2)}, u32[]{:S(2)}) %all-to-all-start) | async-done | bytes 262176 | tf_op jit(solution)/shard_map/all_to_all | solution.py:29
  31.9 3.6 %collective-permute-start.1 = (bf16[16,16,512]{2,1,0:T(8,128)(2,1)S(1)}, bf16[16,16,512]{2,1,0:T(8,128)(2,1)S(1)}, u32[]{:S(2)}, u32[]{:S(2)}) collective-permute-start(bf16[16,16,512]{2,1,0:T(8,128)(2,1)S(1)} %all-to-all-done), channel_id=1, source_target_pairs={{0,16},{16,0},{1,17},{17,1},{2,18},{18,2},{3,19},{19,3},{4,20},{20... | collective-permute-start | bytes 786440 | tf_op jit(solution)/shard_map/ppermute | solution.py:25
  37.8 4.7 %shard_map.95 = (bf16[8,128,256]{2,1,0:T(8,128)(2,1)}, f32[8,128,256]{2,1,0:T(8,128)}, bf16[8,128,256]{2,1,0:T(8,128)(2,1)}, f32[8,128,256]{2,1,0:T(8,128)}) custom-call(bf16[2048,512]{1,0:T(8,128)(2,1)} %bitcast.96, bf16[512,512]{1,0:T(8,128)(2,1)} %base_ref.1, bf16[512,512]{1,0:T(8,128)(2,1)} %bitcast.95), custom_call_target="tpu_custom_call" | custom-call | flops 1073741824 | bytes 10737418 | tf_op jit(solution)/shard_map/pallas_call | solution.py:164
  42.5 3.3 %collective-permute-start.4 = (bf16[8,128,256]{2,1,0:T(8,128)(2,1)}, bf16[8,128,256]{2,1,0:T(8,128)(2,1)S(1)}, u32[]{:S(2)}, u32[]{:S(2)}) collective-permute-start(bf16[8,128,256]{2,1,0:T(8,128)(2,1)} %get-tuple-element.15), channel_id=1, source_target_pairs={{0,2},{2,0},{1,3},{3,1},{4,6},{6,4},{5,7},{7,5},{8,10},{10,8},{9,1... | collective-permute-start | bytes 1572872 | tf_op jit(solution)/shard_map/ppermute | solution.py:25
  45.8 3.5 %all-to-all-start.1 = ((bf16[16,16,512]{2,1,0:T(8,128)(2,1)}), bf16[16,16,512]{2,1,0:T(8,128)(2,1)S(1)}, u32[]{:S(2)}, u32[]{:S(2)}) async-start(bf16[16,16,512]{2,1,0:T(8,128)(2,1)} %bitcast.10), calls=%async_computation.1 | async-start | bytes 524288 | tf_op jit(solution)/shard_map/all_to_all | solution.py:29
  49.4 2.2 %collective-permute-start.2 = (bf16[8,128,256]{2,1,0:T(8,128)(2,1)}, bf16[8,128,256]{2,1,0:T(8,128)(2,1)}, u32[]{:S(2)}, u32[]{:S(2)}) collective-permute-start(bf16[8,128,256]{2,1,0:T(8,128)(2,1)} %get-tuple-element.13), channel_id=1, source_target_pairs={{0,1},{1,0},{2,3},{3,2},{4,5},{5,4},{6,7},{7,6},{8,9},{9,8},{10,11... | collective-permute-start | bytes 1572872 | tf_op jit(solution)/shard_map/ppermute | solution.py:25
  51.6 10.1 %all-to-all-done.1.first_ref = bf16[16,16,512]{2,1,0:T(8,128)(2,1)S(1)} async-done(((bf16[16,16,512]{2,1,0:T(8,128)(2,1)}), bf16[16,16,512]{2,1,0:T(8,128)(2,1)S(1)}, u32[]{:S(2)}, u32[]{:S(2)}) %all-to-all-start.1) | async-done | bytes 262176 | tf_op jit(solution)/shard_map/all_to_all | solution.py:29
  62.5 2.9 %shard_map.93 = f32[32,16,128]{2,1,0:T(8,128)} custom-call(bf16[16,16,512]{2,1,0:T(8,128)(2,1)} %copy-done.6, f32[32,512]{1,0:T(8,128)} %bitcast.100), custom_call_target="tpu_custom_call" | custom-call | flops 40000000 | bytes 400000 | tf_op jit(solution)/shard_map/pallas_call | solution.py:144
  65.3 6.2 %all-to-all-start.2 = ((f32[32,16,128]{2,1,0:T(8,128)}), f32[32,16,128]{2,1,0:T(8,128)S(1)}, u32[]{:S(2)}, u32[]{:S(2)}) async-start(f32[32,16,128]{2,1,0:T(8,128)} %shard_map.93), calls=%async_computation.2 | async-start | bytes 524288 | tf_op jit(solution)/shard_map/all_to_all | solution.py:29
  78.0 5.8 %all-to-all-done.2.second_ref = f32[32,16,128]{2,1,0:T(8,128)S(1)} async-done(((f32[32,16,128]{2,1,0:T(8,128)}), f32[32,16,128]{2,1,0:T(8,128)S(1)}, u32[]{:S(2)}, u32[]{:S(2)}) %all-to-all-start.2) | async-done | bytes 262176 | tf_op jit(solution)/shard_map/all_to_all | solution.py:29
  84.5 3.7 %shard_map.94 = f32[16,48,128]{2,1,0:T(8,128)} custom-call(f32[32,16,128]{2,1,0:T(8,128)} %copy-done.1, bf16[2048,512]{1,0:T(8,128)(2,1)} %bitcast.97), custom_call_target="tpu_custom_call" | custom-call | flops 500000000 | bytes 5000000 | tf_op jit(solution)/shard_map/pallas_call | solution.py:186
  88.3 6.1 %all-to-all-start.3 = ((f32[16,48,128]{2,1,0:T(8,128)}), f32[16,48,128]{2,1,0:T(8,128)}, u32[]{:S(2)}, u32[]{:S(2)}) async-start(f32[16,48,128]{2,1,0:T(8,128)} %shard_map.94), calls=%async_computation.3 | async-start | bytes 786432 | tf_op jit(solution)/shard_map/all_to_all | solution.py:29
  95.1 3.2 %collective-permute-start.3 = (bf16[4,128,256]{2,1,0:T(8,128)(2,1)}, bf16[4,128,256]{2,1,0:T(8,128)(2,1)}, u32[]{:S(2)}, u32[]{:S(2)}) collective-permute-start(bf16[4,128,256]{2,1,0:T(8,128)(2,1)} %fusion.5), channel_id=1, source_target_pairs={{0,2},{2,0},{1,3},{3,1},{4,6},{6,4},{5,7},{7,5},{8,10},{10,8},{9,1... | collective-permute-start | bytes 786440 | tf_op jit(solution)/shard_map/ppermute | solution.py:25
  99.4 10.7 %collective-permute-done.3 = bf16[4,128,256]{2,1,0:T(8,128)(2,1)} collective-permute-done((bf16[4,128,256]{2,1,0:T(8,128)(2,1)}, bf16[4,128,256]{2,1,0:T(8,128)(2,1)}, u32[]{:S(2)}, u32[]{:S(2)}) %collective-permute-start.3) | collective-permute-done | bytes 262176 | tf_op jit(solution)/shard_map/ppermute | solution.py:25
  112.1 4.7 %collective-permute-start.8 = (bf16[128,512]{1,0:T(8,128)(2,1)}, bf16[128,512]{1,0:T(8,128)(2,1)}, u32[]{:S(2)}, u32[]{:S(2)}) collective-permute-start(bf16[128,512]{1,0:T(8,128)(2,1)} %get-tuple-element.18), channel_id=1, source_target_pairs={{0,12},{4,8},{8,4},{12,0},{1,13},{5,9},{9,5},{13,1},{2,14},{6,10},... | collective-permute-start | bytes 393224 | tf_op jit(solution)/shard_map/ppermute | solution.py:183
  116.9 4.0 %collective-permute-start.7 = (bf16[128,512]{1,0:T(8,128)(2,1)}, bf16[128,512]{1,0:T(8,128)(2,1)}, u32[]{:S(2)}, u32[]{:S(2)}) collective-permute-start(bf16[128,512]{1,0:T(8,128)(2,1)} %get-tuple-element.17), channel_id=1, source_target_pairs={{0,8},{4,12},{8,0},{12,4},{1,9},{5,13},{9,1},{13,5},{2,10},{6,14},... | collective-permute-start | bytes 393224 | tf_op jit(solution)/shard_map/ppermute | solution.py:183
  120.9 2.6 %collective-permute-start.6 = (bf16[128,512]{1,0:T(8,128)(2,1)}, bf16[128,512]{1,0:T(8,128)(2,1)}, u32[]{:S(2)}, u32[]{:S(2)}) collective-permute-start(bf16[128,512]{1,0:T(8,128)(2,1)} %get-tuple-element.16), channel_id=1, source_target_pairs={{0,4},{4,0},{8,12},{12,8},{1,5},{5,1},{9,13},{13,9},{2,6},{6,2},{1... | collective-permute-start | bytes 393224 | tf_op jit(solution)/shard_map/ppermute | solution.py:183
  125.7 2.9 %cholesky.17 = f32[32,32]{1,0:T(8,128)S(1)} custom-call(f32[32,32]{1,0:T(8,128)S(1)} %fusion.35), custom_call_target="Cholesky" | custom-call | tf_op jit(solution)/shard_map/jit(cholesky)/cholesky | solution.py:203
  130.0 2.4 %custom-call.7 = f32[1,32,32]{1,2,0:T(8,128)S(1)} custom-call(f32[1,32,32]{2,1,0:T(8,128)S(1)} %fusion.24), custom_call_target="InvertDiagBlocksLowerTriangular" | custom-call | tf_op jit(solution)/shard_map/jit(_solve_triangular)/triangular_solve | solution.py:204
  133.1 7.2 %all-to-all-start.4 = ((f32[32,16,128]{2,1,0:T(8,128)}), f32[32,16,128]{2,1,0:T(8,128)}, u32[]{:S(2)}, u32[]{:S(2)}) async-start(f32[32,16,128]{2,1,0:T(8,128)} %broadcast_in_dim.15), calls=%async_computation.4 | async-start | bytes 524288 | tf_op jit(solution)/shard_map/all_to_all | solution.py:29
  142.2 10.5 %all-to-all-done.4 = f32[32,16,128]{2,1,0:T(8,128)} async-done(((f32[32,16,128]{2,1,0:T(8,128)}), f32[32,16,128]{2,1,0:T(8,128)}, u32[]{:S(2)}, u32[]{:S(2)}) %all-to-all-start.4) | async-done | bytes 262176 | tf_op jit(solution)/shard_map/all_to_all | solution.py:29
  154.2 2.3 %fusion.3 = (bf16[1,512,512]{2,1,0:T(8,128)(2,1)}, bf16[512,512]{1,0:T(8,128)(2,1)}) fusion(f32[512,512]{1,0:T(8,128)S(1)} %fusion.1, bf16[512,512]{0,1:T(8,128)(2,1)S(1)} %copy-done.4, bf16[512,512]{1,0:T(8,128)(2,1)S(1)} %copy-done.3, f32[512,32]{0,1:T(8,128)S(1)} %fusion.41, f32[512,32]{0,1:T(8,128)S(1)} %fusion.42), kind=kOutput, calls=%fused_computation.18 | convolution fusion | flops 103546880 | bytes 3276800 | tf_op jit(solution)/shard_map/dot_general | solution.py:212
  (68 shorter events, 27.5 us)
Async XLA Ops:
  0.6 10.4 %copy-start.8 = (bf16[512,16]{0,1:T(8,128)(2,1)S(1)}, bf16[512,16]{0,1:T(8,128)(2,1)}, u32[]{:S(2)}) copy-start(bf16[512,16]{0,1:T(8,128)(2,1)} %param.8) | copy-start | bytes 49156
  2.3 16.8 %collective-permute-start = (f32[256,512]{1,0:T(8,128)S(1)}, f32[256,512]{1,0:T(8,128)S(1)}, u32[]{:S(2)}, u32[]{:S(2)}) collective-permute-start(f32[256,512]{1,0:T(8,128)S(1)} %dynamic-slice_bitcast_fusion), channel_id=1, source_target_pairs={{0,16},{16,0},{1,17},{17,1},{2,18},{18,2},{3,19},{19,3},{4,20},{20... | collective-permute-start | bytes 1572872 | tf_op jit(solution)/shard_map/ppermute | solution.py:25
  11.8 20.1 %all-to-all-start = ((bf16[16,16,512]{2,1,0:T(8,128)(2,1)}), bf16[16,16,512]{2,1,0:T(8,128)(2,1)S(1)}, u32[]{:S(2)}, u32[]{:S(2)}) async-start(bf16[16,16,512]{2,1,0:T(8,128)(2,1)} %broadcast_in_dim.14), calls=%async_computation | async-start | bytes 524288 | tf_op jit(solution)/shard_map/all_to_all | solution.py:29
  31.9 4.8 %collective-permute-start.1 = (bf16[16,16,512]{2,1,0:T(8,128)(2,1)S(1)}, bf16[16,16,512]{2,1,0:T(8,128)(2,1)S(1)}, u32[]{:S(2)}, u32[]{:S(2)}) collective-permute-start(bf16[16,16,512]{2,1,0:T(8,128)(2,1)S(1)} %all-to-all-done), channel_id=1, source_target_pairs={{0,16},{16,0},{1,17},{17,1},{2,18},{18,2},{3,19},{19,3},{4,20},{20... | collective-permute-start | bytes 786440 | tf_op jit(solution)/shard_map/ppermute | solution.py:25
  42.5 29.9 %copy-start.5 = (f32[8,128,256]{2,1,0:T(8,128)S(1)}, f32[8,128,256]{2,1,0:T(8,128)}, u32[]{:S(2)}) copy-start(f32[8,128,256]{2,1,0:T(8,128)} %get-tuple-element.14) | copy-start | bytes 3145732
  42.5 29.1 %collective-permute-start.4 = (bf16[8,128,256]{2,1,0:T(8,128)(2,1)}, bf16[8,128,256]{2,1,0:T(8,128)(2,1)S(1)}, u32[]{:S(2)}, u32[]{:S(2)}) collective-permute-start(bf16[8,128,256]{2,1,0:T(8,128)(2,1)} %get-tuple-element.15), channel_id=1, source_target_pairs={{0,2},{2,0},{1,3},{3,1},{4,6},{6,4},{5,7},{7,5},{8,10},{10,8},{9,1... | collective-permute-start | bytes 1572872 | tf_op jit(solution)/shard_map/ppermute | solution.py:25
  45.8 15.9 %all-to-all-start.1 = ((bf16[16,16,512]{2,1,0:T(8,128)(2,1)}), bf16[16,16,512]{2,1,0:T(8,128)(2,1)S(1)}, u32[]{:S(2)}, u32[]{:S(2)}) async-start(bf16[16,16,512]{2,1,0:T(8,128)(2,1)} %bitcast.10), calls=%async_computation.1 | async-start | bytes 524288 | tf_op jit(solution)/shard_map/all_to_all | solution.py:29
  49.4 27.2 %collective-permute-start.2 = (bf16[8,128,256]{2,1,0:T(8,128)(2,1)}, bf16[8,128,256]{2,1,0:T(8,128)(2,1)}, u32[]{:S(2)}, u32[]{:S(2)}) collective-permute-start(bf16[8,128,256]{2,1,0:T(8,128)(2,1)} %get-tuple-element.13), channel_id=1, source_target_pairs={{0,1},{1,0},{2,3},{3,2},{4,5},{5,4},{6,7},{7,6},{8,9},{9,8},{10,11... | collective-permute-start | bytes 1572872 | tf_op jit(solution)/shard_map/ppermute | solution.py:25
  61.8 0.7 copy-start.6
  65.3 18.5 %all-to-all-start.2 = ((f32[32,16,128]{2,1,0:T(8,128)}), f32[32,16,128]{2,1,0:T(8,128)S(1)}, u32[]{:S(2)}, u32[]{:S(2)}) async-start(f32[32,16,128]{2,1,0:T(8,128)} %shard_map.93), calls=%async_computation.2 | async-start | bytes 524288 | tf_op jit(solution)/shard_map/all_to_all | solution.py:29
  71.6 0.8 copy-start.7
  74.3 24.1 %collective-permute-start.5 = (bf16[4,128,256]{2,1,0:T(8,128)(2,1)}, bf16[4,128,256]{2,1,0:T(8,128)(2,1)}, u32[]{:S(2)}, u32[]{:S(2)}) collective-permute-start(bf16[4,128,256]{2,1,0:T(8,128)(2,1)} %fusion.6), channel_id=1, source_target_pairs={{0,1},{1,0},{2,3},{3,2},{4,5},{5,4},{6,7},{7,6},{8,9},{9,8},{10,11... | collective-permute-start | bytes 786440 | tf_op jit(solution)/shard_map/ppermute | solution.py:25
  78.0 20.4 %copy-start = (f32[8,128,256]{2,1,0:T(8,128)}, f32[8,128,256]{2,1,0:T(8,128)S(1)}, u32[]{:S(2)}) copy-start(f32[8,128,256]{2,1,0:T(8,128)S(1)} %convert_add_fusion.1) | copy-start | bytes 3145732
  83.8 0.7 copy-start.1
  88.3 35.2 %all-to-all-start.3 = ((f32[16,48,128]{2,1,0:T(8,128)}), f32[16,48,128]{2,1,0:T(8,128)}, u32[]{:S(2)}, u32[]{:S(2)}) async-start(f32[16,48,128]{2,1,0:T(8,128)} %shard_map.94), calls=%async_computation.3 | async-start | bytes 786432 | tf_op jit(solution)/shard_map/all_to_all | solution.py:29
  95.1 15.0 %collective-permute-start.3 = (bf16[4,128,256]{2,1,0:T(8,128)(2,1)}, bf16[4,128,256]{2,1,0:T(8,128)(2,1)}, u32[]{:S(2)}, u32[]{:S(2)}) collective-permute-start(bf16[4,128,256]{2,1,0:T(8,128)(2,1)} %fusion.5), channel_id=1, source_target_pairs={{0,2},{2,0},{1,3},{3,1},{4,6},{6,4},{5,7},{7,5},{8,10},{10,8},{9,1... | collective-permute-start | bytes 786440 | tf_op jit(solution)/shard_map/ppermute | solution.py:25
  99.4 42.4 %copy-start.2 = (f32[32,16,128]{2,1,0:T(8,128)S(1)}, f32[32,16,128]{2,1,0:T(8,128)}, u32[]{:S(2)}) copy-start(f32[32,16,128]{2,1,0:T(8,128)} %copy-done.1) | copy-start | bytes 786436
  111.3 42.8 %copy-start.3 = (bf16[512,512]{1,0:T(8,128)(2,1)S(1)}, bf16[512,512]{1,0:T(8,128)(2,1)}, u32[]{:S(2)}) copy-start(bf16[512,512]{1,0:T(8,128)(2,1)} %base_ref.1) | copy-start | bytes 1572868
  111.3 42.8 %copy-start.4 = (bf16[512,512]{0,1:T(8,128)(2,1)S(1)}, bf16[512,512]{0,1:T(8,128)(2,1)}, u32[]{:S(2)}) copy-start(bf16[512,512]{0,1:T(8,128)(2,1)} %copy.30) | copy-start | bytes 1572868
  112.1 45.7 %collective-permute-start.8 = (bf16[128,512]{1,0:T(8,128)(2,1)}, bf16[128,512]{1,0:T(8,128)(2,1)}, u32[]{:S(2)}, u32[]{:S(2)}) collective-permute-start(bf16[128,512]{1,0:T(8,128)(2,1)} %get-tuple-element.18), channel_id=1, source_target_pairs={{0,12},{4,8},{8,4},{12,0},{1,13},{5,9},{9,5},{13,1},{2,14},{6,10},... | collective-permute-start | bytes 393224 | tf_op jit(solution)/shard_map/ppermute | solution.py:183
  116.9 40.9 %collective-permute-start.7 = (bf16[128,512]{1,0:T(8,128)(2,1)}, bf16[128,512]{1,0:T(8,128)(2,1)}, u32[]{:S(2)}, u32[]{:S(2)}) collective-permute-start(bf16[128,512]{1,0:T(8,128)(2,1)} %get-tuple-element.17), channel_id=1, source_target_pairs={{0,8},{4,12},{8,0},{12,4},{1,9},{5,13},{9,1},{13,5},{2,10},{6,14},... | collective-permute-start | bytes 393224 | tf_op jit(solution)/shard_map/ppermute | solution.py:183
  120.9 36.9 %collective-permute-start.6 = (bf16[128,512]{1,0:T(8,128)(2,1)}, bf16[128,512]{1,0:T(8,128)(2,1)}, u32[]{:S(2)}, u32[]{:S(2)}) collective-permute-start(bf16[128,512]{1,0:T(8,128)(2,1)} %get-tuple-element.16), channel_id=1, source_target_pairs={{0,4},{4,0},{8,12},{12,8},{1,5},{5,1},{9,13},{13,9},{2,6},{6,2},{1... | collective-permute-start | bytes 393224 | tf_op jit(solution)/shard_map/ppermute | solution.py:183
  133.1 19.5 %all-to-all-start.4 = ((f32[32,16,128]{2,1,0:T(8,128)}), f32[32,16,128]{2,1,0:T(8,128)}, u32[]{:S(2)}, u32[]{:S(2)}) async-start(f32[32,16,128]{2,1,0:T(8,128)} %broadcast_in_dim.15), calls=%async_computation.4 | async-start | bytes 524288 | tf_op jit(solution)/shard_map/all_to_all | solution.py:29

commit v3 on v2

--- a/solution.py
+++ b/solution.py
@@ -107,13 +107,78 @@
         kb_ref[j] = dot(rows((j // 2) * 4 + y0 * 2 + j % 2), right, ((1,), (0,)))
 
 
-def in_vmem(kernel, out_shape, n, mib, flops):
+def shard_sums(third_ref, copies_ref, total_ref):
+    total = jnp.sum(third_ref[...], axis=0)
+    total_ref[...] = total
+    copies_ref[...] = jnp.broadcast_to(
+        total[None, : copies_ref.shape[1]], copies_ref.shape
+    )
+
+
+def bases(total_ref, second_ref, basis_ref, token_ref, inverse_ref, *, own, rank):
+    total = total_ref[...]
+    lanes = total.shape[1]
+    sums, token_sum = total[:own], total[own:]
+    left = jnp.concatenate(
+        [pltpu.roll(sums, lanes - rank, 1), pltpu.roll(sums, lanes - 2 * rank, 1)], axis=0
+    )
+    row = lax.broadcasted_iota(jnp.int32, (rank, lanes), 0)
+    lane = lax.broadcasted_iota(jnp.int32, (rank, lanes), 1)
+    work = jnp.where(lane < rank, left, jnp.where(lane == row + rank, 1.0, 0.0))
+    for j in range(rank - 1):
+        ratio = work[:, j : j + 1] / work[j : j + 1, j : j + 1]
+        work = work - jnp.where(row > j, ratio * work[j : j + 1], 0.0)
+    pivot = jnp.sum(jnp.where(lane == row, work, 0.0), axis=1, keepdims=True)
+    work = jnp.where((lane >= rank) & (lane < 2 * rank), work / jnp.sqrt(pivot), 0.0)
+    rest = jnp.zeros((lanes - rank, lanes), f32)
+    at = [
+        jnp.concatenate([pltpu.roll(work, ((i - 1) * rank) % lanes, 1), rest], axis=0)
+        for i in (0, 2, 3)
+    ]
+    at.insert(1, jnp.concatenate([work, rest], axis=0))
+    flat = second_ref[...].reshape(-1, lanes)
+    basis_ref[...] = dot(flat, at[0], ((1,), (1,)), highest)
+    token_ref[...] = jnp.concatenate(
+        [dot(token_sum, a, ((1,), (1,)), highest) for a in at], axis=0
+    )
+    inverse_ref[...] = at[3]
+
+
+def outputs(
+    fourth_ref, inverse_ref, basis_ref, token_ref, local_ref, base_ref, error_ref,
+    full_ref, momentum_ref, base_out, momentum_out, error_out, key_out, q_scratch,
+):
+    last = ((1,), (1,))
+    rows_, cols = base_ref.shape[0], momentum_ref.shape[0]
+    flat = fourth_ref[...].reshape(-1, fourth_ref.shape[2])
+    q = dot(flat, inverse_ref[...], last, highest)
+    q_scratch[...] = q
+    key_out[...] = own_upd * dot(token_ref[...], q, last, highest)
+    at = lax.axis_index(chips + ("core",)) * cols
+    own_q = q_scratch[pl.ds(pl.multiple_of(at, cols), cols)]
+    momentum_out[...] = (
+        outer_mu * momentum_ref[...].astype(f32)
+        + dot(own_q, basis_ref[...], last, highest)
+    ).astype(bf16)
+    step = rows_ // 4
+    for i in range(4):
+        here = slice(i * step, (i + 1) * step)
+        update = dot(basis_ref[here], q, last, highest)
+        base = base_ref[here].astype(f32)
+        pseudo = base - local_ref[here].astype(f32) + error_ref[here].astype(f32)
+        error_out[here] = (pseudo - update).astype(bf16)
+        moment = outer_mu * full_ref[here].astype(f32) + update
+        base_out[here] = (base - outer_rate * (outer_mu * moment + update)).astype(bf16)
+
+
+def in_vmem(kernel, out_shape, n, mib, flops, scratch=()):
     whole = pl.BlockSpec(memory_space=pltpu.VMEM)
     return pl.pallas_call(
         kernel,
         out_shape=out_shape,
         in_specs=[whole] * n,
         out_specs=jax.tree.map(lambda _: whole, out_shape),
+        scratch_shapes=scratch,
         cost_estimate=pl.CostEstimate(
             flops=flops, bytes_accessed=flops // 100, transcendentals=0
         ),
@@ -175,13 +240,9 @@
     quarter = (shards // 4, 2, block, kv // 2)
     key_a = halve(key_a.reshape(quarter), "y0", 1)
     key_b = halve(key_b.reshape(quarter), "xl", 1)
-    key_part = jnp.concatenate([key_a, key_b], axis=-1)
-    place = lax.axis_index(("y2", "y1"))
-    key_sum = pick(key_part, place, 0)
-    for d in (1, 2, 3):
-        away = pick(key_part, place ^ d, 0).astype(bf16)
-        away = lax.ppermute(away, ("y2", "y1"), [(i, i ^ d) for i in range(4)])
-        key_sum = key_sum + away.astype(f32)
+    key_part = jnp.concatenate([key_a, key_b], axis=-1).reshape(2, 2, block, kv)
+    key_part = halve(key_part, "y1", 1)
+    key_sum = halve(key_part, "y2", 0)
 
     third = in_vmem(
         functools.partial(token_products, own=own, rank=rank),
@@ -191,40 +252,51 @@
         500000000,
     )(second, own_tokens)
     third = exchange(third, shard)
-    third = jnp.sum(third, axis=0)
-    sums, token_sum = third[:own], third[own:]
-    fourth = copy_for_each(sums, peers)
-
-    token_sum = jnp.concatenate(
-        [token_sum[:, i * rank : (i + 1) * rank] for i in range(4)], axis=0
-    )
-    gram = jnp.concatenate([sums[:, rank : 2 * rank], sums[:, 2 * rank : 3 * rank]], axis=0)
-    p_mean = second[:, :, :rank].reshape(rows, rank)
-    factor_low = jnp.linalg.cholesky(gram)
-    inverse = jax.scipy.linalg.solve_triangular(
-        factor_low, jnp.eye(rank, dtype=f32), lower=True
-    )
-    basis = jnp.dot(p_mean, inverse.T, precision=highest)
-    token_basis = jnp.dot(token_sum, inverse.T, precision=highest)
-
-    q_sum = fourth[:, :, 3 * rank :].reshape(kv, rank)
-    q_mean = jnp.dot(q_sum, inverse.T, precision=highest)
-    update = jnp.dot(basis, q_mean.T, precision=highest)
-    new_error = (pseudo - update).astype(bf16)[None]
-    moment = outer_mu * full_momentum.astype(f32) + update
-    new_base = (base - outer_rate * (outer_mu * moment + update)).astype(bf16)
-    at = lax.axis_index(chips + ("core",)) * cols
-    own_q = lax.dynamic_slice_in_dim(q_mean, at, cols, 0)
-    new_momentum = outer_mu * momentum.astype(f32) + jnp.dot(
-        basis, own_q.T, precision=highest
-    )
-    key_rows = key_sum - own_upd * jnp.dot(token_basis, q_mean.T, precision=highest)
-    return (
-        new_base,
-        new_momentum.astype(bf16),
-        new_error,
-        key_rows.astype(bf16)[None],
-    )
+    lanes = 4 * rank
+    copies, total = in_vmem(
+        shard_sums,
+        (shape((replicas, own, lanes), f32), shape(third.shape[1:], f32)),
+        1,
+        0,
+        1000000,
+    )(third)
+    fourth = exchange(copies, peers)
+    basis, token_basis, inverse = in_vmem(
+        functools.partial(bases, own=own, rank=rank),
+        (
+            shape((rows, lanes), f32),
+            shape((block, lanes), f32),
+            shape((lanes, lanes), f32),
+        ),
+        2,
+        0,
+        100000000,
+    )(total, second)
+    new_base, new_momentum, new_error, key_low = in_vmem(
+        outputs,
+        (
+            shape((rows, kv), bf16),
+            shape((cols, rows), bf16),
+            shape((rows, kv), bf16),
+            shape((block, kv), f32),
+        ),
+        9,
+        0,
+        400000000,
+        (pltpu.VMEM((kv, lanes), f32),),
+    )(
+        fourth,
+        inverse,
+        basis,
+        token_basis,
+        local_weights[0],
+        outer_base,
+        error_feedback[0],
+        full_momentum,
+        momentum.T,
+    )
+    key_rows = (key_sum - key_low).astype(bf16)
+    return new_base, new_momentum.T, new_error[None], key_rows[None]
 
 
 def solution(mesh):

time: 161 us -> 143 us (0.89)
  waiting for transfers between devices: 50.4 us -> 36.6 us
  Pallas kernels: 11.3 us -> 22.9 us
  other arithmetic: 17.6 us -> 7.66 us
  matrix products: 4.81 us -> 0 us
  local copies, waits for them, and re-layouts: 9.36 us -> 6.39 us
  starting transfers between devices: 65 us -> 67 us
    pallas_call x0 -> x3, Pallas kernels: none -> 11.5 us  [the longest x1 4.93 us: on_device(): in_vmem(functools.partial(bases, own=own, rank=rank), (shape((rows, lanes...]
    ppermute x3 -> x0, starting transfers between devices: 11.4 us -> none  [on_device(): away = lax.ppermute(away, ('y2', 'y1'), [(i, i ^ d) for i in range(4)])]
    ppermute x6 -> x8, waiting for transfers between devices: 11.9 us -> 1.15 us  [swap(): return lax.ppermute(x, axis, [(0, 1), (1, 0)])]
    ppermute x6 -> x8, starting transfers between devices: 23.3 us -> 31 us  [swap(): return lax.ppermute(x, axis, [(0, 1), (1, 0)])]
    another operation x5 -> x0, other arithmetic: 6.69 us -> none  [the longest x3 3.6 us: on_device(): factor_low = jnp.linalg.cholesky(gram)]
    all_to_all x5, starting transfers between devices: 30.3 us -> 36 us  [exchange(): return lax.all_to_all(x, axis, 0, 0, tiled=True)]
    dot_general x6 -> x0, matrix products: 4.62 us -> none  [the longest x1 2.27 us: on_device(): update = jnp.dot(basis, q_mean.T, precision=highest)]
    all_to_all x5, waiting for transfers between devices: 38.5 us -> 35.5 us  [exchange(): return lax.all_to_all(x, axis, 0, 0, tiled=True)]
  transfers between devices with their start and end apart: 14 -> 13, of which waited for: 6 -> 6; matrix products, arithmetic and copies ran while one was open for 16% -> 4% of each run, Pallas kernels for 4% -> 13%
where the time goes in v3:
time: 143 us; the launch traced here: 142 us
  starting transfers between devices  67 us (47%)
  waiting for transfers between devices  36.6 us (26%)
  Pallas kernels  22.9 us (16%)
  other arithmetic  7.66 us (5%)
  local copies, waits for them, and re-layouts  6.39 us (4%)
    all_to_all x5, starting transfers between devices, exchange(): return lax.all_to_all(x, axis, 0, 0, tiled=True)  36 us
    all_to_all x5, waiting for transfers between devices, exchange(): return lax.all_to_all(x, axis, 0, 0, tiled=True)  35.5 us
    ppermute x8, starting transfers between devices, swap(): return lax.ppermute(x, axis, [(0, 1), (1, 0)])  31 us
    pallas_call x1, Pallas kernels, on_device(): in_vmem(functools.partial(bases, own=own, rank=rank), (shape((rows, lanes...  4.93 us
    pallas_call x1, Pallas kernels, on_device(): in_vmem(outputs, (shape((rows, kv), bf16), shape((cols, rows), bf16), sha...  4.82 us
    pallas_call x1, Pallas kernels, on_device(): in_vmem(key_products, (shape(part, bf16), shape(part, f32), shape(part, b...  4.7 us
    pallas_call x1, Pallas kernels, on_device(): in_vmem(functools.partial(token_products, own=own, rank=rank), shape((sha...  3.74 us
    unnamed x16, local copies, waits for them, and re-layouts  3.7 us
  transfers between devices with their start and end apart: 13, of which 6 were waited for; matrix products, arithmetic and copies ran while one was open for 4% of the time, Pallas kernels for 13%

profile of v3, /device:TPU:1, one launch (start us, length us, event | category | flops | bytes accessed | tf_op | source)
XLA Modules:
  0.0 141.5 jit_solution(3649847514497780748)
XLA Ops:
  2.3 8.7 %collective-permute-start = (f32[256,512]{1,0:T(8,128)S(1)}, f32[256,512]{1,0:T(8,128)S(1)}, u32[]{:S(2)}, u32[]{:S(2)}) collective-permute-start(f32[256,512]{1,0:T(8,128)S(1)} %dynamic-slice_bitcast_fusion), channel_id=1, source_target_pairs={{0,16},{16,0},{1,17},{17,1},{2,18},{18,2},{3,19},{19,3},{4,20},{20... | collective-permute-start | bytes 1572872 | tf_op jit(solution)/shard_map/ppermute | solution.py:25
  11.8 7.3 %all-to-all-start = ((bf16[16,16,512]{2,1,0:T(8,128)(2,1)}), bf16[16,16,512]{2,1,0:T(8,128)(2,1)S(1)}, u32[]{:S(2)}, u32[]{:S(2)}) async-start(bf16[16,16,512]{2,1,0:T(8,128)(2,1)} %broadcast_in_dim.9), calls=%async_computation | async-start | bytes 524288 | tf_op jit(solution)/shard_map/all_to_all | solution.py:29
  19.8 12.1 %all-to-all-done = bf16[16,16,512]{2,1,0:T(8,128)(2,1)S(1)} async-done(((bf16[16,16,512]{2,1,0:T(8,128)(2,1)}), bf16[16,16,512]{2,1,0:T(8,128)(2,1)S(1)}, u32[]{:S(2)}, u32[]{:S(2)}) %all-to-all-start) | async-done | bytes 262176 | tf_op jit(solution)/shard_map/all_to_all | solution.py:29
  31.9 3.6 %collective-permute-start.1 = (bf16[16,16,512]{2,1,0:T(8,128)(2,1)S(1)}, bf16[16,16,512]{2,1,0:T(8,128)(2,1)S(1)}, u32[]{:S(2)}, u32[]{:S(2)}) collective-permute-start(bf16[16,16,512]{2,1,0:T(8,128)(2,1)S(1)} %all-to-all-done), channel_id=1, source_target_pairs={{0,16},{16,0},{1,17},{17,1},{2,18},{18,2},{3,19},{19,3},{4,20},{20... | collective-permute-start | bytes 786440 | tf_op jit(solution)/shard_map/ppermute | solution.py:25
  37.8 4.7 %shard_map.98 = (bf16[8,128,256]{2,1,0:T(8,128)(2,1)}, f32[8,128,256]{2,1,0:T(8,128)}, bf16[8,128,256]{2,1,0:T(8,128)(2,1)}, f32[8,128,256]{2,1,0:T(8,128)}) custom-call(bf16[2048,512]{1,0:T(8,128)(2,1)} %bitcast.70, bf16[512,512]{1,0:T(8,128)(2,1)} %base_ref.3, bf16[512,512]{1,0:T(8,128)(2,1)} %bitcast.75), custom_call_target="tpu_custom_call" | custom-call | flops 1073741824 | bytes 10737418 | tf_op jit(solution)/shard_map/pallas_call | solution.py:229
  42.5 2.3 %collective-permute-start.2 = (bf16[8,128,256]{2,1,0:T(8,128)(2,1)}, bf16[8,128,256]{2,1,0:T(8,128)(2,1)S(1)}, u32[]{:S(2)}, u32[]{:S(2)}) collective-permute-start(bf16[8,128,256]{2,1,0:T(8,128)(2,1)} %get-tuple-element.30), channel_id=1, source_target_pairs={{0,1},{1,0},{2,3},{3,2},{4,5},{5,4},{6,7},{7,6},{8,9},{9,8},{10,11... | collective-permute-start | bytes 1572872 | tf_op jit(solution)/shard_map/ppermute | solution.py:25
  44.9 3.5 %all-to-all-start.1 = ((bf16[16,16,512]{2,1,0:T(8,128)(2,1)}), bf16[16,16,512]{2,1,0:T(8,128)(2,1)S(1)}, u32[]{:S(2)}, u32[]{:S(2)}) async-start(bf16[16,16,512]{2,1,0:T(8,128)(2,1)} %bitcast.6), calls=%async_computation.1 | async-start | bytes 524288 | tf_op jit(solution)/shard_map/all_to_all | solution.py:29
  48.4 3.2 %collective-permute-start.4 = (bf16[8,128,256]{2,1,0:T(8,128)(2,1)}, bf16[8,128,256]{2,1,0:T(8,128)(2,1)}, u32[]{:S(2)}, u32[]{:S(2)}) collective-permute-start(bf16[8,128,256]{2,1,0:T(8,128)(2,1)} %get-tuple-element.32), channel_id=1, source_target_pairs={{0,2},{2,0},{1,3},{3,1},{4,6},{6,4},{5,7},{7,5},{8,10},{10,8},{9,1... | collective-permute-start | bytes 1572872 | tf_op jit(solution)/shard_map/ppermute | solution.py:25
  51.7 9.2 %all-to-all-done.1.first_ref = bf16[16,16,512]{2,1,0:T(8,128)(2,1)S(1)} async-done(((bf16[16,16,512]{2,1,0:T(8,128)(2,1)}), bf16[16,16,512]{2,1,0:T(8,128)(2,1)S(1)}, u32[]{:S(2)}, u32[]{:S(2)}) %all-to-all-start.1) | async-done | bytes 262176 | tf_op jit(solution)/shard_map/all_to_all | solution.py:29
  61.6 3.0 %shard_map.93 = f32[32,16,128]{2,1,0:T(8,128)} custom-call(bf16[16,16,512]{2,1,0:T(8,128)(2,1)} %copy-done.3, f32[32,512]{1,0:T(8,128)} %bitcast.79), custom_call_target="tpu_custom_call" | custom-call | flops 40000000 | bytes 400000 | tf_op jit(solution)/shard_map/pallas_call | solution.py:209
  64.5 6.1 %all-to-all-start.2 = ((f32[32,16,128]{2,1,0:T(8,128)}), f32[32,16,128]{2,1,0:T(8,128)S(1)}, u32[]{:S(2)}, u32[]{:S(2)}) async-start(f32[32,16,128]{2,1,0:T(8,128)} %shard_map.93), calls=%async_computation.2 | async-start | bytes 524288 | tf_op jit(solution)/shard_map/all_to_all | solution.py:29
  73.4 3.2 %collective-permute-start.3 = (bf16[4,128,256]{2,1,0:T(8,128)(2,1)}, bf16[4,128,256]{2,1,0:T(8,128)(2,1)}, u32[]{:S(2)}, u32[]{:S(2)}) collective-permute-start(bf16[4,128,256]{2,1,0:T(8,128)(2,1)} %fusion.1), channel_id=1, source_target_pairs={{0,2},{2,0},{1,3},{3,1},{4,6},{6,4},{5,7},{7,5},{8,10},{10,8},{9,1... | collective-permute-start | bytes 786440 | tf_op jit(solution)/shard_map/ppermute | solution.py:25
  77.8 3.1 %collective-permute-start.5 = (bf16[4,128,256]{2,1,0:T(8,128)(2,1)S(1)}, bf16[4,128,256]{2,1,0:T(8,128)(2,1)S(1)}, u32[]{:S(2)}, u32[]{:S(2)}) collective-permute-start(bf16[4,128,256]{2,1,0:T(8,128)(2,1)S(1)} %fusion.2), channel_id=1, source_target_pairs={{0,1},{1,0},{2,3},{3,2},{4,5},{5,4},{6,7},{7,6},{8,9},{9,8},{10,11... | collective-permute-start | bytes 786440 | tf_op jit(solution)/shard_map/ppermute | solution.py:25
  80.9 2.1 %all-to-all-done.2.second_ref = f32[32,16,128]{2,1,0:T(8,128)S(1)} async-done(((f32[32,16,128]{2,1,0:T(8,128)}), f32[32,16,128]{2,1,0:T(8,128)S(1)}, u32[]{:S(2)}, u32[]{:S(2)}) %all-to-all-start.2) | async-done | bytes 262176 | tf_op jit(solution)/shard_map/all_to_all | solution.py:29
  83.6 3.7 %shard_map.94 = f32[16,48,128]{2,1,0:T(8,128)} custom-call(f32[32,16,128]{2,1,0:T(8,128)} %copy-done.4, bf16[2048,512]{1,0:T(8,128)(2,1)} %bitcast.71), custom_call_target="tpu_custom_call" | custom-call | flops 500000000 | bytes 5000000 | tf_op jit(solution)/shard_map/pallas_call | solution.py:247
  87.4 7.8 %all-to-all-start.3 = ((f32[16,48,128]{2,1,0:T(8,128)}), f32[16,48,128]{2,1,0:T(8,128)S(1)}, u32[]{:S(2)}, u32[]{:S(2)}) async-start(f32[16,48,128]{2,1,0:T(8,128)} %shard_map.94), calls=%async_computation.3 | async-start | bytes 786432 | tf_op jit(solution)/shard_map/all_to_all | solution.py:29
  96.5 4.2 %collective-permute-start.6 = (bf16[2,128,512]{2,1,0:T(8,128)(2,1)S(1)}, bf16[2,128,512]{2,1,0:T(8,128)(2,1)S(1)}, u32[]{:S(2)}, u32[]{:S(2)}) collective-permute-start(bf16[2,128,512]{2,1,0:T(8,128)(2,1)S(1)} %fusion.3), channel_id=1, source_target_pairs={{0,4},{4,0},{1,5},{5,1},{2,6},{6,2},{3,7},{7,3},{8,12},{12,8},{9,1... | collective-permute-start | bytes 786440 | tf_op jit(solution)/shard_map/ppermute | solution.py:25
  100.7 7.6 %all-to-all-done.3.third_ref = f32[16,48,128]{2,1,0:T(8,128)S(1)} async-done(((f32[16,48,128]{2,1,0:T(8,128)}), f32[16,48,128]{2,1,0:T(8,128)S(1)}, u32[]{:S(2)}, u32[]{:S(2)}) %all-to-all-start.3) | async-done | bytes 393248 | tf_op jit(solution)/shard_map/all_to_all | solution.py:29
  109.0 1.7 %shard_map.95 = (f32[32,16,128]{2,1,0:T(8,128)}, f32[48,128]{1,0:T(8,128)}) custom-call(f32[16,48,128]{2,1,0:T(8,128)} %copy-done), custom_call_target="tpu_custom_call" | custom-call | flops 1000000 | bytes 10000 | tf_op jit(solution)/shard_map/pallas_call | solution.py:256
  110.8 11.3 %all-to-all-start.4 = ((f32[32,16,128]{2,1,0:T(8,128)}), f32[32,16,128]{2,1,0:T(8,128)S(1)}, u32[]{:S(2)}, u32[]{:S(2)}) async-start(f32[32,16,128]{2,1,0:T(8,128)} %get-tuple-element.20), calls=%async_computation.4 | async-start | bytes 524288 | tf_op jit(solution)/shard_map/all_to_all | solution.py:29
  122.2 2.7 %collective-permute-start.7 = (bf16[128,512]{1,0:T(8,128)(2,1)S(1)}, bf16[128,512]{1,0:T(8,128)(2,1)S(1)}, u32[]{:S(2)}, u32[]{:S(2)}) collective-permute-start(bf16[128,512]{1,0:T(8,128)(2,1)S(1)} %fusion.6), channel_id=1, source_target_pairs={{0,8},{8,0},{1,9},{9,1},{2,10},{10,2},{3,11},{11,3},{4,12},{12,4},... | collective-permute-start | bytes 393224 | tf_op jit(solution)/shard_map/ppermute | solution.py:25
  124.8 4.9 %shard_map.96 = (f32[512,128]{1,0:T(8,128)}, f32[128,128]{1,0:T(8,128)}, f32[128,128]{1,0:T(8,128)}) custom-call(f32[48,128]{1,0:T(8,128)} %get-tuple-element.21.total_ref, f32[32,16,128]{2,1,0:T(8,128)} %copy-done.4), custom_call_target="tpu_custom_call" | custom-call | flops 100000000 | bytes 1000000 | tf_op jit(solution)/shard_map/pallas_call | solution.py:264
  129.8 4.5 %all-to-all-done.4.fourth_ref = f32[32,16,128]{2,1,0:T(8,128)S(1)} async-done(((f32[32,16,128]{2,1,0:T(8,128)}), f32[32,16,128]{2,1,0:T(8,128)S(1)}, u32[]{:S(2)}, u32[]{:S(2)}) %all-to-all-start.4) | async-done | bytes 262176 | tf_op jit(solution)/shard_map/all_to_all | solution.py:29
  135.0 4.8 %shard_map.97 = (bf16[512,512]{1,0:T(8,128)(2,1)}, bf16[16,512]{1,0:T(8,128)(2,1)}, bf16[512,512]{1,0:T(8,128)(2,1)}, f32[128,512]{1,0:T(8,128)}) custom-call(f32[32,16,128]{2,1,0:T(8,128)} %copy-done.5, f32[128,128]{1,0:T(8,128)} %get-tuple-element.22.inverse_ref, f32[512,128]{1,0:T(8,128)} %get-tuple-element.23.basis_ref, ...), custom_call_target="tpu_custom_call" | custom-call | flops 400000000 | bytes 4000000 | tf_op jit(solution)/shard_map/pallas_call | solution.py:275
  (43 shorter events, 15.2 us)
Async XLA Ops:
  0.6 10.4 %copy-start.7 = (bf16[512,16]{0,1:T(8,128)(2,1)S(1)}, bf16[512,16]{0,1:T(8,128)(2,1)}, u32[]{:S(2)}) copy-start(bf16[512,16]{0,1:T(8,128)(2,1)} %param.8) | copy-start | bytes 49156
  2.3 16.8 %collective-permute-start = (f32[256,512]{1,0:T(8,128)S(1)}, f32[256,512]{1,0:T(8,128)S(1)}, u32[]{:S(2)}, u32[]{:S(2)}) collective-permute-start(f32[256,512]{1,0:T(8,128)S(1)} %dynamic-slice_bitcast_fusion), channel_id=1, source_target_pairs={{0,16},{16,0},{1,17},{17,1},{2,18},{18,2},{3,19},{19,3},{4,20},{20... | collective-permute-start | bytes 1572872 | tf_op jit(solution)/shard_map/ppermute | solution.py:25
  11.8 20.1 %all-to-all-start = ((bf16[16,16,512]{2,1,0:T(8,128)(2,1)}), bf16[16,16,512]{2,1,0:T(8,128)(2,1)S(1)}, u32[]{:S(2)}, u32[]{:S(2)}) async-start(bf16[16,16,512]{2,1,0:T(8,128)(2,1)} %broadcast_in_dim.9), calls=%async_computation | async-start | bytes 524288 | tf_op jit(solution)/shard_map/all_to_all | solution.py:29
  31.9 4.8 %collective-permute-start.1 = (bf16[16,16,512]{2,1,0:T(8,128)(2,1)S(1)}, bf16[16,16,512]{2,1,0:T(8,128)(2,1)S(1)}, u32[]{:S(2)}, u32[]{:S(2)}) collective-permute-start(bf16[16,16,512]{2,1,0:T(8,128)(2,1)S(1)} %all-to-all-done), channel_id=1, source_target_pairs={{0,16},{16,0},{1,17},{17,1},{2,18},{18,2},{3,19},{19,3},{4,20},{20... | collective-permute-start | bytes 786440 | tf_op jit(solution)/shard_map/ppermute | solution.py:25
  42.5 28.9 %copy-start.2 = (f32[8,128,256]{2,1,0:T(8,128)S(1)}, f32[8,128,256]{2,1,0:T(8,128)}, u32[]{:S(2)}) copy-start(f32[8,128,256]{2,1,0:T(8,128)} %get-tuple-element.29) | copy-start | bytes 3145732
  42.5 28.1 %collective-permute-start.2 = (bf16[8,128,256]{2,1,0:T(8,128)(2,1)}, bf16[8,128,256]{2,1,0:T(8,128)(2,1)S(1)}, u32[]{:S(2)}, u32[]{:S(2)}) collective-permute-start(bf16[8,128,256]{2,1,0:T(8,128)(2,1)} %get-tuple-element.30), channel_id=1, source_target_pairs={{0,1},{1,0},{2,3},{3,2},{4,5},{5,4},{6,7},{7,6},{8,9},{9,8},{10,11... | collective-permute-start | bytes 1572872 | tf_op jit(solution)/shard_map/ppermute | solution.py:25
  44.9 15.9 %all-to-all-start.1 = ((bf16[16,16,512]{2,1,0:T(8,128)(2,1)}), bf16[16,16,512]{2,1,0:T(8,128)(2,1)S(1)}, u32[]{:S(2)}, u32[]{:S(2)}) async-start(bf16[16,16,512]{2,1,0:T(8,128)(2,1)} %bitcast.6), calls=%async_computation.1 | async-start | bytes 524288 | tf_op jit(solution)/shard_map/all_to_all | solution.py:29
  48.4 28.2 %collective-permute-start.4 = (bf16[8,128,256]{2,1,0:T(8,128)(2,1)}, bf16[8,128,256]{2,1,0:T(8,128)(2,1)}, u32[]{:S(2)}, u32[]{:S(2)}) collective-permute-start(bf16[8,128,256]{2,1,0:T(8,128)(2,1)} %get-tuple-element.32), channel_id=1, source_target_pairs={{0,2},{2,0},{1,3},{3,1},{4,6},{6,4},{5,7},{7,5},{8,10},{10,8},{9,1... | collective-permute-start | bytes 1572872 | tf_op jit(solution)/shard_map/ppermute | solution.py:25
  60.8 0.7 copy-start.3
  61.6 15.0 %copy-start.1 = (f32[8,128,256]{2,1,0:T(8,128)S(1)}, f32[8,128,256]{2,1,0:T(8,128)}, u32[]{:S(2)}) copy-start(f32[8,128,256]{2,1,0:T(8,128)} %get-tuple-element.31) | copy-start | bytes 3145732
  64.5 18.4 %all-to-all-start.2 = ((f32[32,16,128]{2,1,0:T(8,128)}), f32[32,16,128]{2,1,0:T(8,128)S(1)}, u32[]{:S(2)}, u32[]{:S(2)}) async-start(f32[32,16,128]{2,1,0:T(8,128)} %shard_map.93), calls=%async_computation.2 | async-start | bytes 524288 | tf_op jit(solution)/shard_map/all_to_all | solution.py:29
  70.7 0.8 copy-start.6
  73.4 21.8 %collective-permute-start.3 = (bf16[4,128,256]{2,1,0:T(8,128)(2,1)}, bf16[4,128,256]{2,1,0:T(8,128)(2,1)}, u32[]{:S(2)}, u32[]{:S(2)}) collective-permute-start(bf16[4,128,256]{2,1,0:T(8,128)(2,1)} %fusion.1), channel_id=1, source_target_pairs={{0,2},{2,0},{1,3},{3,1},{4,6},{6,4},{5,7},{7,5},{8,10},{10,8},{9,1... | collective-permute-start | bytes 786440 | tf_op jit(solution)/shard_map/ppermute | solution.py:25
  77.8 18.4 %collective-permute-start.5 = (bf16[4,128,256]{2,1,0:T(8,128)(2,1)S(1)}, bf16[4,128,256]{2,1,0:T(8,128)(2,1)S(1)}, u32[]{:S(2)}, u32[]{:S(2)}) collective-permute-start(bf16[4,128,256]{2,1,0:T(8,128)(2,1)S(1)} %fusion.2), channel_id=1, source_target_pairs={{0,1},{1,0},{2,3},{3,2},{4,5},{5,4},{6,7},{7,6},{8,9},{9,8},{10,11... | collective-permute-start | bytes 786440 | tf_op jit(solution)/shard_map/ppermute | solution.py:25
  82.9 0.7 copy-start.4
  87.4 20.9 %all-to-all-start.3 = ((f32[16,48,128]{2,1,0:T(8,128)}), f32[16,48,128]{2,1,0:T(8,128)S(1)}, u32[]{:S(2)}, u32[]{:S(2)}) async-start(f32[16,48,128]{2,1,0:T(8,128)} %shard_map.94), calls=%async_computation.3 | async-start | bytes 786432 | tf_op jit(solution)/shard_map/all_to_all | solution.py:29
  96.5 25.6 %collective-permute-start.6 = (bf16[2,128,512]{2,1,0:T(8,128)(2,1)S(1)}, bf16[2,128,512]{2,1,0:T(8,128)(2,1)S(1)}, u32[]{:S(2)}, u32[]{:S(2)}) collective-permute-start(bf16[2,128,512]{2,1,0:T(8,128)(2,1)S(1)} %fusion.3), channel_id=1, source_target_pairs={{0,4},{4,0},{1,5},{5,1},{2,6},{6,2},{3,7},{7,3},{8,12},{12,8},{9,1... | collective-permute-start | bytes 786440 | tf_op jit(solution)/shard_map/ppermute | solution.py:25
  108.3 0.7 copy-start
  110.8 23.5 %all-to-all-start.4 = ((f32[32,16,128]{2,1,0:T(8,128)}), f32[32,16,128]{2,1,0:T(8,128)S(1)}, u32[]{:S(2)}, u32[]{:S(2)}) async-start(f32[32,16,128]{2,1,0:T(8,128)} %get-tuple-element.20), calls=%async_computation.4 | async-start | bytes 524288 | tf_op jit(solution)/shard_map/all_to_all | solution.py:29
  122.2 17.7 %collective-permute-start.7 = (bf16[128,512]{1,0:T(8,128)(2,1)S(1)}, bf16[128,512]{1,0:T(8,128)(2,1)S(1)}, u32[]{:S(2)}, u32[]{:S(2)}) collective-permute-start(bf16[128,512]{1,0:T(8,128)(2,1)S(1)} %fusion.6), channel_id=1, source_target_pairs={{0,8},{8,0},{1,9},{9,1},{2,10},{10,2},{3,11},{11,3},{4,12},{12,4},... | collective-permute-start | bytes 393224 | tf_op jit(solution)/shard_map/ppermute | solution.py:25
  134.3 0.7 copy-start.5

commit v4 on v3

--- a/solution.py
+++ b/solution.py
@@ -53,7 +53,7 @@
     return lax.broadcasted_iota(jnp.int32, shape, 1) // rank
 
 
-def moments(first_ref, q_ref, out_ref, *, own, rank, replicas):
+def moments(first_ref, q_ref, hbm_ref, out_ref, *, own, rank, replicas):
     mean = jnp.sum(first_ref[...].astype(f32), axis=0) * (1.0 / replicas)
     q = jnp.concatenate([q_ref[...]] * 4, axis=0)
     p = dot(mean, q, ((1,), (1,)), highest)
@@ -64,9 +64,10 @@
     same = p_at[0] + upper[:own] + lower[own : 2 * own]
     q_rows = dot(mean, p_at[3], ((0,), (0,)), highest)
     out_ref[...] = q_rows.reshape(out_ref.shape) + same[None]
-
-
-def token_products(second_ref, tokens_ref, out_ref, *, own, rank):
+    pltpu.sync_copy(out_ref, hbm_ref)
+
+
+def token_products(second_ref, tokens_ref, hbm_ref, out_ref, *, own, rank):
     peers_, rows_, lanes = second_ref.shape
     shards = out_ref.shape[0]
     block = tokens_ref.shape[0] // shards
@@ -85,34 +86,44 @@
         total = total + dot(part, high, ((1,), (0,))) + dot(part, low, ((1,), (0,)))
     out_ref[:, :own] = jnp.broadcast_to(sums[None], (shards, own, lanes))
     out_ref[:, own:] = total.reshape(shards, step, lanes)
-
-
-def key_products(tokens_ref, base_ref, momentum_ref, sa_ref, ka_ref, sb_ref, kb_ref):
-    xl, y0 = lax.axis_index("xl"), lax.axis_index("y0")
-    block, half = sa_ref.shape[1:]
+    pltpu.sync_copy(out_ref, hbm_ref)
+
+
+def key_products(
+    tokens_ref, base_ref, momentum_ref, left_ref, right_ref, keep_ref, sent, sems
+):
+    y0 = lax.axis_index("y0")
     settled = base_ref[...].astype(f32) - own_mom * momentum_ref[...].astype(f32)
     settled = settled.astype(bf16)
-    left, right = settled[:, :half], settled[:, half:]
-
-    def rows(i):
-        return tokens_ref[pl.ds(pl.multiple_of(i * block, block), block)]
-
-    for j in range(sa_ref.shape[0]):
-        sa_ref[j] = dot(rows(2 * j + 1 - xl), left, ((1,), (0,))).astype(bf16)
-        sb_ref[j] = dot(
-            rows((j // 2) * 4 + (1 - y0) * 2 + j % 2), right, ((1,), (0,))
-        ).astype(bf16)
-    for j in range(sa_ref.shape[0]):
-        ka_ref[j] = dot(rows(2 * j + xl), left, ((1,), (0,)))
-        kb_ref[j] = dot(rows((j // 2) * 4 + y0 * 2 + j % 2), right, ((1,), (0,)))
-
-
-def shard_sums(third_ref, copies_ref, total_ref):
+    groups, block, cols = keep_ref.shape[0] // 2, keep_ref.shape[1], keep_ref.shape[2]
+    half = cols // 2
+
+    def product(i, parity):
+        at = pl.multiple_of((2 * i + parity) * 2 * block, 2 * block)
+        part = dot(tokens_ref[pl.ds(at, 2 * block)], settled, ((1,), (0,)))
+        return part.reshape(2, block, cols)
+
+    for i in range(groups):
+        sent[2 * i : 2 * i + 2] = product(i, 1 - y0).astype(bf16)
+    copies = [
+        pltpu.make_async_copy(sent.at[:, :, :half], left_ref, sems.at[0]),
+        pltpu.make_async_copy(sent.at[:, :, half:], right_ref, sems.at[1]),
+    ]
+    for copy in copies:
+        copy.start()
+    for i in range(groups):
+        keep_ref[2 * i : 2 * i + 2] = product(i, y0)
+    for copy in copies:
+        copy.wait()
+
+
+def shard_sums(third_ref, hbm_ref, total_ref, copies_ref):
     total = jnp.sum(third_ref[...], axis=0)
     total_ref[...] = total
     copies_ref[...] = jnp.broadcast_to(
         total[None, : copies_ref.shape[1]], copies_ref.shape
     )
+    pltpu.sync_copy(copies_ref, hbm_ref)
 
 
 def bases(total_ref, second_ref, basis_ref, token_ref, inverse_ref, *, own, rank):
@@ -171,18 +182,19 @@
         base_out[here] = (base - outer_rate * (outer_mu * moment + update)).astype(bf16)
 
 
-def in_vmem(kernel, out_shape, n, mib, flops, scratch=()):
+def in_vmem(kernel, out_shape, n, mib, flops, scratch=(), far=0):
     whole = pl.BlockSpec(memory_space=pltpu.VMEM)
+    hbm = pl.BlockSpec(memory_space=pltpu.HBM)
     return pl.pallas_call(
         kernel,
         out_shape=out_shape,
         in_specs=[whole] * n,
-        out_specs=jax.tree.map(lambda _: whole, out_shape),
+        out_specs=tuple(hbm if i < far else whole for i in range(len(out_shape))),
         scratch_shapes=scratch,
         cost_estimate=pl.CostEstimate(
             flops=flops, bytes_accessed=flops // 100, transcendentals=0
         ),
-        compiler_params=pltpu.CompilerParams(vmem_limit_bytes=mib << 20) if mib else None,
+        compiler_params=pltpu.CompilerParams(vmem_limit_bytes=mib << 20),
     )
 
 
@@ -206,12 +218,15 @@
     pair = (pick(halves, core, 0) + pair).astype(bf16)
     pair, my_momentum = lax.optimization_barrier((pair, my_momentum))
     first = exchange(pair.reshape(replicas // 2, own, kv), chips)
-    second = in_vmem(
+    lanes = 4 * rank
+    (second,) = in_vmem(
         functools.partial(moments, own=own, rank=rank, replicas=replicas),
-        shape((replicas, own, 4 * rank), f32),
+        (shape((replicas, own, lanes), f32),),
         2,
-        0,
+        6,
         40000000,
+        (pltpu.VMEM((replicas, own, lanes), f32),),
+        1,
     )(first, q_start.T)
     second = exchange(second, peers)
 
@@ -226,39 +241,45 @@
     full_momentum = full_momentum.T
 
     part = (shards // 2, block, kv // 2)
-    send_a, keep_a, send_b, keep_b = in_vmem(
+    left, right, keep = in_vmem(
         key_products,
-        (shape(part, bf16), shape(part, f32), shape(part, bf16), shape(part, f32)),
+        (shape(part, bf16), shape(part, bf16), shape((*part[:2], kv), f32)),
         3,
-        0,
+        12,
         2 * tokens.shape[1] * rows * kv,
+        (pltpu.VMEM((*part[:2], kv), bf16), pltpu.SemaphoreType.DMA((2,))),
+        2,
     )(own_tokens, outer_base, full_momentum)
-    key_a = swap(send_a, "xl")
-    key_b = swap(send_b, "y0")
-    key_a = keep_a + key_a.astype(f32)
-    key_b = keep_b + key_b.astype(f32)
-    quarter = (shards // 4, 2, block, kv // 2)
-    key_a = halve(key_a.reshape(quarter), "y0", 1)
-    key_b = halve(key_b.reshape(quarter), "xl", 1)
-    key_part = jnp.concatenate([key_a, key_b], axis=-1).reshape(2, 2, block, kv)
+    across = ("y2", "y1", "y0")
+    left = lax.ppermute(left, across, [(i, i ^ 1) for i in range(8)])
+    right = lax.ppermute(
+        right, across, [(i, (i + 1 if i % 2 else i - 1) % 8) for i in range(8)]
+    )
+    key_part = keep + jnp.concatenate([left, right], axis=-1).astype(f32)
+    key_part = halve(key_part.reshape(4, 2, block, kv), "xl", 1)
+    key_part = key_part.reshape(2, 2, block, kv)
     key_part = halve(key_part, "y1", 1)
     key_sum = halve(key_part, "y2", 0)
 
-    third = in_vmem(
+    tall = (shards, own + block // 4, lanes)
+    (third,) = in_vmem(
         functools.partial(token_products, own=own, rank=rank),
-        shape((shards, own + block // 4, 4 * rank), f32),
+        (shape(tall, f32),),
         2,
-        0,
+        12,
         500000000,
+        (pltpu.VMEM(tall, f32),),
+        1,
     )(second, own_tokens)
     third = exchange(third, shard)
-    lanes = 4 * rank
     copies, total = in_vmem(
         shard_sums,
         (shape((replicas, own, lanes), f32), shape(third.shape[1:], f32)),
         1,
-        0,
+        4,
         1000000,
+        (pltpu.VMEM((replicas, own, lanes), f32),),
+        1,
     )(third)
     fourth = exchange(copies, peers)
     basis, token_basis, inverse = in_vmem(
@@ -269,7 +290,7 @@
             shape((lanes, lanes), f32),
         ),
         2,
-        0,
+        6,
         100000000,
     )(total, second)
     new_base, new_momentum, new_error, key_low = in_vmem(
@@ -281,7 +302,7 @@
             shape((block, kv), f32),
         ),
         9,
-        0,
+        12,
         400000000,
         (pltpu.VMEM((kv, lanes), f32),),
     )(

time: 143 us -> 132 us (0.923)
  Pallas kernels: 22.9 us -> 12.8 us
  starting transfers between devices: 67 us -> 57.9 us
  waiting for transfers between devices: 36.6 us -> 41.3 us
  other arithmetic: 7.66 us -> 10.4 us
  local copies, waits for them, and re-layouts: 6.39 us -> 8.27 us
    ppermute x8 -> x5, starting transfers between devices: 31 us -> 20.7 us  [swap(): return lax.ppermute(x, axis, [(0, 1), (1, 0)])]
    ppermute x0 -> x2, starting transfers between devices: none -> 8.06 us  [the longest x1 4.87 us: on_device(): lax.ppermute(right, across, [(i, (i + 1 if i % 2 else i - 1) % 8) for i i...]
    all_to_all x5, starting transfers between devices: 36 us -> 29.1 us  [exchange(): return lax.all_to_all(x, axis, 0, 0, tiled=True)]
    ppermute x8 -> x5, waiting for transfers between devices: 1.15 us -> 7.65 us  [swap(): return lax.ppermute(x, axis, [(0, 1), (1, 0)])]
    pallas_call x2, Pallas kernels: 8.45 us -> 3.81 us  [the longest x1 2.05 us: on_device(): in_vmem(functools.partial(token_products, own=own, rank=rank), (shape(tal...]
    add x3 -> x2, other arithmetic: 1.14 us -> 3.66 us  [halve(): return pick(x, me, dim) + other.astype(f32)]
    convert_element_type x4 -> x3, local copies, waits for them, and re-layouts: 0.85 us -> 3.26 us  [halve(): other = swap(pick(x, 1 - me, dim).astype(bf16), axis)]
    all_to_all x5, waiting for transfers between devices: 35.5 us -> 33.6 us  [exchange(): return lax.all_to_all(x, axis, 0, 0, tiled=True)]
  transfers between devices with their start and end apart: 13 -> 12, of which waited for: 6 -> 9; matrix products, arithmetic and copies ran while one was open for 4% -> 9% of each run, Pallas kernels for 13% -> 8%
where the time goes in v4:
time: 132 us
  starting transfers between devices  57.9 us (44%)
  waiting for transfers between devices  41.3 us (31%)
  Pallas kernels  12.8 us (10%)
  other arithmetic  10.4 us (8%)
  local copies, waits for them, and re-layouts  8.27 us (6%)
    all_to_all x5, waiting for transfers between devices, exchange(): return lax.all_to_all(x, axis, 0, 0, tiled=True)  33.6 us
    all_to_all x5, starting transfers between devices, exchange(): return lax.all_to_all(x, axis, 0, 0, tiled=True)  29.1 us
    ppermute x5, starting transfers between devices, swap(): return lax.ppermute(x, axis, [(0, 1), (1, 0)])  20.7 us
    ppermute x5, waiting for transfers between devices, swap(): return lax.ppermute(x, axis, [(0, 1), (1, 0)])  7.65 us
    ppermute x1, starting transfers between devices, on_device(): lax.ppermute(right, across, [(i, (i + 1 if i % 2 else i - 1) % 8) for i i...  4.87 us
    add x2, other arithmetic, halve(): return pick(x, me, dim) + other.astype(f32)  3.66 us
    add x1, other arithmetic, on_device(): key_part = keep + jnp.concatenate([left, right], axis=-1).astype(f32)  3.59 us
    convert_element_type x3, local copies, waits for them, and re-layouts, halve(): other = swap(pick(x, 1 - me, dim).astype(bf16), axis)  3.26 us
  transfers between devices with their start and end apart: 12, of which 9 were waited for; matrix products, arithmetic and copies ran while one was open for 9% of the time, Pallas kernels for 8%

profile of v4, /device:TPU:1, one launch (start us, length us, event | category | flops | bytes accessed | tf_op | source)
XLA Modules:
  0.0 131.5 jit_solution(9380575874212194512)
XLA Ops:
  2.3 8.7 %collective-permute-start = (f32[256,512]{1,0:T(8,128)S(1)}, f32[256,512]{1,0:T(8,128)S(1)}, u32[]{:S(2)}, u32[]{:S(2)}) collective-permute-start(f32[256,512]{1,0:T(8,128)S(1)} %dynamic-slice_bitcast_fusion), channel_id=1, source_target_pairs={{0,16},{16,0},{1,17},{17,1},{2,18},{18,2},{3,19},{19,3},{4,20},{20... | collective-permute-start | bytes 1572872 | tf_op jit(solution)/shard_map/ppermute | solution.py:25
  11.8 7.3 %all-to-all-start = ((bf16[16,16,512]{2,1,0:T(8,128)(2,1)}), bf16[16,16,512]{2,1,0:T(8,128)(2,1)S(1)}, u32[]{:S(2)}, u32[]{:S(2)}) async-start(bf16[16,16,512]{2,1,0:T(8,128)(2,1)} %broadcast_in_dim.9), calls=%async_computation | async-start | bytes 524288 | tf_op jit(solution)/shard_map/all_to_all | solution.py:29
  19.8 12.1 %all-to-all-done = bf16[16,16,512]{2,1,0:T(8,128)(2,1)S(1)} async-done(((bf16[16,16,512]{2,1,0:T(8,128)(2,1)}), bf16[16,16,512]{2,1,0:T(8,128)(2,1)S(1)}, u32[]{:S(2)}, u32[]{:S(2)}) %all-to-all-start) | async-done | bytes 262176 | tf_op jit(solution)/shard_map/all_to_all | solution.py:29
  31.9 3.6 %collective-permute-start.1 = (bf16[16,16,512]{2,1,0:T(8,128)(2,1)S(1)}, bf16[16,16,512]{2,1,0:T(8,128)(2,1)S(1)}, u32[]{:S(2)}, u32[]{:S(2)}) collective-permute-start(bf16[16,16,512]{2,1,0:T(8,128)(2,1)S(1)} %all-to-all-done), channel_id=1, source_target_pairs={{0,16},{16,0},{1,17},{17,1},{2,18},{18,2},{3,19},{19,3},{4,20},{20... | collective-permute-start | bytes 786440 | tf_op jit(solution)/shard_map/ppermute | solution.py:25
  41.9 3.2 %collective-permute-start.2 = (bf16[8,128,256]{2,1,0:T(8,128)(2,1)}, bf16[8,128,256]{2,1,0:T(8,128)(2,1)}, u32[]{:S(2)}, u32[]{:S(2)}) collective-permute-start(bf16[8,128,256]{2,1,0:T(8,128)(2,1)} %get-tuple-element.29), channel_id=1, source_target_pairs={{0,2},{2,0},{4,6},{6,4},{8,10},{10,8},{12,14},{14,12},{1,3},{3,1},... | collective-permute-start | bytes 1572872 | tf_op jit(solution)/shard_map/ppermute | solution.py:254
  45.2 4.9 %collective-permute-start.3 = (bf16[8,128,256]{2,1,0:T(8,128)(2,1)}, bf16[8,128,256]{2,1,0:T(8,128)(2,1)}, u32[]{:S(2)}, u32[]{:S(2)}) collective-permute-start(bf16[8,128,256]{2,1,0:T(8,128)(2,1)} %get-tuple-element.30), channel_id=1, source_target_pairs={{0,14},{2,4},{4,2},{6,8},{8,6},{10,12},{12,10},{14,0},{1,15},{3,5}... | collective-permute-start | bytes 1572872 | tf_op jit(solution)/shard_map/ppermute | solution.py:255
  50.0 3.5 %all-to-all-start.1 = ((bf16[16,16,512]{2,1,0:T(8,128)(2,1)}), bf16[16,16,512]{2,1,0:T(8,128)(2,1)S(1)}, u32[]{:S(2)}, u32[]{:S(2)}) async-start(bf16[16,16,512]{2,1,0:T(8,128)(2,1)} %bitcast.65), calls=%async_computation.1 | async-start | bytes 524288 | tf_op jit(solution)/shard_map/all_to_all | solution.py:29
  53.6 12.0 %all-to-all-done.1.first_ref = bf16[16,16,512]{2,1,0:T(8,128)(2,1)S(1)} async-done(((bf16[16,16,512]{2,1,0:T(8,128)(2,1)}), bf16[16,16,512]{2,1,0:T(8,128)(2,1)S(1)}, u32[]{:S(2)}, u32[]{:S(2)}) %all-to-all-start.1) | async-done | bytes 262176 | tf_op jit(solution)/shard_map/all_to_all | solution.py:29
  65.6 1.9 %shard_map.93 = f32[32,16,128]{2,1,0:T(8,128)} custom-call(bf16[16,16,512]{2,1,0:T(8,128)(2,1)S(1)} %all-to-all-done.1.first_ref, f32[32,512]{1,0:T(8,128)S(1)} %bitcast.61), custom_call_target="tpu_custom_call" | custom-call | flops 40000000 | bytes 400000 | tf_op jit(solution)/shard_map/pallas_call | solution.py:222
  67.5 6.5 %all-to-all-start.2 = ((f32[32,16,128]{2,1,0:T(8,128)}), f32[32,16,128]{2,1,0:T(8,128)S(1)}, u32[]{:S(2)}, u32[]{:S(2)}) async-start(f32[32,16,128]{2,1,0:T(8,128)} %shard_map.93), calls=%async_computation.2 | async-start | bytes 524288 | tf_op jit(solution)/shard_map/all_to_all | solution.py:29
  74.1 3.6 %convert_add_fusion = f32[8,128,512]{2,1,0:T(8,128)} fusion(f32[8,128,512]{2,1,0:T(8,128)} %copy-done.1, bf16[8,128,256]{2,1,0:T(8,128)(2,1)} %collective-permute-done.3, bf16[8,128,256]{2,1,0:T(8,128)(2,1)} %collective-permute-done.2), kind=kLoop, calls=%fused_computation | loop fusion | flops 2621440 | bytes 5242880 | tf_op jit(solution)/shard_map/add | solution.py:258
  77.7 2.1 %fusion = bf16[4,128,512]{2,1,0:T(8,128)(2,1)} fusion(f32[4,2,128,512]{3,2,1,0:T(8,128)} %bitcast.15, s32[]{:T(128)S(6)} %select_n.46), kind=kLoop, calls=%fused_computation.4 | loop fusion | bytes 1048580 | tf_op jit(solution)/shard_map/convert_element_type | solution.py:42
  79.7 2.2 %collective-permute-start.4 = (bf16[4,128,512]{2,1,0:T(8,128)(2,1)}, bf16[4,128,512]{2,1,0:T(8,128)(2,1)}, u32[]{:S(2)}, u32[]{:S(2)}) collective-permute-start(bf16[4,128,512]{2,1,0:T(8,128)(2,1)} %fusion), channel_id=1, source_target_pairs={{0,1},{1,0},{2,3},{3,2},{4,5},{5,4},{6,7},{7,6},{8,9},{9,8},{10,11... | collective-permute-start | bytes 1572872 | tf_op jit(solution)/shard_map/ppermute | solution.py:25
  82.0 4.4 %all-to-all-done.2.second_ref = f32[32,16,128]{2,1,0:T(8,128)S(1)} async-done(((f32[32,16,128]{2,1,0:T(8,128)}), f32[32,16,128]{2,1,0:T(8,128)S(1)}, u32[]{:S(2)}, u32[]{:S(2)}) %all-to-all-start.2) | async-done | bytes 262176 | tf_op jit(solution)/shard_map/all_to_all | solution.py:29
  86.3 2.1 %shard_map.94 = f32[16,48,128]{2,1,0:T(8,128)} custom-call(f32[32,16,128]{2,1,0:T(8,128)S(1)} %all-to-all-done.2.second_ref, bf16[2048,512]{1,0:T(8,128)(2,1)S(1)} %bitcast.54), custom_call_target="tpu_custom_call" | custom-call | flops 500000000 | bytes 5000000 | tf_op jit(solution)/shard_map/pallas_call | solution.py:265
  88.4 3.6 %all-to-all-start.3 = ((f32[16,48,128]{2,1,0:T(8,128)}), f32[16,48,128]{2,1,0:T(8,128)S(1)}, u32[]{:S(2)}, u32[]{:S(2)}) async-start(f32[16,48,128]{2,1,0:T(8,128)} %shard_map.94), calls=%async_computation.3 | async-start | bytes 786432 | tf_op jit(solution)/shard_map/all_to_all | solution.py:29
  91.9 3.2 %collective-permute-done.4 = bf16[4,128,512]{2,1,0:T(8,128)(2,1)} collective-permute-done((bf16[4,128,512]{2,1,0:T(8,128)(2,1)}, bf16[4,128,512]{2,1,0:T(8,128)(2,1)}, u32[]{:S(2)}, u32[]{:S(2)}) %collective-permute-start.4) | collective-permute-done | bytes 524320 | tf_op jit(solution)/shard_map/ppermute | solution.py:25
  95.2 2.5 %bitcast_add_fusion = f32[4,128,512]{2,1,0:T(8,128)} fusion(bf16[4,128,512]{2,1,0:T(8,128)(2,1)} %collective-permute-done.4, f32[4,2,128,512]{3,2,1,0:T(8,128)} %bitcast.15, s32[]{:T(128)S(6)} %select_n.45), kind=kLoop, calls=%fused_computation.2 | loop fusion | flops 524288 | bytes 2621444 | tf_op jit(solution)/shard_map/add | solution.py:43
  98.9 1.9 %collective-permute-start.5 = (bf16[2,128,512]{2,1,0:T(8,128)(2,1)S(1)}, bf16[2,128,512]{2,1,0:T(8,128)(2,1)S(1)}, u32[]{:S(2)}, u32[]{:S(2)}) collective-permute-start(bf16[2,128,512]{2,1,0:T(8,128)(2,1)S(1)} %fusion.2), channel_id=1, source_target_pairs={{0,4},{4,0},{1,5},{5,1},{2,6},{6,2},{3,7},{7,3},{8,12},{12,8},{9,1... | collective-permute-start | bytes 786440 | tf_op jit(solution)/shard_map/ppermute | solution.py:25
  100.8 4.0 %all-to-all-done.3.third_ref = f32[16,48,128]{2,1,0:T(8,128)S(1)} async-done(((f32[16,48,128]{2,1,0:T(8,128)}), f32[16,48,128]{2,1,0:T(8,128)S(1)}, u32[]{:S(2)}, u32[]{:S(2)}) %all-to-all-start.3) | async-done | bytes 393248 | tf_op jit(solution)/shard_map/all_to_all | solution.py:29
  105.6 8.2 %all-to-all-start.4 = ((f32[32,16,128]{2,1,0:T(8,128)}), f32[32,16,128]{2,1,0:T(8,128)S(1)}, u32[]{:S(2)}, u32[]{:S(2)}) async-start(f32[32,16,128]{2,1,0:T(8,128)} %get-tuple-element.19), calls=%async_computation.4 | async-start | bytes 524288 | tf_op jit(solution)/shard_map/all_to_all | solution.py:29
  117.5 4.2 %collective-permute-start.6 = (bf16[128,512]{1,0:T(8,128)(2,1)S(1)}, bf16[128,512]{1,0:T(8,128)(2,1)S(1)}, u32[]{:S(2)}, u32[]{:S(2)}) collective-permute-start(bf16[128,512]{1,0:T(8,128)(2,1)S(1)} %fusion.5), channel_id=1, source_target_pairs={{0,8},{8,0},{1,9},{9,1},{2,10},{10,2},{3,11},{11,3},{4,12},{12,4},... | collective-permute-start | bytes 393224 | tf_op jit(solution)/shard_map/ppermute | solution.py:25
  121.7 3.2 %shard_map.96 = (f32[512,128]{1,0:T(8,128)S(1)}, f32[128,128]{1,0:T(8,128)S(1)}, f32[128,128]{1,0:T(8,128)S(1)}) custom-call(f32[48,128]{1,0:T(8,128)S(1)} %get-tuple-element.20.total_ref, f32[32,16,128]{2,1,0:T(8,128)S(1)} %all-to-all-done.2.second_ref), custom_call_target="tpu_custom_call" | custom-call | flops 100000000 | bytes 1000000 | tf_op jit(solution)/shard_map/pallas_call | solution.py:285
  126.1 3.1 %shard_map.97 = (bf16[512,512]{1,0:T(8,128)(2,1)}, bf16[16,512]{1,0:T(8,128)(2,1)}, bf16[512,512]{1,0:T(8,128)(2,1)}, f32[128,512]{1,0:T(8,128)S(1)}) custom-call(f32[32,16,128]{2,1,0:T(8,128)S(1)} %all-to-all-done.4.fourth_ref, f32[128,128]{1,0:T(8,128)S(1)} %get-tuple-element.21.inverse_ref, f32[512,128]{1,0:T(8,128)S(1)} %get-tuple-element.22.basis_ref, ...), custom_call_target="tpu_custom_call" | custom-call | flops 400000000 | bytes 4000000 | tf_op jit(solution)/shard_map/pallas_call | solution.py:296
  (39 shorter events, 18.5 us)
Async XLA Ops:
  0.6 10.4 %copy-start.5 = (bf16[512,16]{0,1:T(8,128)(2,1)S(1)}, bf16[512,16]{0,1:T(8,128)(2,1)}, u32[]{:S(2)}) copy-start(bf16[512,16]{0,1:T(8,128)(2,1)} %param.8) | copy-start | bytes 49156
  2.3 16.8 %collective-permute-start = (f32[256,512]{1,0:T(8,128)S(1)}, f32[256,512]{1,0:T(8,128)S(1)}, u32[]{:S(2)}, u32[]{:S(2)}) collective-permute-start(f32[256,512]{1,0:T(8,128)S(1)} %dynamic-slice_bitcast_fusion), channel_id=1, source_target_pairs={{0,16},{16,0},{1,17},{17,1},{2,18},{18,2},{3,19},{19,3},{4,20},{20... | collective-permute-start | bytes 1572872 | tf_op jit(solution)/shard_map/ppermute | solution.py:25
  11.8 20.1 %all-to-all-start = ((bf16[16,16,512]{2,1,0:T(8,128)(2,1)}), bf16[16,16,512]{2,1,0:T(8,128)(2,1)S(1)}, u32[]{:S(2)}, u32[]{:S(2)}) async-start(bf16[16,16,512]{2,1,0:T(8,128)(2,1)} %broadcast_in_dim.9), calls=%async_computation | async-start | bytes 524288 | tf_op jit(solution)/shard_map/all_to_all | solution.py:29
  31.9 4.8 %collective-permute-start.1 = (bf16[16,16,512]{2,1,0:T(8,128)(2,1)S(1)}, bf16[16,16,512]{2,1,0:T(8,128)(2,1)S(1)}, u32[]{:S(2)}, u32[]{:S(2)}) collective-permute-start(bf16[16,16,512]{2,1,0:T(8,128)(2,1)S(1)} %all-to-all-done), channel_id=1, source_target_pairs={{0,16},{16,0},{1,17},{17,1},{2,18},{18,2},{3,19},{19,3},{4,20},{20... | collective-permute-start | bytes 786440 | tf_op jit(solution)/shard_map/ppermute | solution.py:25
  35.5 3.3 %copy-start = (bf16[1,2048,512]{2,1,0:T(8,128)(2,1)S(1)}, bf16[1,2048,512]{2,1,0:T(8,128)(2,1)}, u32[]{:S(2)}) copy-start(bf16[1,2048,512]{2,1,0:T(8,128)(2,1)} %param.11) | copy-start | bytes 6291460
  35.5 3.3 %copy-start.2 = (bf16[512,512]{1,0:T(8,128)(2,1)S(1)}, bf16[512,512]{1,0:T(8,128)(2,1)}, u32[]{:S(2)}) copy-start(bf16[512,512]{1,0:T(8,128)(2,1)} %base_ref.3) | copy-start | bytes 1572868
  38.9 26.7 %copy-start.6 = (f32[512,32]{0,1:T(8,128)S(1)}, f32[512,32]{0,1:T(8,128)}, u32[]{:S(2)}) copy-start(f32[512,32]{0,1:T(8,128)} %param.10) | copy-start | bytes 196612
  40.6 1.3 copy-start.1
  41.9 32.1 %collective-permute-start.2 = (bf16[8,128,256]{2,1,0:T(8,128)(2,1)}, bf16[8,128,256]{2,1,0:T(8,128)(2,1)}, u32[]{:S(2)}, u32[]{:S(2)}) collective-permute-start(bf16[8,128,256]{2,1,0:T(8,128)(2,1)} %get-tuple-element.29), channel_id=1, source_target_pairs={{0,2},{2,0},{4,6},{6,4},{8,10},{10,8},{12,14},{14,12},{1,3},{3,1},... | collective-permute-start | bytes 1572872 | tf_op jit(solution)/shard_map/ppermute | solution.py:254
  45.2 28.9 %collective-permute-start.3 = (bf16[8,128,256]{2,1,0:T(8,128)(2,1)}, bf16[8,128,256]{2,1,0:T(8,128)(2,1)}, u32[]{:S(2)}, u32[]{:S(2)}) collective-permute-start(bf16[8,128,256]{2,1,0:T(8,128)(2,1)} %get-tuple-element.30), channel_id=1, source_target_pairs={{0,14},{2,4},{4,2},{6,8},{8,6},{10,12},{12,10},{14,0},{1,15},{3,5}... | collective-permute-start | bytes 1572872 | tf_op jit(solution)/shard_map/ppermute | solution.py:255
  50.0 15.5 %all-to-all-start.1 = ((bf16[16,16,512]{2,1,0:T(8,128)(2,1)}), bf16[16,16,512]{2,1,0:T(8,128)(2,1)S(1)}, u32[]{:S(2)}, u32[]{:S(2)}) async-start(bf16[16,16,512]{2,1,0:T(8,128)(2,1)} %bitcast.65), calls=%async_computation.1 | async-start | bytes 524288 | tf_op jit(solution)/shard_map/all_to_all | solution.py:29
  67.5 18.8 %all-to-all-start.2 = ((f32[32,16,128]{2,1,0:T(8,128)}), f32[32,16,128]{2,1,0:T(8,128)S(1)}, u32[]{:S(2)}, u32[]{:S(2)}) async-start(f32[32,16,128]{2,1,0:T(8,128)} %shard_map.93), calls=%async_computation.2 | async-start | bytes 524288 | tf_op jit(solution)/shard_map/all_to_all | solution.py:29
  79.7 15.4 %collective-permute-start.4 = (bf16[4,128,512]{2,1,0:T(8,128)(2,1)}, bf16[4,128,512]{2,1,0:T(8,128)(2,1)}, u32[]{:S(2)}, u32[]{:S(2)}) collective-permute-start(bf16[4,128,512]{2,1,0:T(8,128)(2,1)} %fusion), channel_id=1, source_target_pairs={{0,1},{1,0},{2,3},{3,2},{4,5},{5,4},{6,7},{7,6},{8,9},{9,8},{10,11... | collective-permute-start | bytes 1572872 | tf_op jit(solution)/shard_map/ppermute | solution.py:25
  88.4 16.5 %all-to-all-start.3 = ((f32[16,48,128]{2,1,0:T(8,128)}), f32[16,48,128]{2,1,0:T(8,128)S(1)}, u32[]{:S(2)}, u32[]{:S(2)}) async-start(f32[16,48,128]{2,1,0:T(8,128)} %shard_map.94), calls=%async_computation.3 | async-start | bytes 786432 | tf_op jit(solution)/shard_map/all_to_all | solution.py:29
  97.7 28.4 %copy-start.3 = (bf16[1,512,512]{2,1,0:T(8,128)(2,1)S(1)}, bf16[1,512,512]{2,1,0:T(8,128)(2,1)}, u32[]{:S(2)}) copy-start(bf16[1,512,512]{2,1,0:T(8,128)(2,1)} %param.9) | copy-start | bytes 1572868
  97.7 28.4 %copy-start.4 = (bf16[1,512,512]{2,1,0:T(8,128)(2,1)S(1)}, bf16[1,512,512]{2,1,0:T(8,128)(2,1)}, u32[]{:S(2)}) copy-start(bf16[1,512,512]{2,1,0:T(8,128)(2,1)} %param.6) | copy-start | bytes 1572868
  98.9 16.6 %collective-permute-start.5 = (bf16[2,128,512]{2,1,0:T(8,128)(2,1)S(1)}, bf16[2,128,512]{2,1,0:T(8,128)(2,1)S(1)}, u32[]{:S(2)}, u32[]{:S(2)}) collective-permute-start(bf16[2,128,512]{2,1,0:T(8,128)(2,1)S(1)} %fusion.2), channel_id=1, source_target_pairs={{0,4},{4,0},{1,5},{5,1},{2,6},{6,2},{3,7},{7,3},{8,12},{12,8},{9,1... | collective-permute-start | bytes 786440 | tf_op jit(solution)/shard_map/ppermute | solution.py:25
  105.6 20.5 %all-to-all-start.4 = ((f32[32,16,128]{2,1,0:T(8,128)}), f32[32,16,128]{2,1,0:T(8,128)S(1)}, u32[]{:S(2)}, u32[]{:S(2)}) async-start(f32[32,16,128]{2,1,0:T(8,128)} %get-tuple-element.19), calls=%async_computation.4 | async-start | bytes 524288 | tf_op jit(solution)/shard_map/all_to_all | solution.py:29
  116.6 0.8 copy-start.7
  117.5 13.3 %collective-permute-start.6 = (bf16[128,512]{1,0:T(8,128)(2,1)S(1)}, bf16[128,512]{1,0:T(8,128)(2,1)S(1)}, u32[]{:S(2)}, u32[]{:S(2)}) collective-permute-start(bf16[128,512]{1,0:T(8,128)(2,1)S(1)} %fusion.5), channel_id=1, source_target_pairs={{0,8},{8,0},{1,9},{9,1},{2,10},{10,2},{3,11},{11,3},{4,12},{12,4},... | collective-permute-start | bytes 393224 | tf_op jit(solution)/shard_map/ppermute | solution.py:25
  126.1 4.7 %copy-start.8 = (f32[2,128,512]{2,1,0:T(8,128)S(1)}, f32[2,128,512]{2,1,0:T(8,128)}, u32[]{:S(2)}) copy-start(f32[2,128,512]{2,1,0:T(8,128)} %copy-done.7) | copy-start | bytes 1572868

commit v5 on v4

--- a/solution.py
+++ b/solution.py
@@ -29,20 +29,6 @@
     return lax.all_to_all(x, axis, 0, 0, tiled=True)
 
 
-def copy_for_each(x, axis):
-    return exchange(jnp.broadcast_to(x, (lax.axis_size(axis), *x.shape)), axis)
-
-
-def pick(x, at, dim):
-    return lax.dynamic_index_in_dim(x, at, dim, keepdims=False)
-
-
-def halve(x, axis, dim):
-    me = lax.axis_index(axis)
-    other = swap(pick(x, 1 - me, dim).astype(bf16), axis)
-    return pick(x, me, dim) + other.astype(f32)
-
-
 def dot(a, b, dims, precision=None):
     return lax.dot_general(
         a, b, (dims, ((), ())), precision=precision, preferred_element_type=f32
@@ -54,7 +40,7 @@
 
 
 def moments(first_ref, q_ref, hbm_ref, out_ref, *, own, rank, replicas):
-    mean = jnp.sum(first_ref[...].astype(f32), axis=0) * (1.0 / replicas)
+    mean = jnp.sum(first_ref[:, :own].astype(f32), axis=0) * (1.0 / replicas)
     q = jnp.concatenate([q_ref[...]] * 4, axis=0)
     p = dot(mean, q, ((1,), (1,)), highest)
     group = lane_group(p.shape, rank)
@@ -89,13 +75,44 @@
     pltpu.sync_copy(out_ref, hbm_ref)
 
 
+def pseudo_halves(
+    local_hbm, base_hbm, error_hbm, send_ref, keep_ref, local_ref, base_ref, error_ref, sems
+):
+    core = lax.axis_index("core")
+    half = keep_ref.shape[0]
+    pairs = ((local_hbm, local_ref), (base_hbm, base_ref), (error_hbm, error_ref))
+    for i, (src, dst) in enumerate(pairs):
+        pltpu.make_async_copy(src, dst, sems.at[i]).start()
+    for i, (src, dst) in enumerate(pairs):
+        pltpu.make_async_copy(src, dst, sems.at[i]).wait()
+
+    def pseudo(which):
+        at = pl.ds(pl.multiple_of(which * half, half), half)
+        base, local = base_ref[at].astype(f32), local_ref[at].astype(f32)
+        return base - local + error_ref[at].astype(f32)
+
+    send_ref[...] = pseudo(1 - core)
+    keep_ref[...] = pseudo(core)
+
+
 def key_products(
-    tokens_ref, base_ref, momentum_ref, left_ref, right_ref, keep_ref, sent, sems
+    tokens_ref, base_ref, first_ref, its_ref,
+    left_ref, right_ref, kept_ref, full_ref, sent, keep, sems,
 ):
-    y0 = lax.axis_index("y0")
-    settled = base_ref[...].astype(f32) - own_mom * momentum_ref[...].astype(f32)
-    settled = settled.astype(bf16)
-    groups, block, cols = keep_ref.shape[0] // 2, keep_ref.shape[1], keep_ref.shape[2]
+    y0, core = lax.axis_index("y0"), lax.axis_index("core")
+    mine = first_ref[:, its_ref.shape[1] :].astype(f32)
+    other = its_ref[...].astype(f32)
+    pairs = jnp.concatenate(
+        [
+            jnp.where(core == 0, mine, other)[:, None],
+            jnp.where(core == 0, other, mine)[:, None],
+        ],
+        axis=1,
+    )
+    momentum = pairs.reshape(base_ref.shape[1], base_ref.shape[0]).T
+    full_ref[...] = momentum.astype(bf16)
+    settled = (base_ref[...].astype(f32) - own_mom * momentum).astype(bf16)
+    groups, block, cols = keep.shape[0] // 2, keep.shape[1], keep.shape[2]
     half = cols // 2
 
     def product(i, parity):
@@ -108,13 +125,77 @@
     copies = [
         pltpu.make_async_copy(sent.at[:, :, :half], left_ref, sems.at[0]),
         pltpu.make_async_copy(sent.at[:, :, half:], right_ref, sems.at[1]),
+        pltpu.make_async_copy(keep, kept_ref, sems.at[2]),
     ]
-    for copy in copies:
+    for copy in copies[:2]:
         copy.start()
     for i in range(groups):
-        keep_ref[2 * i : 2 * i + 2] = product(i, y0)
+        keep[2 * i : 2 * i + 2] = product(i, y0)
+    copies[2].start()
     for copy in copies:
         copy.wait()
+
+
+def fold(*refs, axis, n):
+    came_ref, kept_ref, send_ref, keep_ref = refs[:n], refs[n], refs[n + 1], refs[n + 2]
+    came, held, sent, sems = refs[n + 3 : 2 * n + 3], *refs[2 * n + 3 :]
+    me = lax.axis_index(axis)
+    halves = (1 - me, me)
+    loads = [
+        [
+            pltpu.make_async_copy(
+                src.at[:, half], dst.at[:, i], sems.at[i * (n + 1) + j]
+            )
+            for j, (src, dst) in enumerate(zip((*came_ref, kept_ref), (*came, held)))
+        ]
+        for i, half in enumerate(halves)
+    ]
+    for load in loads[0] + loads[1]:
+        load.start()
+    out = [
+        pltpu.make_async_copy(sent, send_ref, sems.at[2 * n + 2]),
+        pltpu.make_async_copy(held.at[:, 1], keep_ref, sems.at[2 * n + 3]),
+    ]
+    for i in range(2):
+        for load in loads[i]:
+            load.wait()
+        at, width = 0, held.shape[-1] // n
+        for part in came:
+            here = slice(at, at + width)
+            total = held[:, i, :, here] + part[:, i].astype(f32)
+            if i == 0:
+                sent[:, :, here] = total.astype(bf16)
+            else:
+                held[:, i, :, here] = total
+            at += width
+        out[i].start()
+    for copy in out:
+        copy.wait()
+
+
+def fold_call(came, kept, axis):
+    groups, _, block, cols = kept.shape
+    n = len(came)
+    hbm = pl.BlockSpec(memory_space=pltpu.HBM)
+    shape = jax.ShapeDtypeStruct
+    return pl.pallas_call(
+        functools.partial(fold, axis=axis, n=n),
+        out_shape=(
+            shape((groups, block, cols), bf16),
+            shape((groups, block, cols), f32),
+        ),
+        in_specs=[hbm] * (n + 1),
+        out_specs=(hbm, hbm),
+        scratch_shapes=(
+            *[pltpu.VMEM(c.shape, bf16) for c in came],
+            pltpu.VMEM(kept.shape, f32),
+            pltpu.VMEM((groups, block, cols), bf16),
+            pltpu.SemaphoreType.DMA((2 * n + 4,)),
+        ),
+        cost_estimate=pl.CostEstimate(
+            flops=kept.size, bytes_accessed=kept.size * 6, transcendentals=0
+        ),
+    )(*came, kept)
 
 
 def shard_sums(third_ref, hbm_ref, total_ref, copies_ref):
@@ -182,13 +263,13 @@
         base_out[here] = (base - outer_rate * (outer_mu * moment + update)).astype(bf16)
 
 
-def in_vmem(kernel, out_shape, n, mib, flops, scratch=(), far=0):
+def in_vmem(kernel, out_shape, n, mib, flops, scratch=(), far=0, far_in=False):
     whole = pl.BlockSpec(memory_space=pltpu.VMEM)
     hbm = pl.BlockSpec(memory_space=pltpu.HBM)
     return pl.pallas_call(
         kernel,
         out_shape=out_shape,
-        in_specs=[whole] * n,
+        in_specs=[hbm if far_in else whole] * n,
         out_specs=tuple(hbm if i < far else whole for i in range(len(out_shape))),
         scratch_shapes=scratch,
         cost_estimate=pl.CostEstimate(
@@ -204,20 +285,33 @@
     rank = q_start.shape[1]
     own = rows // replicas
     cols = kv // replicas
-    core = lax.axis_index("core")
-    base = outer_base.astype(f32)
     own_tokens = tokens[0]
     block = own_tokens.shape[0] // shards
     shape = jax.ShapeDtypeStruct
 
-    my_momentum = copy_for_each(momentum.T, chips)
-
-    pseudo = base - local_weights[0].astype(f32) + error_feedback[0].astype(f32)
-    halves = pseudo.reshape(2, rows // 2, kv)
-    pair = swap(pick(halves, 1 - core, 0), "core")
-    pair = (pick(halves, core, 0) + pair).astype(bf16)
-    pair, my_momentum = lax.optimization_barrier((pair, my_momentum))
-    first = exchange(pair.reshape(replicas // 2, own, kv), chips)
+    half = shape((rows // 2, kv), f32)
+    given = pltpu.VMEM((rows, kv), bf16)
+    send, pair = in_vmem(
+        pseudo_halves,
+        (half, half),
+        3,
+        8,
+        1000000,
+        (given, given, given, pltpu.SemaphoreType.DMA((3,))),
+        far_in=True,
+    )(local_weights[0], outer_base, error_feedback[0])
+    send = swap(send, "core")
+    pair = (pair + send).astype(bf16)
+    first = exchange(
+        jnp.concatenate(
+            [
+                pair.reshape(replicas // 2, own, kv),
+                jnp.broadcast_to(momentum.T, (replicas // 2, cols, rows)),
+            ],
+            axis=1,
+        ),
+        chips,
+    )
     lanes = 4 * rank
     (second,) = in_vmem(
         functools.partial(moments, own=own, rank=rank, replicas=replicas),
@@ -230,36 +324,38 @@
     )(first, q_start.T)
     second = exchange(second, peers)
 
-    its_momentum = swap(my_momentum, "core")
-    full_momentum = jnp.stack(
-        [
-            jnp.where(core == 0, my_momentum, its_momentum),
-            jnp.where(core == 0, its_momentum, my_momentum),
-        ],
-        axis=1,
-    ).reshape(kv, rows)
-    full_momentum = full_momentum.T
+    its_momentum = swap(first[:, own:], "core")
 
     part = (shards // 2, block, kv // 2)
-    left, right, keep = in_vmem(
+    whole = (*part[:2], kv)
+    left, right, kept, full_momentum = in_vmem(
         key_products,
-        (shape(part, bf16), shape(part, bf16), shape((*part[:2], kv), f32)),
+        (shape(part, bf16), shape(part, bf16), shape(whole, f32), shape((rows, kv), bf16)),
+        4,
+        16,
+        2 * tokens.shape[1] * rows * kv,
+        (
+            pltpu.VMEM(whole, bf16),
+            pltpu.VMEM(whole, f32),
+            pltpu.SemaphoreType.DMA((3,)),
+        ),
         3,
-        12,
-        2 * tokens.shape[1] * rows * kv,
-        (pltpu.VMEM((*part[:2], kv), bf16), pltpu.SemaphoreType.DMA((2,))),
-        2,
-    )(own_tokens, outer_base, full_momentum)
+    )(own_tokens, outer_base, first, its_momentum)
     across = ("y2", "y1", "y0")
     left = lax.ppermute(left, across, [(i, i ^ 1) for i in range(8)])
     right = lax.ppermute(
         right, across, [(i, (i + 1 if i % 2 else i - 1) % 8) for i in range(8)]
     )
-    key_part = keep + jnp.concatenate([left, right], axis=-1).astype(f32)
-    key_part = halve(key_part.reshape(4, 2, block, kv), "xl", 1)
-    key_part = key_part.reshape(2, 2, block, kv)
-    key_part = halve(key_part, "y1", 1)
-    key_sum = halve(key_part, "y2", 0)
+    for axis, groups, came in (
+        ("xl", 4, (left, right)), ("y1", 2, None), ("y2", 1, None)
+    ):
+        view = (groups, 2, block)
+        send, kept = fold_call(
+            [c.reshape(*view, -1) for c in came or (send,)],
+            kept.reshape(*view, kv),
+            axis,
+        )
+        send = swap(send, axis)
 
     tall = (shards, own + block // 4, lanes)
     (third,) = in_vmem(
@@ -316,7 +412,7 @@
         full_momentum,
         momentum.T,
     )
-    key_rows = (key_sum - key_low).astype(bf16)
+    key_rows = (kept[0] + send[0].astype(f32) - key_low).astype(bf16)
     return new_base, new_momentum.T, new_error[None], key_rows[None]
 
 

time: 132 us -> 135 us (1.023)
  blocking collectives: 0 us -> 24.7 us
  waiting for transfers between devices: 41.3 us -> 26.7 us
  other arithmetic: 10.4 us -> 0.84 us
  Pallas kernels: 12.8 us -> 20.5 us
  starting transfers between devices: 57.9 us -> 53.9 us
  local copies, waits for them, and re-layouts: 8.27 us -> 6.82 us
    all_to_all x5 -> x3, waiting for transfers between devices: 33.6 us -> 0.01 us  [exchange(): return lax.all_to_all(x, axis, 0, 0, tiled=True)]
    all_to_all x0 -> x1, blocking collectives: none -> 24.7 us  [exchange(): return lax.all_to_all(x, axis, 0, 0, tiled=True)]
    ppermute x5, waiting for transfers between devices: 7.65 us -> 17 us  [swap(): return lax.ppermute(x, axis, [(0, 1), (1, 0)])]
    add x4 -> x0, other arithmetic: 8.8 us -> none  [the longest x2 3.66 us: halve(): return pick(x, me, dim) + other.astype(f32)]
    ppermute x1, waiting for transfers between devices: 0.01 us -> 8.03 us  [on_device(): lax.ppermute(right, across, [(i, (i + 1 if i % 2 else i - 1) % 8) for i i...]
    pallas_call x1 -> x5, Pallas kernels: 1.76 us -> 9.44 us  [the longest x3 7.19 us: fold_call(): pl.pallas_call(functools.partial(fold, axis=axis, n=n), out_shape=(shape(...]
    all_to_all x5 -> x3, starting transfers between devices: 29.1 us -> 23.1 us  [exchange(): return lax.all_to_all(x, axis, 0, 0, tiled=True)]
    unnamed x18 -> x32, local copies, waits for them, and re-layouts: 2.14 us -> 6.78 us
  transfers between devices with their start and end apart: 12 -> 10, of which waited for: 9 -> 6; matrix products, arithmetic and copies ran while one was open for 9% -> 0% of each run, Pallas kernels for 8% -> 14%
where the time goes in v5:
time: 135 us; the launch traced here: 134 us
  starting transfers between devices  53.9 us (40%)
  waiting for transfers between devices  26.7 us (20%)
  blocking collectives  24.7 us (18%)
  Pallas kernels  20.5 us (15%)
  local copies, waits for them, and re-layouts  6.82 us (5%)
    all_to_all x1, blocking collectives, exchange(): return lax.all_to_all(x, axis, 0, 0, tiled=True)  24.7 us
    all_to_all x3, starting transfers between devices, exchange(): return lax.all_to_all(x, axis, 0, 0, tiled=True)  23.1 us
    ppermute x5, starting transfers between devices, swap(): return lax.ppermute(x, axis, [(0, 1), (1, 0)])  22.7 us
    ppermute x5, waiting for transfers between devices, swap(): return lax.ppermute(x, axis, [(0, 1), (1, 0)])  17 us
    ppermute x1, waiting for transfers between devices, on_device(): lax.ppermute(right, across, [(i, (i + 1 if i % 2 else i - 1) % 8) for i i...  8.03 us
    pallas_call x3, Pallas kernels, fold_call(): pl.pallas_call(functools.partial(fold, axis=axis, n=n), out_shape=(shape(...  7.19 us
    unnamed x32, local copies, waits for them, and re-layouts  6.78 us
    ppermute x1, starting transfers between devices, on_device(): lax.ppermute(right, across, [(i, (i + 1 if i % 2 else i - 1) % 8) for i i...  4.87 us
  transfers between devices with their start and end apart: 10, of which 6 were waited for; matrix products, arithmetic and copies ran while one was open for 0% of the time, Pallas kernels for 14%

profile of v5, /device:TPU:1, one launch (start us, length us, event | category | flops | bytes accessed | tf_op | source)
XLA Modules:
  0.0 134.4 jit_solution(8994061716566858767)
XLA Ops:
  4.1 8.9 %collective-permute-start = (f32[256,512]{1,0:T(8,128)S(1)}, f32[256,512]{1,0:T(8,128)S(1)}, u32[]{:S(2)}, u32[]{:S(2)}) collective-permute-start(f32[256,512]{1,0:T(8,128)S(1)} %get-tuple-element.26), channel_id=1, source_target_pairs={{0,16},{16,0},{1,17},{17,1},{2,18},{18,2},{3,19},{19,3},{4,20},{20... | collective-permute-start | bytes 1572872 | tf_op jit(solution)/shard_map/ppermute | solution.py:25
  13.0 1.5 %collective-permute-done = f32[256,512]{1,0:T(8,128)S(1)} collective-permute-done((f32[256,512]{1,0:T(8,128)S(1)}, f32[256,512]{1,0:T(8,128)S(1)}, u32[]{:S(2)}, u32[]{:S(2)}) %collective-permute-start) | collective-permute-done | bytes 524320 | tf_op jit(solution)/shard_map/ppermute | solution.py:25
  14.7 24.7 %all_to_all.20.first_ref = bf16[16,32,512]{2,1,0:T(8,128)(2,1)S(1)} all-to-all(bf16[16,32,512]{2,1,0:T(8,128)(2,1)S(1)} %pad_maximum_fusion), channel_id=1, replica_groups=mesh['z'=8,'xh'=2,'core'=2,'y2'=2,'y1'=2,'y0'=2,'xl'=2] {'z','xh'}, dimensions={0} | all-to-all | bytes 1048576 | tf_op jit(solution)/shard_map/all_to_all | solution.py:29
  39.4 1.9 %shard_map.94 = f32[32,16,128]{2,1,0:T(8,128)} custom-call(bf16[16,32,512]{2,1,0:T(8,128)(2,1)S(1)} %all_to_all.20.first_ref, f32[32,512]{1,0:T(8,128)S(1)} %bitcast.32), custom_call_target="tpu_custom_call" | custom-call | flops 40000000 | bytes 400000 | tf_op jit(solution)/shard_map/pallas_call | solution.py:316
  41.3 6.2 %all-to-all-start.1 = ((f32[32,16,128]{2,1,0:T(8,128)}), f32[32,16,128]{2,1,0:T(8,128)S(1)}, u32[]{:S(2)}, u32[]{:S(2)}) async-start(f32[32,16,128]{2,1,0:T(8,128)} %shard_map.94), calls=%async_computation.1 | async-start | bytes 524288 | tf_op jit(solution)/shard_map/all_to_all | solution.py:29
  47.6 2.2 %collective-permute-start.1 = (bf16[16,16,512]{2,1,0:T(8,128)(2,1)S(1)}, bf16[16,16,512]{2,1,0:T(8,128)(2,1)S(1)}, u32[]{:S(2)}, u32[]{:S(2)}) collective-permute-start(bf16[16,16,512]{2,1,0:T(8,128)(2,1)S(1)} %slice.4), channel_id=1, source_target_pairs={{0,16},{16,0},{1,17},{17,1},{2,18},{18,2},{3,19},{19,3},{4,20},{20... | collective-permute-start | bytes 786440 | tf_op jit(solution)/shard_map/ppermute | solution.py:25
  51.0 1.9 %shard_map.98 = (bf16[8,128,256]{2,1,0:T(8,128)(2,1)}, bf16[8,128,256]{2,1,0:T(8,128)(2,1)}, f32[8,128,512]{2,1,0:T(8,128)S(1)}, bf16[512,512]{1,0:T(8,128)(2,1)S(1)}) custom-call(bf16[2048,512]{1,0:T(8,128)(2,1)S(1)} %bitcast.24, bf16[512,512]{1,0:T(8,128)(2,1)S(1)} %copy-done.5, bf16[16,32,512]{2,1,0:T(8,128)(2,1)S(1)} %all_to_all.20.first_ref, ...), custom_call_target="tpu_custom_call" | custom-call | flops 1073741824 | bytes 10737418 | tf_op jit(solution)/shard_map/pallas_call | solution.py:331
  53.0 1.3 copy-done
  55.1 3.2 %collective-permute-start.2 = (bf16[8,128,256]{2,1,0:T(8,128)(2,1)}, bf16[8,128,256]{2,1,0:T(8,128)(2,1)S(1)}, u32[]{:S(2)}, u32[]{:S(2)}) collective-permute-start(bf16[8,128,256]{2,1,0:T(8,128)(2,1)} %get-tuple-element.36), channel_id=1, source_target_pairs={{0,2},{2,0},{4,6},{6,4},{8,10},{10,8},{12,14},{14,12},{1,3},{3,1},... | collective-permute-start | bytes 1572872 | tf_op jit(solution)/shard_map/ppermute | solution.py:345
  58.3 4.9 %collective-permute-start.3 = (bf16[8,128,256]{2,1,0:T(8,128)(2,1)}, bf16[8,128,256]{2,1,0:T(8,128)(2,1)}, u32[]{:S(2)}, u32[]{:S(2)}) collective-permute-start(bf16[8,128,256]{2,1,0:T(8,128)(2,1)} %get-tuple-element.37), channel_id=1, source_target_pairs={{0,14},{2,4},{4,2},{6,8},{8,6},{10,12},{12,10},{14,0},{1,15},{3,5}... | collective-permute-start | bytes 1572872 | tf_op jit(solution)/shard_map/ppermute | solution.py:346
  63.2 2.1 %shard_map.95 = f32[16,48,128]{2,1,0:T(8,128)} custom-call(f32[32,16,128]{2,1,0:T(8,128)S(1)} %all-to-all-done.1.second_ref, bf16[2048,512]{1,0:T(8,128)(2,1)S(1)} %bitcast.25), custom_call_target="tpu_custom_call" | custom-call | flops 500000000 | bytes 5000000 | tf_op jit(solution)/shard_map/pallas_call | solution.py:361
  65.3 3.6 %all-to-all-start.2 = ((f32[16,48,128]{2,1,0:T(8,128)}), f32[16,48,128]{2,1,0:T(8,128)S(1)}, u32[]{:S(2)}, u32[]{:S(2)}) async-start(f32[16,48,128]{2,1,0:T(8,128)} %shard_map.95), calls=%async_computation.2 | async-start | bytes 786432 | tf_op jit(solution)/shard_map/all_to_all | solution.py:29
  68.9 1.7 %collective-permute-done.2 = bf16[8,128,256]{2,1,0:T(8,128)(2,1)S(1)} collective-permute-done((bf16[8,128,256]{2,1,0:T(8,128)(2,1)}, bf16[8,128,256]{2,1,0:T(8,128)(2,1)S(1)}, u32[]{:S(2)}, u32[]{:S(2)}) %collective-permute-start.2) | collective-permute-done | bytes 524320 | tf_op jit(solution)/shard_map/ppermute | solution.py:345
  70.5 8.0 %collective-permute-done.3 = bf16[8,128,256]{2,1,0:T(8,128)(2,1)} collective-permute-done((bf16[8,128,256]{2,1,0:T(8,128)(2,1)}, bf16[8,128,256]{2,1,0:T(8,128)(2,1)}, u32[]{:S(2)}, u32[]{:S(2)}) %collective-permute-start.3) | collective-permute-done | bytes 524320 | tf_op jit(solution)/shard_map/ppermute | solution.py:346
  78.6 3.0 %shard_map.100 = (bf16[4,128,512]{2,1,0:T(8,128)(2,1)}, f32[4,128,512]{2,1,0:T(8,128)}) custom-call(bf16[4,2,128,256]{3,2,1,0:T(8,128)(2,1)} %bitcast.37, bf16[4,2,128,256]{3,2,1,0:T(8,128)(2,1)} %bitcast.9.refs_1_, f32[4,2,128,512]{3,2,1,0:T(8,128)} %bitcast.23), custom_call_target="tpu_custom_call" | custom-call | flops 524288 | bytes 3145728 | tf_op jit(solution)/shard_map/pallas_call | solution.py:181
  81.6 2.3 %collective-permute-start.4 = (bf16[4,128,512]{2,1,0:T(8,128)(2,1)}, bf16[4,128,512]{2,1,0:T(8,128)(2,1)S(1)}, u32[]{:S(2)}, u32[]{:S(2)}) collective-permute-start(bf16[4,128,512]{2,1,0:T(8,128)(2,1)} %get-tuple-element.39), channel_id=1, source_target_pairs={{0,1},{1,0},{2,3},{3,2},{4,5},{5,4},{6,7},{7,6},{8,9},{9,8},{10,11... | collective-permute-start | bytes 1572872 | tf_op jit(solution)/shard_map/ppermute | solution.py:25
  84.7 13.3 %all-to-all-start.3 = ((f32[32,16,128]{2,1,0:T(8,128)}), f32[32,16,128]{2,1,0:T(8,128)S(1)}, u32[]{:S(2)}, u32[]{:S(2)}) async-start(f32[32,16,128]{2,1,0:T(8,128)} %get-tuple-element.27), calls=%async_computation.3 | async-start | bytes 524288 | tf_op jit(solution)/shard_map/all_to_all | solution.py:29
  98.8 2.2 %shard_map.101 = (bf16[2,128,512]{2,1,0:T(8,128)(2,1)}, f32[2,128,512]{2,1,0:T(8,128)}) custom-call(bf16[2,2,128,512]{3,2,1,0:T(8,128)(2,1)} %bitcast.35, f32[2,2,128,512]{3,2,1,0:T(8,128)} %bitcast.33), custom_call_target="tpu_custom_call" | custom-call | flops 262144 | bytes 1572864 | tf_op jit(solution)/shard_map/pallas_call | solution.py:181
  101.0 2.8 %collective-permute-start.5 = (bf16[2,128,512]{2,1,0:T(8,128)(2,1)}, bf16[2,128,512]{2,1,0:T(8,128)(2,1)S(1)}, u32[]{:S(2)}, u32[]{:S(2)}) collective-permute-start(bf16[2,128,512]{2,1,0:T(8,128)(2,1)} %get-tuple-element.41), channel_id=1, source_target_pairs={{0,4},{4,0},{1,5},{5,1},{2,6},{6,2},{3,7},{7,3},{8,12},{12,8},{9,1... | collective-permute-start | bytes 786440 | tf_op jit(solution)/shard_map/ppermute | solution.py:25
  103.8 13.7 %collective-permute-done.5 = bf16[2,128,512]{2,1,0:T(8,128)(2,1)S(1)} collective-permute-done((bf16[2,128,512]{2,1,0:T(8,128)(2,1)}, bf16[2,128,512]{2,1,0:T(8,128)(2,1)S(1)}, u32[]{:S(2)}, u32[]{:S(2)}) %collective-permute-start.5) | collective-permute-done | bytes 262176 | tf_op jit(solution)/shard_map/ppermute | solution.py:25
  118.3 1.9 %shard_map.102 = (bf16[1,128,512]{2,1,0:T(8,128)(2,1)}, f32[1,128,512]{2,1,0:T(8,128)}) custom-call(bf16[1,2,128,512]{3,2,1,0:T(8,128)(2,1)} %bitcast.38, f32[1,2,128,512]{3,2,1,0:T(8,128)} %bitcast.36), custom_call_target="tpu_custom_call" | custom-call | flops 131072 | bytes 786432 | tf_op jit(solution)/shard_map/pallas_call | solution.py:181
  120.2 6.5 %collective-permute-start.6 = (bf16[1,128,512]{2,1,0:T(8,128)(2,1)}, bf16[1,128,512]{2,1,0:T(8,128)(2,1)S(1)}, u32[]{:S(2)}, u32[]{:S(2)}) collective-permute-start(bf16[1,128,512]{2,1,0:T(8,128)(2,1)} %get-tuple-element.44), channel_id=1, source_target_pairs={{0,8},{8,0},{1,9},{9,1},{2,10},{10,2},{3,11},{11,3},{4,12},{12,4},... | collective-permute-start | bytes 393224 | tf_op jit(solution)/shard_map/ppermute | solution.py:25
  126.8 3.2 %shard_map.97 = (f32[512,128]{1,0:T(8,128)S(1)}, f32[128,128]{1,0:T(8,128)S(1)}, f32[128,128]{1,0:T(8,128)S(1)}) custom-call(f32[48,128]{1,0:T(8,128)S(1)} %get-tuple-element.28.total_ref, f32[32,16,128]{2,1,0:T(8,128)S(1)} %all-to-all-done.1.second_ref), custom_call_target="tpu_custom_call" | custom-call | flops 100000000 | bytes 1000000 | tf_op jit(solution)/shard_map/pallas_call | solution.py:381
  130.0 3.1 %shard_map.99 = (bf16[512,512]{1,0:T(8,128)(2,1)}, bf16[16,512]{1,0:T(8,128)(2,1)}, bf16[512,512]{1,0:T(8,128)(2,1)}, f32[128,512]{1,0:T(8,128)S(1)}) custom-call(f32[32,16,128]{2,1,0:T(8,128)S(1)} %all-to-all-done.3.fourth_ref, f32[128,128]{1,0:T(8,128)S(1)} %get-tuple-element.29.inverse_ref, f32[512,128]{1,0:T(8,128)S(1)} %get-tuple-element.30.basis_ref, ...), custom_call_target="tpu_custom_call" | custom-call | flops 400000000 | bytes 4000000 | tf_op jit(solution)/shard_map/pallas_call | solution.py:392
  (44 shorter events, 9.2 us)
Async XLA Ops:
  0.6 1.0 copy-start.2
  1.7 1.0 copy-start.4
  2.7 1.0 copy-start.6
  3.8 10.8 %copy-start.10 = (bf16[512,16]{0,1:T(8,128)(2,1)S(1)}, bf16[512,16]{0,1:T(8,128)(2,1)}, u32[]{:S(2)}) copy-start(bf16[512,16]{0,1:T(8,128)(2,1)} %param.8) | copy-start | bytes 49156
  4.1 35.3 %copy-start.11 = (f32[512,32]{0,1:T(8,128)S(1)}, f32[512,32]{0,1:T(8,128)}, u32[]{:S(2)}) copy-start(f32[512,32]{0,1:T(8,128)} %param.10) | copy-start | bytes 196612
  4.1 10.4 %collective-permute-start = (f32[256,512]{1,0:T(8,128)S(1)}, f32[256,512]{1,0:T(8,128)S(1)}, u32[]{:S(2)}, u32[]{:S(2)}) collective-permute-start(f32[256,512]{1,0:T(8,128)S(1)} %get-tuple-element.26), channel_id=1, source_target_pairs={{0,16},{16,0},{1,17},{17,1},{2,18},{18,2},{3,19},{19,3},{4,20},{20... | collective-permute-start | bytes 1572872 | tf_op jit(solution)/shard_map/ppermute | solution.py:25
  14.6 36.4 %copy-start.1 = (bf16[1,2048,512]{2,1,0:T(8,128)(2,1)S(1)}, bf16[1,2048,512]{2,1,0:T(8,128)(2,1)}, u32[]{:S(2)}) copy-start(bf16[1,2048,512]{2,1,0:T(8,128)(2,1)} %param.11) | copy-start | bytes 6291460
  14.6 36.4 %copy-start.5 = (bf16[512,512]{1,0:T(8,128)(2,1)S(1)}, bf16[512,512]{1,0:T(8,128)(2,1)}, u32[]{:S(2)}) copy-start(bf16[512,512]{1,0:T(8,128)(2,1)} %base_ref.3) | copy-start | bytes 1572868
  41.3 21.9 %all-to-all-start.1 = ((f32[32,16,128]{2,1,0:T(8,128)}), f32[32,16,128]{2,1,0:T(8,128)S(1)}, u32[]{:S(2)}, u32[]{:S(2)}) async-start(f32[32,16,128]{2,1,0:T(8,128)} %shard_map.94), calls=%async_computation.1 | async-start | bytes 524288 | tf_op jit(solution)/shard_map/all_to_all | solution.py:29
  47.6 3.4 %collective-permute-start.1 = (bf16[16,16,512]{2,1,0:T(8,128)(2,1)S(1)}, bf16[16,16,512]{2,1,0:T(8,128)(2,1)S(1)}, u32[]{:S(2)}, u32[]{:S(2)}) collective-permute-start(bf16[16,16,512]{2,1,0:T(8,128)(2,1)S(1)} %slice.4), channel_id=1, source_target_pairs={{0,16},{16,0},{1,17},{17,1},{2,18},{18,2},{3,19},{19,3},{4,20},{20... | collective-permute-start | bytes 786440 | tf_op jit(solution)/shard_map/ppermute | solution.py:25
  53.0 1.3 copy-start
  55.1 15.4 %collective-permute-start.2 = (bf16[8,128,256]{2,1,0:T(8,128)(2,1)}, bf16[8,128,256]{2,1,0:T(8,128)(2,1)S(1)}, u32[]{:S(2)}, u32[]{:S(2)}) collective-permute-start(bf16[8,128,256]{2,1,0:T(8,128)(2,1)} %get-tuple-element.36), channel_id=1, source_target_pairs={{0,2},{2,0},{4,6},{6,4},{8,10},{10,8},{12,14},{14,12},{1,3},{3,1},... | collective-permute-start | bytes 1572872 | tf_op jit(solution)/shard_map/ppermute | solution.py:345
  58.3 20.3 %collective-permute-start.3 = (bf16[8,128,256]{2,1,0:T(8,128)(2,1)}, bf16[8,128,256]{2,1,0:T(8,128)(2,1)}, u32[]{:S(2)}, u32[]{:S(2)}) collective-permute-start(bf16[8,128,256]{2,1,0:T(8,128)(2,1)} %get-tuple-element.37), channel_id=1, source_target_pairs={{0,14},{2,4},{4,2},{6,8},{8,6},{10,12},{12,10},{14,0},{1,15},{3,5}... | collective-permute-start | bytes 1572872 | tf_op jit(solution)/shard_map/ppermute | solution.py:346
  65.3 18.7 %all-to-all-start.2 = ((f32[16,48,128]{2,1,0:T(8,128)}), f32[16,48,128]{2,1,0:T(8,128)S(1)}, u32[]{:S(2)}, u32[]{:S(2)}) async-start(f32[16,48,128]{2,1,0:T(8,128)} %shard_map.95), calls=%async_computation.2 | async-start | bytes 786432 | tf_op jit(solution)/shard_map/all_to_all | solution.py:29
  70.5 8.0 %copy-start.13 = (bf16[8,128,256]{2,1,0:T(8,128)(2,1)}, bf16[8,128,256]{2,1,0:T(8,128)(2,1)S(1)}, u32[]{:S(2)}) copy-start(bf16[8,128,256]{2,1,0:T(8,128)(2,1)S(1)} %collective-permute-done.2) | copy-start | bytes 1572868
  81.6 48.4 %copy-start.3 = (bf16[1,512,512]{2,1,0:T(8,128)(2,1)S(1)}, bf16[1,512,512]{2,1,0:T(8,128)(2,1)}, u32[]{:S(2)}) copy-start(bf16[1,512,512]{2,1,0:T(8,128)(2,1)} %param.6) | copy-start | bytes 1572868
  81.6 48.4 %copy-start.7 = (bf16[1,512,512]{2,1,0:T(8,128)(2,1)S(1)}, bf16[1,512,512]{2,1,0:T(8,128)(2,1)}, u32[]{:S(2)}) copy-start(bf16[1,512,512]{2,1,0:T(8,128)(2,1)} %param.9) | copy-start | bytes 1572868
  81.6 48.4 %copy-start.9 = (bf16[512,512]{1,0:T(8,128)(2,1)S(1)}, bf16[512,512]{1,0:T(8,128)(2,1)}, u32[]{:S(2)}) copy-start(bf16[512,512]{1,0:T(8,128)(2,1)} %copy-done.8) | copy-start | bytes 1572868
  81.6 16.4 %collective-permute-start.4 = (bf16[4,128,512]{2,1,0:T(8,128)(2,1)}, bf16[4,128,512]{2,1,0:T(8,128)(2,1)S(1)}, u32[]{:S(2)}, u32[]{:S(2)}) collective-permute-start(bf16[4,128,512]{2,1,0:T(8,128)(2,1)} %get-tuple-element.39), channel_id=1, source_target_pairs={{0,1},{1,0},{2,3},{3,2},{4,5},{5,4},{6,7},{7,6},{8,9},{9,8},{10,11... | collective-permute-start | bytes 1572872 | tf_op jit(solution)/shard_map/ppermute | solution.py:25
  84.7 45.3 %all-to-all-start.3 = ((f32[32,16,128]{2,1,0:T(8,128)}), f32[32,16,128]{2,1,0:T(8,128)S(1)}, u32[]{:S(2)}, u32[]{:S(2)}) async-start(f32[32,16,128]{2,1,0:T(8,128)} %get-tuple-element.27), calls=%async_computation.3 | async-start | bytes 524288 | tf_op jit(solution)/shard_map/all_to_all | solution.py:29
  98.0 0.8 copy-start.12
  101.0 16.5 %collective-permute-start.5 = (bf16[2,128,512]{2,1,0:T(8,128)(2,1)}, bf16[2,128,512]{2,1,0:T(8,128)(2,1)S(1)}, u32[]{:S(2)}, u32[]{:S(2)}) collective-permute-start(bf16[2,128,512]{2,1,0:T(8,128)(2,1)} %get-tuple-element.41), channel_id=1, source_target_pairs={{0,4},{4,0},{1,5},{5,1},{2,6},{6,2},{3,7},{7,3},{8,12},{12,8},{9,1... | collective-permute-start | bytes 786440 | tf_op jit(solution)/shard_map/ppermute | solution.py:25
  120.2 13.4 %collective-permute-start.6 = (bf16[1,128,512]{2,1,0:T(8,128)(2,1)}, bf16[1,128,512]{2,1,0:T(8,128)(2,1)S(1)}, u32[]{:S(2)}, u32[]{:S(2)}) collective-permute-start(bf16[1,128,512]{2,1,0:T(8,128)(2,1)} %get-tuple-element.44), channel_id=1, source_target_pairs={{0,8},{8,0},{1,9},{9,1},{2,10},{10,2},{3,11},{11,3},{4,12},{12,4},... | collective-permute-start | bytes 393224 | tf_op jit(solution)/shard_map/ppermute | solution.py:25
  130.0 3.7 %copy-start.14 = (f32[1,128,512]{2,1,0:T(8,128)S(1)}, f32[1,128,512]{2,1,0:T(8,128)}, u32[]{:S(2)}) copy-start(f32[1,128,512]{2,1,0:T(8,128)} %get-tuple-element.43) | copy-start | bytes 786436
  (2 other events, 1.5 us)

commit v6 on v5

--- a/solution.py
+++ b/solution.py
@@ -76,11 +76,17 @@
 
 
 def pseudo_halves(
-    local_hbm, base_hbm, error_hbm, send_ref, keep_ref, local_ref, base_ref, error_ref, sems
+    local_hbm, base_hbm, error_hbm, momentum_hbm, send_ref, keep_ref,
+    local_ref, base_ref, error_ref, momentum_ref, sems,
 ):
     core = lax.axis_index("core")
     half = keep_ref.shape[0]
-    pairs = ((local_hbm, local_ref), (base_hbm, base_ref), (error_hbm, error_ref))
+    pairs = (
+        (local_hbm, local_ref),
+        (base_hbm, base_ref),
+        (error_hbm, error_ref),
+        (momentum_hbm, momentum_ref),
+    )
     for i, (src, dst) in enumerate(pairs):
         pltpu.make_async_copy(src, dst, sems.at[i]).start()
     for i, (src, dst) in enumerate(pairs):
@@ -91,25 +97,18 @@
         base, local = base_ref[at].astype(f32), local_ref[at].astype(f32)
         return base - local + error_ref[at].astype(f32)
 
-    send_ref[...] = pseudo(1 - core)
+    send_ref[:half] = pseudo(1 - core)
+    send_ref[half:] = momentum_ref[...].astype(f32)
     keep_ref[...] = pseudo(core)
 
 
 def key_products(
-    tokens_ref, base_ref, first_ref, its_ref,
-    left_ref, right_ref, kept_ref, full_ref, sent, keep, sems,
+    tokens_ref, base_ref, first_ref,
+    left_ref, right_ref, kept_ref, full_ref, sent, keep, sems, *, own,
 ):
-    y0, core = lax.axis_index("y0"), lax.axis_index("core")
-    mine = first_ref[:, its_ref.shape[1] :].astype(f32)
-    other = its_ref[...].astype(f32)
-    pairs = jnp.concatenate(
-        [
-            jnp.where(core == 0, mine, other)[:, None],
-            jnp.where(core == 0, other, mine)[:, None],
-        ],
-        axis=1,
-    )
-    momentum = pairs.reshape(base_ref.shape[1], base_ref.shape[0]).T
+    y0 = lax.axis_index("y0")
+    momentum = first_ref[:, own:].reshape(base_ref.shape[1], base_ref.shape[0])
+    momentum = momentum.astype(f32).T
     full_ref[...] = momentum.astype(bf16)
     settled = (base_ref[...].astype(f32) - own_mom * momentum).astype(bf16)
     groups, block, cols = keep.shape[0] // 2, keep.shape[1], keep.shape[2]
@@ -137,64 +136,27 @@
 
 
 def fold(*refs, axis, n):
-    came_ref, kept_ref, send_ref, keep_ref = refs[:n], refs[n], refs[n + 1], refs[n + 2]
-    came, held, sent, sems = refs[n + 3 : 2 * n + 3], *refs[2 * n + 3 :]
+    came, kept_ref, send_ref, keep_ref = refs[:n], *refs[n:]
     me = lax.axis_index(axis)
-    halves = (1 - me, me)
-    loads = [
-        [
-            pltpu.make_async_copy(
-                src.at[:, half], dst.at[:, i], sems.at[i * (n + 1) + j]
-            )
-            for j, (src, dst) in enumerate(zip((*came_ref, kept_ref), (*came, held)))
-        ]
-        for i, half in enumerate(halves)
-    ]
-    for load in loads[0] + loads[1]:
-        load.start()
-    out = [
-        pltpu.make_async_copy(sent, send_ref, sems.at[2 * n + 2]),
-        pltpu.make_async_copy(held.at[:, 1], keep_ref, sems.at[2 * n + 3]),
-    ]
-    for i in range(2):
-        for load in loads[i]:
-            load.wait()
-        at, width = 0, held.shape[-1] // n
-        for part in came:
-            here = slice(at, at + width)
-            total = held[:, i, :, here] + part[:, i].astype(f32)
-            if i == 0:
-                sent[:, :, here] = total.astype(bf16)
-            else:
-                held[:, i, :, here] = total
-            at += width
-        out[i].start()
-    for copy in out:
-        copy.wait()
+    width = kept_ref.shape[-1] // n
+    for g in range(kept_ref.shape[0]):
+        for i, part in enumerate(came):
+            at = slice(i * width, (i + 1) * width)
+            send_ref[g, :, at] = (
+                kept_ref[g, 1 - me, :, at] + part[g, 1 - me].astype(f32)
+            ).astype(bf16)
+            keep_ref[g, :, at] = kept_ref[g, me, :, at] + part[g, me].astype(f32)
 
 
 def fold_call(came, kept, axis):
     groups, _, block, cols = kept.shape
-    n = len(came)
-    hbm = pl.BlockSpec(memory_space=pltpu.HBM)
     shape = jax.ShapeDtypeStruct
-    return pl.pallas_call(
-        functools.partial(fold, axis=axis, n=n),
-        out_shape=(
-            shape((groups, block, cols), bf16),
-            shape((groups, block, cols), f32),
-        ),
-        in_specs=[hbm] * (n + 1),
-        out_specs=(hbm, hbm),
-        scratch_shapes=(
-            *[pltpu.VMEM(c.shape, bf16) for c in came],
-            pltpu.VMEM(kept.shape, f32),
-            pltpu.VMEM((groups, block, cols), bf16),
-            pltpu.SemaphoreType.DMA((2 * n + 4,)),
-        ),
-        cost_estimate=pl.CostEstimate(
-            flops=kept.size, bytes_accessed=kept.size * 6, transcendentals=0
-        ),
+    return in_vmem(
+        functools.partial(fold, axis=axis, n=len(came)),
+        (shape((groups, block, cols), bf16), shape((groups, block, cols), f32)),
+        len(came) + 1,
+        12,
+        kept.size,
     )(*came, kept)
 
 
@@ -275,7 +237,7 @@
         cost_estimate=pl.CostEstimate(
             flops=flops, bytes_accessed=flops // 100, transcendentals=0
         ),
-        compiler_params=pltpu.CompilerParams(vmem_limit_bytes=mib << 20),
+        compiler_params=pltpu.CompilerParams(vmem_limit_bytes=(mib << 20) or None),
     )
 
 
@@ -285,28 +247,40 @@
     rank = q_start.shape[1]
     own = rows // replicas
     cols = kv // replicas
+    core = lax.axis_index("core")
     own_tokens = tokens[0]
     block = own_tokens.shape[0] // shards
     shape = jax.ShapeDtypeStruct
 
-    half = shape((rows // 2, kv), f32)
+    half = rows // 2
     given = pltpu.VMEM((rows, kv), bf16)
     send, pair = in_vmem(
         pseudo_halves,
-        (half, half),
-        3,
-        8,
+        (shape((half + cols, kv), f32), shape((half, kv), f32)),
+        4,
+        0,
         1000000,
-        (given, given, given, pltpu.SemaphoreType.DMA((3,))),
+        (
+            given,
+            given,
+            given,
+            pltpu.VMEM((cols, rows), bf16),
+            pltpu.SemaphoreType.DMA((4,)),
+        ),
         far_in=True,
-    )(local_weights[0], outer_base, error_feedback[0])
-    send = swap(send, "core")
-    pair = (pair + send).astype(bf16)
+    )(local_weights[0], outer_base, error_feedback[0], momentum.T)
+    came = swap(send, "core")
+    pair = (pair + came[:half]).astype(bf16)
+    mine, its = momentum.T, came[half:].astype(bf16)
+    core = lax.axis_index("core")
+    both = jnp.concatenate(
+        [jnp.where(core == 0, mine, its), jnp.where(core == 0, its, mine)], axis=0
+    )
     first = exchange(
         jnp.concatenate(
             [
                 pair.reshape(replicas // 2, own, kv),
-                jnp.broadcast_to(momentum.T, (replicas // 2, cols, rows)),
+                jnp.broadcast_to(both, (replicas // 2, 2 * cols, rows)),
             ],
             axis=1,
         ),
@@ -324,14 +298,12 @@
     )(first, q_start.T)
     second = exchange(second, peers)
 
-    its_momentum = swap(first[:, own:], "core")
-
     part = (shards // 2, block, kv // 2)
     whole = (*part[:2], kv)
     left, right, kept, full_momentum = in_vmem(
-        key_products,
+        functools.partial(key_products, own=own),
         (shape(part, bf16), shape(part, bf16), shape(whole, f32), shape((rows, kv), bf16)),
-        4,
+        3,
         16,
         2 * tokens.shape[1] * rows * kv,
         (
@@ -340,7 +312,7 @@
             pltpu.SemaphoreType.DMA((3,)),
         ),
         3,
-    )(own_tokens, outer_base, first, its_momentum)
+    )(own_tokens, outer_base, first)
     across = ("y2", "y1", "y0")
     left = lax.ppermute(left, across, [(i, i ^ 1) for i in range(8)])
     right = lax.ppermute(

time: 135 us -> 134 us (level)
  blocking collectives: 24.7 us -> 31 us
  waiting for transfers between devices: 26.7 us -> 22.5 us
  starting transfers between devices: 53.9 us -> 50.8 us
    ppermute x1, waiting for transfers between devices: 8.03 us -> 0.49 us  [on_device(): lax.ppermute(right, across, [(i, (i + 1 if i % 2 else i - 1) % 8) for i i...]
    all_to_all x3, waiting for transfers between devices: 0.01 us -> 6.54 us  [exchange(): return lax.all_to_all(x, axis, 0, 0, tiled=True)]
    all_to_all x1, blocking collectives: 24.7 us -> 31 us  [exchange(): return lax.all_to_all(x, axis, 0, 0, tiled=True)]
    pallas_call x5, Pallas kernels: 9.44 us -> 6.62 us  [the longest x1 2.46 us: on_device(): in_vmem(pseudo_halves, (shape((half + cols, kv), f32), shape((half, kv),...]
    ppermute x5 -> x4, starting transfers between devices: 22.7 us -> 20.7 us  [swap(): return lax.ppermute(x, axis, [(0, 1), (1, 0)])]
    ppermute x1, waiting for transfers between devices: 1.66 us -> 0.01 us  [on_device(): left = lax.ppermute(left, across, [(i, i ^ 1) for i in range(8)])]
    ppermute x5 -> x4, waiting for transfers between devices: 17 us -> 15.4 us  [swap(): return lax.ppermute(x, axis, [(0, 1), (1, 0)])]
    unnamed x32 -> x26, local copies, waits for them, and re-layouts: 6.78 us -> 6.8 us
  transfers between devices with their start and end apart: 10 -> 9, of which waited for: 6 -> 4; matrix products, arithmetic and copies ran while one was open for 0% -> 0% of each run, Pallas kernels for 14% -> 11%
where the time goes in v6:
time: 134 us; the launch traced here: 133 us
  starting transfers between devices  50.8 us (38%)
  blocking collectives  31 us (23%)
  waiting for transfers between devices  22.5 us (17%)
  Pallas kernels  19.6 us (15%)
  local copies, waits for them, and re-layouts  6.84 us (5%)
  other arithmetic  1.9 us (1%)
    all_to_all x1, blocking collectives, exchange(): return lax.all_to_all(x, axis, 0, 0, tiled=True)  31 us
    all_to_all x3, starting transfers between devices, exchange(): return lax.all_to_all(x, axis, 0, 0, tiled=True)  21.9 us
    ppermute x4, starting transfers between devices, swap(): return lax.ppermute(x, axis, [(0, 1), (1, 0)])  20.7 us
    ppermute x4, waiting for transfers between devices, swap(): return lax.ppermute(x, axis, [(0, 1), (1, 0)])  15.4 us
    unnamed x26, local copies, waits for them, and re-layouts  6.8 us
    all_to_all x3, waiting for transfers between devices, exchange(): return lax.all_to_all(x, axis, 0, 0, tiled=True)  6.54 us
    ppermute x1, starting transfers between devices, on_device(): lax.ppermute(right, across, [(i, (i + 1 if i % 2 else i - 1) % 8) for i i...  4.87 us
    pallas_call x1, Pallas kernels, on_device(): in_vmem(functools.partial(bases, own=own, rank=rank), (shape((rows, lanes...  4.16 us
  transfers between devices with their start and end apart: 9, of which 4 were waited for; matrix products, arithmetic and copies ran while one was open for 0% of the time, Pallas kernels for 11%

profile of v6, /device:TPU:1, one launch (start us, length us, event | category | flops | bytes accessed | tf_op | source)
XLA Modules:
  0.0 133.5 jit_solution(5858031719683789579)
XLA Ops:
  0.6 2.5 %shard_map.93 = (f32[272,512]{1,0:T(8,128)}, f32[256,512]{1,0:T(8,128)}) custom-call(bf16[512,512]{1,0:T(8,128)(2,1)} %bitcast.28, bf16[512,512]{1,0:T(8,128)(2,1)} %base_ref.3, bf16[512,512]{1,0:T(8,128)(2,1)} %bitcast.30, bf16[16,512]{1,0:T(8,128)(2,1)} %bitcast.36), custom_call_target="tpu_custom_call" | custom-call | flops 1000000 | bytes 10000 | tf_op jit(solution)/shard_map/pallas_call | solution.py:257
  3.1 8.7 %collective-permute-start = (f32[272,512]{1,0:T(8,128)}, f32[272,512]{1,0:T(8,128)S(1)}, u32[]{:S(2)}, u32[]{:S(2)}) collective-permute-start(f32[272,512]{1,0:T(8,128)} %get-tuple-element.26), channel_id=1, source_target_pairs={{0,16},{16,0},{1,17},{17,1},{2,18},{18,2},{3,19},{19,3},{4,20},{20... | collective-permute-start | bytes 1671176 | tf_op jit(solution)/shard_map/ppermute | solution.py:25
  11.9 1.8 %collective-permute-done = f32[272,512]{1,0:T(8,128)S(1)} collective-permute-done((f32[272,512]{1,0:T(8,128)}, f32[272,512]{1,0:T(8,128)S(1)}, u32[]{:S(2)}, u32[]{:S(2)}) %collective-permute-start) | collective-permute-done | bytes 557088 | tf_op jit(solution)/shard_map/ppermute | solution.py:25
  13.7 1.1 fusion
  14.9 31.0 %all_to_all.20.first_ref = bf16[16,48,512]{2,1,0:T(8,128)(2,1)S(1)} all-to-all(bf16[16,48,512]{2,1,0:T(8,128)(2,1)S(1)} %pad_maximum_fusion), channel_id=1, replica_groups=mesh['z'=8,'xh'=2,'core'=2,'y2'=2,'y1'=2,'y0'=2,'xl'=2] {'z','xh'}, dimensions={0} | all-to-all | bytes 1572864 | tf_op jit(solution)/shard_map/all_to_all | solution.py:29
  46.0 2.0 %shard_map.94 = f32[32,16,128]{2,1,0:T(8,128)} custom-call(bf16[16,48,512]{2,1,0:T(8,128)(2,1)S(1)} %all_to_all.20.first_ref, f32[32,512]{1,0:T(8,128)S(1)} %bitcast.38), custom_call_target="tpu_custom_call" | custom-call | flops 40000000 | bytes 400000 | tf_op jit(solution)/shard_map/pallas_call | solution.py:290
  47.9 6.2 %all-to-all-start.1 = ((f32[32,16,128]{2,1,0:T(8,128)}), f32[32,16,128]{2,1,0:T(8,128)}, u32[]{:S(2)}, u32[]{:S(2)}) async-start(f32[32,16,128]{2,1,0:T(8,128)} %shard_map.94), calls=%async_computation.1 | async-start | bytes 524288 | tf_op jit(solution)/shard_map/all_to_all | solution.py:29
  54.1 1.6 %copy-done = bf16[1,2048,512]{2,1,0:T(8,128)(2,1)S(1)} copy-done((bf16[1,2048,512]{2,1,0:T(8,128)(2,1)S(1)}, bf16[1,2048,512]{2,1,0:T(8,128)(2,1)}, u32[]{:S(2)}) %copy-start) | copy-done | bytes 2097176
  55.7 1.9 %shard_map.98 = (bf16[8,128,256]{2,1,0:T(8,128)(2,1)}, bf16[8,128,256]{2,1,0:T(8,128)(2,1)}, f32[8,128,512]{2,1,0:T(8,128)S(1)}, bf16[512,512]{1,0:T(8,128)(2,1)S(1)}) custom-call(bf16[2048,512]{1,0:T(8,128)(2,1)S(1)} %bitcast.26, bf16[512,512]{1,0:T(8,128)(2,1)S(1)} %copy-done.3, bf16[16,48,512]{2,1,0:T(8,128)(2,1)S(1)} %all_to_all.20.first_ref), custom_call_target="tpu_custom_call" | custom-call | flops 1073741824 | bytes 10737418 | tf_op jit(solution)/shard_map/pallas_call | solution.py:303
  58.4 3.2 %collective-permute-start.1 = (bf16[8,128,256]{2,1,0:T(8,128)(2,1)}, bf16[8,128,256]{2,1,0:T(8,128)(2,1)}, u32[]{:S(2)}, u32[]{:S(2)}) collective-permute-start(bf16[8,128,256]{2,1,0:T(8,128)(2,1)} %get-tuple-element.36), channel_id=1, source_target_pairs={{0,2},{2,0},{4,6},{6,4},{8,10},{10,8},{12,14},{14,12},{1,3},{3,1},... | collective-permute-start | bytes 1572872 | tf_op jit(solution)/shard_map/ppermute | solution.py:317
  61.6 4.9 %collective-permute-start.2 = (bf16[8,128,256]{2,1,0:T(8,128)(2,1)}, bf16[8,128,256]{2,1,0:T(8,128)(2,1)}, u32[]{:S(2)}, u32[]{:S(2)}) collective-permute-start(bf16[8,128,256]{2,1,0:T(8,128)(2,1)} %get-tuple-element.37), channel_id=1, source_target_pairs={{0,14},{2,4},{4,2},{6,8},{8,6},{10,12},{12,10},{14,0},{1,15},{3,5}... | collective-permute-start | bytes 1572872 | tf_op jit(solution)/shard_map/ppermute | solution.py:318
  66.5 1.6 %copy-done.1 = bf16[1,2048,512]{2,1,0:T(8,128)(2,1)S(1)} copy-done((bf16[1,2048,512]{2,1,0:T(8,128)(2,1)S(1)}, bf16[1,2048,512]{2,1,0:T(8,128)(2,1)}, u32[]{:S(2)}) %copy-start.1) | copy-done | bytes 2097176
  68.1 3.0 %shard_map.95 = f32[16,48,128]{2,1,0:T(8,128)} custom-call(f32[32,16,128]{2,1,0:T(8,128)} %all-to-all-done.1.second_ref, bf16[2048,512]{1,0:T(8,128)(2,1)S(1)} %bitcast.27), custom_call_target="tpu_custom_call" | custom-call | flops 500000000 | bytes 5000000 | tf_op jit(solution)/shard_map/pallas_call | solution.py:333
  71.1 6.9 %all-to-all-start.2 = ((f32[16,48,128]{2,1,0:T(8,128)}), f32[16,48,128]{2,1,0:T(8,128)S(1)}, u32[]{:S(2)}, u32[]{:S(2)}) async-start(f32[16,48,128]{2,1,0:T(8,128)} %shard_map.95), calls=%async_computation.2 | async-start | bytes 786432 | tf_op jit(solution)/shard_map/all_to_all | solution.py:29
  78.5 2.1 %shard_map.100 = (bf16[4,128,512]{2,1,0:T(8,128)(2,1)}, f32[4,128,512]{2,1,0:T(8,128)S(1)}) custom-call(bf16[4,2,128,256]{3,2,1,0:T(8,128)(2,1)} %bitcast.8.refs_0_, bf16[4,2,128,256]{3,2,1,0:T(8,128)(2,1)} %bitcast.9.refs_1_, f32[4,2,128,512]{3,2,1,0:T(8,128)S(1)} %bitcast.25), custom_call_target="tpu_custom_call" | custom-call | flops 524288 | bytes 5242 | tf_op jit(solution)/shard_map/pallas_call | solution.py:154
  81.6 2.8 %collective-permute-start.3 = (bf16[4,128,512]{2,1,0:T(8,128)(2,1)}, bf16[4,128,512]{2,1,0:T(8,128)(2,1)S(1)}, u32[]{:S(2)}, u32[]{:S(2)}) collective-permute-start(bf16[4,128,512]{2,1,0:T(8,128)(2,1)} %get-tuple-element.39), channel_id=1, source_target_pairs={{0,1},{1,0},{2,3},{3,2},{4,5},{5,4},{6,7},{7,6},{8,9},{9,8},{10,11... | collective-permute-start | bytes 1572872 | tf_op jit(solution)/shard_map/ppermute | solution.py:25
  84.4 6.5 %all-to-all-done.2.third_ref = f32[16,48,128]{2,1,0:T(8,128)S(1)} async-done(((f32[16,48,128]{2,1,0:T(8,128)}), f32[16,48,128]{2,1,0:T(8,128)S(1)}, u32[]{:S(2)}, u32[]{:S(2)}) %all-to-all-start.2) | async-done | bytes 393248 | tf_op jit(solution)/shard_map/all_to_all | solution.py:29
  92.3 8.9 %all-to-all-start.3 = ((f32[32,16,128]{2,1,0:T(8,128)}), f32[32,16,128]{2,1,0:T(8,128)S(1)}, u32[]{:S(2)}, u32[]{:S(2)}) async-start(f32[32,16,128]{2,1,0:T(8,128)} %get-tuple-element.27), calls=%async_computation.3 | async-start | bytes 524288 | tf_op jit(solution)/shard_map/all_to_all | solution.py:29
  101.2 1.2 copy-done.6
  102.5 3.1 %collective-permute-start.4 = (bf16[2,128,512]{2,1,0:T(8,128)(2,1)S(1)}, bf16[2,128,512]{2,1,0:T(8,128)(2,1)S(1)}, u32[]{:S(2)}, u32[]{:S(2)}) collective-permute-start(bf16[2,128,512]{2,1,0:T(8,128)(2,1)S(1)} %get-tuple-element.41), channel_id=1, source_target_pairs={{0,4},{4,0},{1,5},{5,1},{2,6},{6,2},{3,7},{7,3},{8,12},{12,8},{9,1... | collective-permute-start | bytes 786440 | tf_op jit(solution)/shard_map/ppermute | solution.py:25
  105.6 13.7 %collective-permute-done.4 = bf16[2,128,512]{2,1,0:T(8,128)(2,1)S(1)} collective-permute-done((bf16[2,128,512]{2,1,0:T(8,128)(2,1)S(1)}, bf16[2,128,512]{2,1,0:T(8,128)(2,1)S(1)}, u32[]{:S(2)}, u32[]{:S(2)}) %collective-permute-start.4) | collective-permute-done | bytes 262176 | tf_op jit(solution)/shard_map/ppermute | solution.py:25
  119.3 6.1 %collective-permute-start.5 = (bf16[1,128,512]{2,1,0:T(8,128)(2,1)S(1)}, bf16[1,128,512]{2,1,0:T(8,128)(2,1)S(1)}, u32[]{:S(2)}, u32[]{:S(2)}) collective-permute-start(bf16[1,128,512]{2,1,0:T(8,128)(2,1)S(1)} %get-tuple-element.44), channel_id=1, source_target_pairs={{0,8},{8,0},{1,9},{9,1},{2,10},{10,2},{3,11},{11,3},{4,12},{12,4},... | collective-permute-start | bytes 393224 | tf_op jit(solution)/shard_map/ppermute | solution.py:25
  125.5 4.2 %shard_map.97 = (f32[512,128]{1,0:T(8,128)S(1)}, f32[128,128]{1,0:T(8,128)S(1)}, f32[128,128]{1,0:T(8,128)S(1)}) custom-call(f32[48,128]{1,0:T(8,128)S(1)} %copy-done.12, f32[32,16,128]{2,1,0:T(8,128)} %all-to-all-done.1.second_ref), custom_call_target="tpu_custom_call" | custom-call | flops 100000000 | bytes 1000000 | tf_op jit(solution)/shard_map/pallas_call | solution.py:353
  129.7 3.1 %shard_map.99 = (bf16[512,512]{1,0:T(8,128)(2,1)}, bf16[16,512]{1,0:T(8,128)(2,1)}, bf16[512,512]{1,0:T(8,128)(2,1)}, f32[128,512]{1,0:T(8,128)S(1)}) custom-call(f32[32,16,128]{2,1,0:T(8,128)S(1)} %all-to-all-done.3.fourth_ref, f32[128,128]{1,0:T(8,128)S(1)} %get-tuple-element.29.inverse_ref, f32[512,128]{1,0:T(8,128)S(1)} %get-tuple-element.30.basis_ref, ...), custom_call_target="tpu_custom_call" | custom-call | flops 400000000 | bytes 4000000 | tf_op jit(solution)/shard_map/pallas_call | solution.py:364
  (37 shorter events, 4.6 us)
Async XLA Ops:
  0.6 13.0 %copy-start.9 = (bf16[512,16]{0,1:T(8,128)(2,1)S(1)}, bf16[512,16]{0,1:T(8,128)(2,1)}, u32[]{:S(2)}) copy-start(bf16[512,16]{0,1:T(8,128)(2,1)} %param.8) | copy-start | bytes 49156
  3.1 10.5 %collective-permute-start = (f32[272,512]{1,0:T(8,128)}, f32[272,512]{1,0:T(8,128)S(1)}, u32[]{:S(2)}, u32[]{:S(2)}) collective-permute-start(f32[272,512]{1,0:T(8,128)} %get-tuple-element.26), channel_id=1, source_target_pairs={{0,16},{16,0},{1,17},{17,1},{2,18},{18,2},{3,19},{19,3},{4,20},{20... | collective-permute-start | bytes 1671176 | tf_op jit(solution)/shard_map/ppermute | solution.py:25
  14.8 31.1 %copy-start.10 = (f32[512,32]{0,1:T(8,128)S(1)}, f32[512,32]{0,1:T(8,128)}, u32[]{:S(2)}) copy-start(f32[512,32]{0,1:T(8,128)} %param.10) | copy-start | bytes 196612
  14.9 39.2 %copy-start.3 = (bf16[512,512]{1,0:T(8,128)(2,1)S(1)}, bf16[512,512]{1,0:T(8,128)(2,1)}, u32[]{:S(2)}) copy-start(bf16[512,512]{1,0:T(8,128)(2,1)} %base_ref.3) | copy-start | bytes 1572868
  47.9 18.6 %all-to-all-start.1 = ((f32[32,16,128]{2,1,0:T(8,128)}), f32[32,16,128]{2,1,0:T(8,128)}, u32[]{:S(2)}, u32[]{:S(2)}) async-start(f32[32,16,128]{2,1,0:T(8,128)} %shard_map.94), calls=%async_computation.1 | async-start | bytes 524288 | tf_op jit(solution)/shard_map/all_to_all | solution.py:29
  54.1 1.6 %copy-start = (bf16[1,2048,512]{2,1,0:T(8,128)(2,1)S(1)}, bf16[1,2048,512]{2,1,0:T(8,128)(2,1)}, u32[]{:S(2)}) copy-start(bf16[1,2048,512]{2,1,0:T(8,128)(2,1)} %param.11) | copy-start | bytes 6291460
  57.6 0.8 copy-start.7
  58.4 19.6 %collective-permute-start.1 = (bf16[8,128,256]{2,1,0:T(8,128)(2,1)}, bf16[8,128,256]{2,1,0:T(8,128)(2,1)}, u32[]{:S(2)}, u32[]{:S(2)}) collective-permute-start(bf16[8,128,256]{2,1,0:T(8,128)(2,1)} %get-tuple-element.36), channel_id=1, source_target_pairs={{0,2},{2,0},{4,6},{6,4},{8,10},{10,8},{12,14},{14,12},{1,3},{3,1},... | collective-permute-start | bytes 1572872 | tf_op jit(solution)/shard_map/ppermute | solution.py:317
  61.6 16.9 %collective-permute-start.2 = (bf16[8,128,256]{2,1,0:T(8,128)(2,1)}, bf16[8,128,256]{2,1,0:T(8,128)(2,1)}, u32[]{:S(2)}, u32[]{:S(2)}) collective-permute-start(bf16[8,128,256]{2,1,0:T(8,128)(2,1)} %get-tuple-element.37), channel_id=1, source_target_pairs={{0,14},{2,4},{4,2},{6,8},{8,6},{10,12},{12,10},{14,0},{1,15},{3,5}... | collective-permute-start | bytes 1572872 | tf_op jit(solution)/shard_map/ppermute | solution.py:318
  66.5 1.6 %copy-start.1 = (bf16[1,2048,512]{2,1,0:T(8,128)(2,1)S(1)}, bf16[1,2048,512]{2,1,0:T(8,128)(2,1)}, u32[]{:S(2)}) copy-start(bf16[1,2048,512]{2,1,0:T(8,128)(2,1)} %param.11) | copy-start | bytes 6291460
  71.1 19.8 %all-to-all-start.2 = ((f32[16,48,128]{2,1,0:T(8,128)}), f32[16,48,128]{2,1,0:T(8,128)S(1)}, u32[]{:S(2)}, u32[]{:S(2)}) async-start(f32[16,48,128]{2,1,0:T(8,128)} %shard_map.95), calls=%async_computation.2 | async-start | bytes 786432 | tf_op jit(solution)/shard_map/all_to_all | solution.py:29
  80.6 1.0 copy-start.5
  81.6 19.6 %collective-permute-start.3 = (bf16[4,128,512]{2,1,0:T(8,128)(2,1)}, bf16[4,128,512]{2,1,0:T(8,128)(2,1)S(1)}, u32[]{:S(2)}, u32[]{:S(2)}) collective-permute-start(bf16[4,128,512]{2,1,0:T(8,128)(2,1)} %get-tuple-element.39), channel_id=1, source_target_pairs={{0,1},{1,0},{2,3},{3,2},{4,5},{5,4},{6,7},{7,6},{8,9},{9,8},{10,11... | collective-permute-start | bytes 1572872 | tf_op jit(solution)/shard_map/ppermute | solution.py:25
  91.7 0.6 copy-start.11
  92.3 37.4 %copy-start.2 = (bf16[1,512,512]{2,1,0:T(8,128)(2,1)S(1)}, bf16[1,512,512]{2,1,0:T(8,128)(2,1)}, u32[]{:S(2)}) copy-start(bf16[1,512,512]{2,1,0:T(8,128)(2,1)} %param.6) | copy-start | bytes 1572868
  92.3 37.4 %copy-start.4 = (bf16[1,512,512]{2,1,0:T(8,128)(2,1)S(1)}, bf16[1,512,512]{2,1,0:T(8,128)(2,1)}, u32[]{:S(2)}) copy-start(bf16[1,512,512]{2,1,0:T(8,128)(2,1)} %param.9) | copy-start | bytes 1572868
  92.3 37.4 %all-to-all-start.3 = ((f32[32,16,128]{2,1,0:T(8,128)}), f32[32,16,128]{2,1,0:T(8,128)S(1)}, u32[]{:S(2)}, u32[]{:S(2)}) async-start(f32[32,16,128]{2,1,0:T(8,128)} %get-tuple-element.27), calls=%async_computation.3 | async-start | bytes 524288 | tf_op jit(solution)/shard_map/all_to_all | solution.py:29
  101.2 1.2 copy-start.6
  102.4 23.0 %copy-start.12 = (f32[48,128]{1,0:T(8,128)S(1)}, f32[48,128]{1,0:T(8,128)}, u32[]{:S(2)}) copy-start(f32[48,128]{1,0:T(8,128)} %copy-done.11) | copy-start | bytes 73732
  102.4 27.2 %copy-start.8 = (bf16[512,512]{1,0:T(8,128)(2,1)S(1)}, bf16[512,512]{1,0:T(8,128)(2,1)}, u32[]{:S(2)}) copy-start(bf16[512,512]{1,0:T(8,128)(2,1)} %copy-done.7) | copy-start | bytes 1572868
  102.5 16.8 %collective-permute-start.4 = (bf16[2,128,512]{2,1,0:T(8,128)(2,1)S(1)}, bf16[2,128,512]{2,1,0:T(8,128)(2,1)S(1)}, u32[]{:S(2)}, u32[]{:S(2)}) collective-permute-start(bf16[2,128,512]{2,1,0:T(8,128)(2,1)S(1)} %get-tuple-element.41), channel_id=1, source_target_pairs={{0,4},{4,0},{1,5},{5,1},{2,6},{6,2},{3,7},{7,3},{8,12},{12,8},{9,1... | collective-permute-start | bytes 786440 | tf_op jit(solution)/shard_map/ppermute | solution.py:25
  119.3 13.4 %collective-permute-start.5 = (bf16[1,128,512]{2,1,0:T(8,128)(2,1)S(1)}, bf16[1,128,512]{2,1,0:T(8,128)(2,1)S(1)}, u32[]{:S(2)}, u32[]{:S(2)}) collective-permute-start(bf16[1,128,512]{2,1,0:T(8,128)(2,1)S(1)} %get-tuple-element.44), channel_id=1, source_target_pairs={{0,8},{8,0},{1,9},{9,1},{2,10},{10,2},{3,11},{11,3},{4,12},{12,4},... | collective-permute-start | bytes 393224 | tf_op jit(solution)/shard_map/ppermute | solution.py:25

commit v7 on v4

--- a/solution.py
+++ b/solution.py
@@ -29,20 +29,6 @@
     return lax.all_to_all(x, axis, 0, 0, tiled=True)
 
 
-def copy_for_each(x, axis):
-    return exchange(jnp.broadcast_to(x, (lax.axis_size(axis), *x.shape)), axis)
-
-
-def pick(x, at, dim):
-    return lax.dynamic_index_in_dim(x, at, dim, keepdims=False)
-
-
-def halve(x, axis, dim):
-    me = lax.axis_index(axis)
-    other = swap(pick(x, 1 - me, dim).astype(bf16), axis)
-    return pick(x, me, dim) + other.astype(f32)
-
-
 def dot(a, b, dims, precision=None):
     return lax.dot_general(
         a, b, (dims, ((), ())), precision=precision, preferred_element_type=f32
@@ -54,7 +40,7 @@
 
 
 def moments(first_ref, q_ref, hbm_ref, out_ref, *, own, rank, replicas):
-    mean = jnp.sum(first_ref[...].astype(f32), axis=0) * (1.0 / replicas)
+    mean = jnp.sum(first_ref[:, :own].astype(f32), axis=0) * (1.0 / replicas)
     q = jnp.concatenate([q_ref[...]] * 4, axis=0)
     p = dot(mean, q, ((1,), (1,)), highest)
     group = lane_group(p.shape, rank)
@@ -90,12 +76,23 @@
 
 
 def key_products(
-    tokens_ref, base_ref, momentum_ref, left_ref, right_ref, keep_ref, sent, sems
+    tokens_ref, base_ref, first_ref, its_ref,
+    left_ref, right_ref, kept_ref, full_ref, sent, keep, sems,
 ):
-    y0 = lax.axis_index("y0")
-    settled = base_ref[...].astype(f32) - own_mom * momentum_ref[...].astype(f32)
-    settled = settled.astype(bf16)
-    groups, block, cols = keep_ref.shape[0] // 2, keep_ref.shape[1], keep_ref.shape[2]
+    y0, core = lax.axis_index("y0"), lax.axis_index("core")
+    mine = first_ref[:, its_ref.shape[1] :].astype(f32)
+    other = its_ref[...].astype(f32)
+    pairs = jnp.concatenate(
+        [
+            jnp.where(core == 0, mine, other)[:, None],
+            jnp.where(core == 0, other, mine)[:, None],
+        ],
+        axis=1,
+    )
+    momentum = pairs.reshape(base_ref.shape[1], base_ref.shape[0]).T
+    full_ref[...] = momentum.astype(bf16)
+    settled = (base_ref[...].astype(f32) - own_mom * momentum).astype(bf16)
+    groups, block, cols = keep.shape[0] // 2, keep.shape[1], keep.shape[2]
     half = cols // 2
 
     def product(i, parity):
@@ -108,13 +105,94 @@
     copies = [
         pltpu.make_async_copy(sent.at[:, :, :half], left_ref, sems.at[0]),
         pltpu.make_async_copy(sent.at[:, :, half:], right_ref, sems.at[1]),
+        pltpu.make_async_copy(
+            keep, kept_ref.at[: keep.shape[0]], sems.at[2]
+        ),
     ]
-    for copy in copies:
+    for copy in copies[:2]:
         copy.start()
     for i in range(groups):
-        keep_ref[2 * i : 2 * i + 2] = product(i, y0)
+        keep[2 * i : 2 * i + 2] = product(i, y0)
+    copies[2].start()
     for copy in copies:
         copy.wait()
+
+
+def fold(*refs, stage):
+    y2, y1, xl = (lax.axis_index(a) for a in ("y2", "y1", "xl"))
+    if stage == 2:
+        blocks = [(2 * q + 1 - xl,) for q in range(4)]
+    elif stage == 3:
+        blocks = [(4 * h + 2 * (1 - y1) + xl, 2 * h + 1 - y1) for h in range(2)]
+    else:
+        blocks = [
+            (4 * h + 2 * y1 + xl, 2 * h + y1, h) for h in (1 - y2, y2)
+        ]
+    n = stage + 1
+    given, outs = refs[:n], refs[n : -(n + 2)]
+    held, sent, sems = refs[-(n + 2) : -2], refs[-2], refs[-1]
+    kept, left, right, *later = held
+    half = left.shape[-1]
+
+    def loads(i):
+        at = (blocks[i][0],) * 2 + blocks[i]
+        return [
+            pltpu.make_async_copy(ref.at[j], buf.at[i], sems.at[i * n + k])
+            for k, (ref, buf, j) in enumerate(zip(given, held, at))
+        ]
+
+    waits = [loads(i) for i in range(len(blocks))]
+    for each in waits:
+        for load in each:
+            load.start()
+    last = len(blocks) * n
+    stores = []
+    for i, each in enumerate(waits):
+        for load in each:
+            load.wait()
+        for came, at in ((left, slice(0, half)), (right, slice(half, 2 * half))):
+            total = kept[i, :, at] + came[i].astype(f32)
+            for more in later:
+                total = total + more[i, :, at].astype(f32)
+            if i < outs[0].shape[0]:
+                sent[i, :, at] = total.astype(bf16)
+            else:
+                outs[1][:, at] = total
+        if i < outs[0].shape[0]:
+            stores.append(
+                pltpu.make_async_copy(sent.at[i], outs[0].at[i], sems.at[last + i])
+            )
+            stores[-1].start()
+    for store in stores:
+        store.wait()
+
+
+def fold_call(stage, kept, *came):
+    count = {2: 4, 3: 2, 4: 1}[stage]
+    block, cols = kept.shape[1:]
+    hbm = pl.BlockSpec(memory_space=pltpu.HBM)
+    shape = jax.ShapeDtypeStruct
+    out_shape, out_specs = (shape((count, block, cols), bf16),), (hbm,)
+    if stage == 4:
+        out_shape += (shape((block, cols), f32),)
+        out_specs += (pl.BlockSpec(memory_space=pltpu.VMEM),)
+    number = max(count, 2)
+    given = (kept, *came)
+    return pl.pallas_call(
+        functools.partial(fold, stage=stage),
+        out_shape=out_shape,
+        in_specs=[hbm] * len(given),
+        out_specs=out_specs,
+        scratch_shapes=(
+            *[pltpu.VMEM((number, *a.shape[1:]), a.dtype) for a in given],
+            pltpu.VMEM((count, block, cols), bf16),
+            pltpu.SemaphoreType.DMA((number * (len(given) + 1),)),
+        ),
+        cost_estimate=pl.CostEstimate(
+            flops=count * block * cols, bytes_accessed=8 * count * block * cols,
+            transcendentals=0,
+        ),
+    )(*given)
 
 
 def shard_sums(third_ref, hbm_ref, total_ref, copies_ref):
@@ -194,7 +272,7 @@
         cost_estimate=pl.CostEstimate(
             flops=flops, bytes_accessed=flops // 100, transcendentals=0
         ),
-        compiler_params=pltpu.CompilerParams(vmem_limit_bytes=mib << 20),
+        compiler_params=pltpu.CompilerParams(vmem_limit_bytes=(mib << 20) or None),
     )
 
 
@@ -205,19 +283,28 @@
     own = rows // replicas
     cols = kv // replicas
     core = lax.axis_index("core")
-    base = outer_base.astype(f32)
     own_tokens = tokens[0]
     block = own_tokens.shape[0] // shards
     shape = jax.ShapeDtypeStruct
 
-    my_momentum = copy_for_each(momentum.T, chips)
-
-    pseudo = base - local_weights[0].astype(f32) + error_feedback[0].astype(f32)
-    halves = pseudo.reshape(2, rows // 2, kv)
-    pair = swap(pick(halves, 1 - core, 0), "core")
-    pair = (pick(halves, core, 0) + pair).astype(bf16)
-    pair, my_momentum = lax.optimization_barrier((pair, my_momentum))
-    first = exchange(pair.reshape(replicas // 2, own, kv), chips)
+    pseudo = (
+        outer_base.astype(f32)
+        - local_weights[0].astype(f32)
+        + error_feedback[0].astype(f32)
+    ).reshape(2, rows // 2, kv)
+    core = lax.axis_index("core")
+    pair = swap(lax.dynamic_index_in_dim(pseudo, 1 - core, 0, False), "core")
+    pair = (lax.dynamic_index_in_dim(pseudo, core, 0, False) + pair).astype(bf16)
+    first = exchange(
+        jnp.concatenate(
+            [
+                pair.reshape(replicas // 2, own, kv),
+                jnp.broadcast_to(momentum.T, (replicas // 2, cols, rows)),
+            ],
+            axis=1,
+        ),
+        chips,
+    )
     lanes = 4 * rank
     (second,) = in_vmem(
         functools.partial(moments, own=own, rank=rank, replicas=replicas),
@@ -230,36 +317,33 @@
     )(first, q_start.T)
     second = exchange(second, peers)
 
-    its_momentum = swap(my_momentum, "core")
-    full_momentum = jnp.stack(
-        [
-            jnp.where(core == 0, my_momentum, its_momentum),
-            jnp.where(core == 0, its_momentum, my_momentum),
-        ],
-        axis=1,
-    ).reshape(kv, rows)
-    full_momentum = full_momentum.T
+    its_momentum = swap(first[:, own:], "core")
 
     part = (shards // 2, block, kv // 2)
-    left, right, keep = in_vmem(
+    whole = (*part[:2], kv)
+    roomy = shape((2 * part[0], *whole[1:]), f32)
+    left, right, kept, full_momentum = in_vmem(
         key_products,
-        (shape(part, bf16), shape(part, bf16), shape((*part[:2], kv), f32)),
+        (shape(part, bf16), shape(part, bf16), roomy, shape((rows, kv), bf16)),
+        4,
+        16,
+        2 * tokens.shape[1] * rows * kv,
+        (
+            pltpu.VMEM(whole, bf16),
+            pltpu.VMEM(whole, f32),
+            pltpu.SemaphoreType.DMA((3,)),
+        ),
         3,
-        12,
-        2 * tokens.shape[1] * rows * kv,
-        (pltpu.VMEM((*part[:2], kv), bf16), pltpu.SemaphoreType.DMA((2,))),
-        2,
-    )(own_tokens, outer_base, full_momentum)
+    )(own_tokens, outer_base, first, its_momentum)
     across = ("y2", "y1", "y0")
     left = lax.ppermute(left, across, [(i, i ^ 1) for i in range(8)])
     right = lax.ppermute(
         right, across, [(i, (i + 1 if i % 2 else i - 1) % 8) for i in range(8)]
     )
-    key_part = keep + jnp.concatenate([left, right], axis=-1).astype(f32)
-    key_part = halve(key_part.reshape(4, 2, block, kv), "xl", 1)
-    key_part = key_part.reshape(2, 2, block, kv)
-    key_part = halve(key_part, "y1", 1)
-    key_sum = halve(key_part, "y2", 0)
+    came = [left, right]
+    for stage, axis in ((2, "xl"), (3, "y1"), (4, "y2")):
+        send, *key_sum = fold_call(stage, kept, *came)
+        came.append(swap(send, axis))
 
     tall = (shards, own + block // 4, lanes)
     (third,) = in_vmem(
@@ -316,7 +400,7 @@
         full_momentum,
         momentum.T,
     )
-    key_rows = (key_sum - key_low).astype(bf16)
+    key_rows = (key_sum[0] + came[-1][0].astype(f32) - key_low).astype(bf16)
     return new_base, new_momentum.T, new_error[None], key_rows[None]
 
 

time: 132 us -> 137 us (1.038)
  blocking collectives: 0 us -> 24.5 us
  waiting for transfers between devices: 41.3 us -> 27.4 us
  Pallas kernels: 12.8 us -> 19.7 us
  other arithmetic: 10.4 us -> 4.51 us
  starting transfers between devices: 57.9 us -> 53.3 us
  local copies, waits for them, and re-layouts: 8.27 us -> 6.13 us
    all_to_all x5 -> x3, waiting for transfers between devices: 33.6 us -> 0.39 us  [exchange(): return lax.all_to_all(x, axis, 0, 0, tiled=True)]
    all_to_all x0 -> x1, blocking collectives: none -> 24.5 us  [exchange(): return lax.all_to_all(x, axis, 0, 0, tiled=True)]
    ppermute x5, waiting for transfers between devices: 7.65 us -> 17.3 us  [swap(): return lax.ppermute(x, axis, [(0, 1), (1, 0)])]
    ppermute x1, waiting for transfers between devices: 0.01 us -> 8.02 us  [on_device(): lax.ppermute(right, across, [(i, (i + 1 if i % 2 else i - 1) % 8) for i i...]
    add x4 -> x1, other arithmetic: 8.8 us -> 1.7 us  [on_device(): outer_base.astype(f32) - local_weights[0].astype(f32)]
    pallas_call x1 -> x4, Pallas kernels: 1.76 us -> 8.71 us  [the longest x3 6.77 us: fold_call(): pl.pallas_call(functools.partial(fold, stage=stage), out_shape=out_shape,...]
    all_to_all x5 -> x3, starting transfers between devices: 29.1 us -> 22.7 us  [exchange(): return lax.all_to_all(x, axis, 0, 0, tiled=True)]
    convert_element_type x3 -> x0, local copies, waits for them, and re-layouts: 3.26 us -> none  [halve(): other = swap(pick(x, 1 - me, dim).astype(bf16), axis)]
  transfers between devices with their start and end apart: 12 -> 10, of which waited for: 9 -> 7; matrix products, arithmetic and copies ran while one was open for 9% -> 0% of each run, Pallas kernels for 8% -> 13%
where the time goes in v7:
time: 137 us
  starting transfers between devices  53.3 us (39%)
  waiting for transfers between devices  27.4 us (20%)
  blocking collectives  24.5 us (18%)
  Pallas kernels  19.7 us (14%)
  local copies, waits for them, and re-layouts  6.13 us (4%)
  other arithmetic  4.51 us (3%)
    all_to_all x1, blocking collectives, exchange(): return lax.all_to_all(x, axis, 0, 0, tiled=True)  24.5 us
    all_to_all x3, starting transfers between devices, exchange(): return lax.all_to_all(x, axis, 0, 0, tiled=True)  22.7 us
    ppermute x5, starting transfers between devices, swap(): return lax.ppermute(x, axis, [(0, 1), (1, 0)])  22.6 us
    ppermute x5, waiting for transfers between devices, swap(): return lax.ppermute(x, axis, [(0, 1), (1, 0)])  17.3 us
    ppermute x1, waiting for transfers between devices, on_device(): lax.ppermute(right, across, [(i, (i + 1 if i % 2 else i - 1) % 8) for i i...  8.02 us
    pallas_call x3, Pallas kernels, fold_call(): pl.pallas_call(functools.partial(fold, stage=stage), out_shape=out_shape,...  6.77 us
    unnamed x24, local copies, waits for them, and re-layouts  5.26 us
    ppermute x1, starting transfers between devices, on_device(): lax.ppermute(right, across, [(i, (i + 1 if i % 2 else i - 1) % 8) for i i...  4.87 us
  transfers between devices with their start and end apart: 10, of which 7 were waited for; matrix products, arithmetic and copies ran while one was open for 0% of the time, Pallas kernels for 13%

profile of v7, /device:TPU:1, one launch (start us, length us, event | category | flops | bytes accessed | tf_op | source)
XLA Modules:
  0.0 136.6 jit_solution(13196508227248553669)
XLA Ops:
  4.2 8.7 %collective-permute-start = (f32[256,512]{1,0:T(8,128)}, f32[256,512]{1,0:T(8,128)S(1)}, u32[]{:S(2)}, u32[]{:S(2)}) collective-permute-start(f32[256,512]{1,0:T(8,128)} %dynamic-slice_bitcast_fusion), channel_id=1, source_target_pairs={{0,16},{16,0},{1,17},{17,1},{2,18},{18,2},{3,19},{19,3},{4,20},{20... | collective-permute-start | bytes 1572872 | tf_op jit(solution)/shard_map/ppermute | solution.py:25
  12.9 1.7 %collective-permute-done = f32[256,512]{1,0:T(8,128)S(1)} collective-permute-done((f32[256,512]{1,0:T(8,128)}, f32[256,512]{1,0:T(8,128)S(1)}, u32[]{:S(2)}, u32[]{:S(2)}) %collective-permute-start) | collective-permute-done | bytes 524320 | tf_op jit(solution)/shard_map/ppermute | solution.py:25
  15.9 24.5 %all_to_all.20.first_ref = bf16[16,32,512]{2,1,0:T(8,128)(2,1)S(1)} all-to-all(bf16[16,32,512]{2,1,0:T(8,128)(2,1)S(1)} %pad_maximum_fusion), channel_id=1, replica_groups=mesh['z'=8,'xh'=2,'core'=2,'y2'=2,'y1'=2,'y0'=2,'xl'=2] {'z','xh'}, dimensions={0} | all-to-all | bytes 1048576 | tf_op jit(solution)/shard_map/all_to_all | solution.py:29
  40.4 1.9 %shard_map.93 = f32[32,16,128]{2,1,0:T(8,128)} custom-call(bf16[16,32,512]{2,1,0:T(8,128)(2,1)S(1)} %all_to_all.20.first_ref, f32[32,512]{1,0:T(8,128)S(1)} %bitcast.28), custom_call_target="tpu_custom_call" | custom-call | flops 40000000 | bytes 400000 | tf_op jit(solution)/shard_map/pallas_call | solution.py:309
  42.3 6.2 %all-to-all-start.1 = ((f32[32,16,128]{2,1,0:T(8,128)}), f32[32,16,128]{2,1,0:T(8,128)S(1)}, u32[]{:S(2)}, u32[]{:S(2)}) async-start(f32[32,16,128]{2,1,0:T(8,128)} %shard_map.93), calls=%async_computation.1 | async-start | bytes 524288 | tf_op jit(solution)/shard_map/all_to_all | solution.py:29
  48.6 2.2 %collective-permute-start.1 = (bf16[16,16,512]{2,1,0:T(8,128)(2,1)S(1)}, bf16[16,16,512]{2,1,0:T(8,128)(2,1)S(1)}, u32[]{:S(2)}, u32[]{:S(2)}) collective-permute-start(bf16[16,16,512]{2,1,0:T(8,128)(2,1)S(1)} %slice.4), channel_id=1, source_target_pairs={{0,16},{16,0},{1,17},{17,1},{2,18},{18,2},{3,19},{19,3},{4,20},{20... | collective-permute-start | bytes 786440 | tf_op jit(solution)/shard_map/ppermute | solution.py:25
  52.1 1.9 %shard_map.97 = (bf16[8,128,256]{2,1,0:T(8,128)(2,1)}, bf16[8,128,256]{2,1,0:T(8,128)(2,1)}, f32[16,128,512]{2,1,0:T(8,128)S(1)}, bf16[512,512]{1,0:T(8,128)(2,1)S(1)}) custom-call(bf16[2048,512]{1,0:T(8,128)(2,1)S(1)} %bitcast.22, bf16[512,512]{1,0:T(8,128)(2,1)S(1)} %copy-done.2, bf16[16,32,512]{2,1,0:T(8,128)(2,1)S(1)} %all_to_all.20.first_ref, ...), custom_call_target="tpu_custom_call" | custom-call | flops 1073741824 | bytes 10737418 | tf_op jit(solution)/shard_map/pallas_call | solution.py:325
  54.0 1.9 %copy-done = f32[16,128,512]{2,1,0:T(8,128)} copy-done((f32[16,128,512]{2,1,0:T(8,128)}, f32[16,128,512]{2,1,0:T(8,128)S(1)}, u32[]{:S(2)}) %copy-start) | copy-done | bytes 4194328
  56.8 3.2 %collective-permute-start.2 = (bf16[8,128,256]{2,1,0:T(8,128)(2,1)}, bf16[8,128,256]{2,1,0:T(8,128)(2,1)}, u32[]{:S(2)}, u32[]{:S(2)}) collective-permute-start(bf16[8,128,256]{2,1,0:T(8,128)(2,1)} %get-tuple-element.29), channel_id=1, source_target_pairs={{0,2},{2,0},{4,6},{6,4},{8,10},{10,8},{12,14},{14,12},{1,3},{3,1},... | collective-permute-start | bytes 1572872 | tf_op jit(solution)/shard_map/ppermute | solution.py:339
  60.0 4.9 %collective-permute-start.3 = (bf16[8,128,256]{2,1,0:T(8,128)(2,1)}, bf16[8,128,256]{2,1,0:T(8,128)(2,1)}, u32[]{:S(2)}, u32[]{:S(2)}) collective-permute-start(bf16[8,128,256]{2,1,0:T(8,128)(2,1)} %get-tuple-element.30), channel_id=1, source_target_pairs={{0,14},{2,4},{4,2},{6,8},{8,6},{10,12},{12,10},{14,0},{1,15},{3,5}... | collective-permute-start | bytes 1572872 | tf_op jit(solution)/shard_map/ppermute | solution.py:340
  64.9 2.1 %shard_map.94 = f32[16,48,128]{2,1,0:T(8,128)} custom-call(f32[32,16,128]{2,1,0:T(8,128)S(1)} %all-to-all-done.1.second_ref, bf16[2048,512]{1,0:T(8,128)(2,1)S(1)} %bitcast.23), custom_call_target="tpu_custom_call" | custom-call | flops 500000000 | bytes 5000000 | tf_op jit(solution)/shard_map/pallas_call | solution.py:349
  66.9 3.6 %all-to-all-start.2 = ((f32[16,48,128]{2,1,0:T(8,128)}), f32[16,48,128]{2,1,0:T(8,128)S(1)}, u32[]{:S(2)}, u32[]{:S(2)}) async-start(f32[16,48,128]{2,1,0:T(8,128)} %shard_map.94), calls=%async_computation.2 | async-start | bytes 786432 | tf_op jit(solution)/shard_map/all_to_all | solution.py:29
  70.5 1.7 %collective-permute-done.2.refs_1_ = bf16[8,128,256]{2,1,0:T(8,128)(2,1)} collective-permute-done((bf16[8,128,256]{2,1,0:T(8,128)(2,1)}, bf16[8,128,256]{2,1,0:T(8,128)(2,1)}, u32[]{:S(2)}, u32[]{:S(2)}) %collective-permute-start.2) | collective-permute-done | bytes 524320 | tf_op jit(solution)/shard_map/ppermute | solution.py:339
  72.2 8.0 %collective-permute-done.3.refs_2_ = bf16[8,128,256]{2,1,0:T(8,128)(2,1)} collective-permute-done((bf16[8,128,256]{2,1,0:T(8,128)(2,1)}, bf16[8,128,256]{2,1,0:T(8,128)(2,1)}, u32[]{:S(2)}, u32[]{:S(2)}) %collective-permute-start.3) | collective-permute-done | bytes 524320 | tf_op jit(solution)/shard_map/ppermute | solution.py:340
  80.2 2.1 %shard_map.99 = bf16[4,128,512]{2,1,0:T(8,128)(2,1)} custom-call(f32[16,128,512]{2,1,0:T(8,128)} %copy-done, bf16[8,128,256]{2,1,0:T(8,128)(2,1)} %collective-permute-done.2.refs_1_, bf16[8,128,256]{2,1,0:T(8,128)(2,1)} %collective-permute-done.3.refs_2_), custom_call_target="tpu_custom_call" | custom-call | flops 262144 | bytes 2097152 | tf_op jit(solution)/shard_map/pallas_call | solution.py:181
  82.4 2.2 %collective-permute-start.4 = (bf16[4,128,512]{2,1,0:T(8,128)(2,1)}, bf16[4,128,512]{2,1,0:T(8,128)(2,1)S(1)}, u32[]{:S(2)}, u32[]{:S(2)}) collective-permute-start(bf16[4,128,512]{2,1,0:T(8,128)(2,1)} %shard_map.99), channel_id=1, source_target_pairs={{0,1},{1,0},{2,3},{3,2},{4,5},{5,4},{6,7},{7,6},{8,9},{9,8},{10,11... | collective-permute-start | bytes 1572872 | tf_op jit(solution)/shard_map/ppermute | solution.py:25
  85.7 12.9 %all-to-all-start.3 = ((f32[32,16,128]{2,1,0:T(8,128)}), f32[32,16,128]{2,1,0:T(8,128)S(1)}, u32[]{:S(2)}, u32[]{:S(2)}) async-start(f32[32,16,128]{2,1,0:T(8,128)} %get-tuple-element.19), calls=%async_computation.3 | async-start | bytes 524288 | tf_op jit(solution)/shard_map/all_to_all | solution.py:29
  99.4 2.0 %shard_map.100 = bf16[2,128,512]{2,1,0:T(8,128)(2,1)} custom-call(f32[16,128,512]{2,1,0:T(8,128)} %copy-done, bf16[8,128,256]{2,1,0:T(8,128)(2,1)} %collective-permute-done.2.refs_1_, bf16[8,128,256]{2,1,0:T(8,128)(2,1)} %collective-permute-done.3.refs_2_, bf16[4,128,512]{2,1,0:T(8,128)(2,1)} %copy-done.10), custom_call_target="tpu_custom_call" | custom-call | flops 131072 | bytes 1048576 | tf_op jit(solution)/shard_map/pallas_call | solution.py:181
  101.5 2.9 %collective-permute-start.5 = (bf16[2,128,512]{2,1,0:T(8,128)(2,1)}, bf16[2,128,512]{2,1,0:T(8,128)(2,1)S(1)}, u32[]{:S(2)}, u32[]{:S(2)}) collective-permute-start(bf16[2,128,512]{2,1,0:T(8,128)(2,1)} %shard_map.100), channel_id=1, source_target_pairs={{0,4},{4,0},{1,5},{5,1},{2,6},{6,2},{3,7},{7,3},{8,12},{12,8},{9,1... | collective-permute-start | bytes 786440 | tf_op jit(solution)/shard_map/ppermute | solution.py:25
  104.4 13.7 %collective-permute-done.5.refs_4_ = bf16[2,128,512]{2,1,0:T(8,128)(2,1)S(1)} collective-permute-done((bf16[2,128,512]{2,1,0:T(8,128)(2,1)}, bf16[2,128,512]{2,1,0:T(8,128)(2,1)S(1)}, u32[]{:S(2)}, u32[]{:S(2)}) %collective-permute-start.5) | collective-permute-done | bytes 262176 | tf_op jit(solution)/shard_map/ppermute | solution.py:25
  118.9 2.6 %shard_map.101 = (bf16[1,128,512]{2,1,0:T(8,128)(2,1)}, f32[128,512]{1,0:T(8,128)}) custom-call(f32[16,128,512]{2,1,0:T(8,128)} %copy-done, bf16[8,128,256]{2,1,0:T(8,128)(2,1)} %collective-permute-done.2.refs_1_, bf16[8,128,256]{2,1,0:T(8,128)(2,1)} %collective-permute-done.3.refs_2_, bf16[4,128,512]{2,1,0:T(8,128)(2,1)} %copy-done.10, ...), custom_call_target="tpu_custom_call" | custom-call | flops 65536 | bytes 524288 | tf_op jit(solution)/shard_map/pallas_call | solution.py:181
  121.5 6.5 %collective-permute-start.6 = (bf16[1,128,512]{2,1,0:T(8,128)(2,1)}, bf16[1,128,512]{2,1,0:T(8,128)(2,1)S(1)}, u32[]{:S(2)}, u32[]{:S(2)}) collective-permute-start(bf16[1,128,512]{2,1,0:T(8,128)(2,1)} %get-tuple-element.32), channel_id=1, source_target_pairs={{0,8},{8,0},{1,9},{9,1},{2,10},{10,2},{3,11},{11,3},{4,12},{12,4},... | collective-permute-start | bytes 393224 | tf_op jit(solution)/shard_map/ppermute | solution.py:25
  128.0 3.2 %shard_map.96 = (f32[512,128]{1,0:T(8,128)S(1)}, f32[128,128]{1,0:T(8,128)S(1)}, f32[128,128]{1,0:T(8,128)S(1)}) custom-call(f32[48,128]{1,0:T(8,128)S(1)} %get-tuple-element.20.total_ref, f32[32,16,128]{2,1,0:T(8,128)S(1)} %all-to-all-done.1.second_ref), custom_call_target="tpu_custom_call" | custom-call | flops 100000000 | bytes 1000000 | tf_op jit(solution)/shard_map/pallas_call | solution.py:369
  131.3 3.1 %shard_map.98 = (bf16[512,512]{1,0:T(8,128)(2,1)}, bf16[16,512]{1,0:T(8,128)(2,1)}, bf16[512,512]{1,0:T(8,128)(2,1)}, f32[128,512]{1,0:T(8,128)S(1)}) custom-call(f32[32,16,128]{2,1,0:T(8,128)S(1)} %all-to-all-done.3.fourth_ref, f32[128,128]{1,0:T(8,128)S(1)} %get-tuple-element.21.inverse_ref, f32[512,128]{1,0:T(8,128)S(1)} %get-tuple-element.22.basis_ref, ...), custom_call_target="tpu_custom_call" | custom-call | flops 400000000 | bytes 4000000 | tf_op jit(solution)/shard_map/pallas_call | solution.py:380
  (37 shorter events, 11.6 us)
Async XLA Ops:
  0.6 15.2 %copy-start.7 = (bf16[512,16]{0,1:T(8,128)(2,1)S(1)}, bf16[512,16]{0,1:T(8,128)(2,1)}, u32[]{:S(2)}) copy-start(bf16[512,16]{0,1:T(8,128)(2,1)} %param.8) | copy-start | bytes 49156
  0.6 39.8 %copy-start.8 = (f32[512,32]{0,1:T(8,128)S(1)}, f32[512,32]{0,1:T(8,128)}, u32[]{:S(2)}) copy-start(f32[512,32]{0,1:T(8,128)} %param.10) | copy-start | bytes 196612
  0.7 51.4 %copy-start.1 = (bf16[1,2048,512]{2,1,0:T(8,128)(2,1)S(1)}, bf16[1,2048,512]{2,1,0:T(8,128)(2,1)}, u32[]{:S(2)}) copy-start(bf16[1,2048,512]{2,1,0:T(8,128)(2,1)} %param.11) | copy-start | bytes 6291460
  0.7 51.4 %copy-start.2 = (bf16[512,512]{1,0:T(8,128)(2,1)S(1)}, bf16[512,512]{1,0:T(8,128)(2,1)}, u32[]{:S(2)}) copy-start(bf16[512,512]{1,0:T(8,128)(2,1)} %base_ref.3) | copy-start | bytes 1572868
  2.4 1.0 copy-start.9
  4.2 10.5 %collective-permute-start = (f32[256,512]{1,0:T(8,128)}, f32[256,512]{1,0:T(8,128)S(1)}, u32[]{:S(2)}, u32[]{:S(2)}) collective-permute-start(f32[256,512]{1,0:T(8,128)} %dynamic-slice_bitcast_fusion), channel_id=1, source_target_pairs={{0,16},{16,0},{1,17},{17,1},{2,18},{18,2},{3,19},{19,3},{4,20},{20... | collective-permute-start | bytes 1572872 | tf_op jit(solution)/shard_map/ppermute | solution.py:25
  42.3 22.5 %all-to-all-start.1 = ((f32[32,16,128]{2,1,0:T(8,128)}), f32[32,16,128]{2,1,0:T(8,128)S(1)}, u32[]{:S(2)}, u32[]{:S(2)}) async-start(f32[32,16,128]{2,1,0:T(8,128)} %shard_map.93), calls=%async_computation.1 | async-start | bytes 524288 | tf_op jit(solution)/shard_map/all_to_all | solution.py:29
  48.6 3.4 %collective-permute-start.1 = (bf16[16,16,512]{2,1,0:T(8,128)(2,1)S(1)}, bf16[16,16,512]{2,1,0:T(8,128)(2,1)S(1)}, u32[]{:S(2)}, u32[]{:S(2)}) collective-permute-start(bf16[16,16,512]{2,1,0:T(8,128)(2,1)S(1)} %slice.4), channel_id=1, source_target_pairs={{0,16},{16,0},{1,17},{17,1},{2,18},{18,2},{3,19},{19,3},{4,20},{20... | collective-permute-start | bytes 786440 | tf_op jit(solution)/shard_map/ppermute | solution.py:25
  54.0 2.0 %copy-start = (f32[16,128,512]{2,1,0:T(8,128)}, f32[16,128,512]{2,1,0:T(8,128)S(1)}, u32[]{:S(2)}) copy-start(f32[16,128,512]{2,1,0:T(8,128)S(1)} %get-tuple-element.28.refs_0_) | copy-start | bytes 12582916
  56.0 0.8 copy-start.5
  56.8 15.4 %collective-permute-start.2 = (bf16[8,128,256]{2,1,0:T(8,128)(2,1)}, bf16[8,128,256]{2,1,0:T(8,128)(2,1)}, u32[]{:S(2)}, u32[]{:S(2)}) collective-permute-start(bf16[8,128,256]{2,1,0:T(8,128)(2,1)} %get-tuple-element.29), channel_id=1, source_target_pairs={{0,2},{2,0},{4,6},{6,4},{8,10},{10,8},{12,14},{14,12},{1,3},{3,1},... | collective-permute-start | bytes 1572872 | tf_op jit(solution)/shard_map/ppermute | solution.py:339
  60.0 20.3 %collective-permute-start.3 = (bf16[8,128,256]{2,1,0:T(8,128)(2,1)}, bf16[8,128,256]{2,1,0:T(8,128)(2,1)}, u32[]{:S(2)}, u32[]{:S(2)}) collective-permute-start(bf16[8,128,256]{2,1,0:T(8,128)(2,1)} %get-tuple-element.30), channel_id=1, source_target_pairs={{0,14},{2,4},{4,2},{6,8},{8,6},{10,12},{12,10},{14,0},{1,15},{3,5}... | collective-permute-start | bytes 1572872 | tf_op jit(solution)/shard_map/ppermute | solution.py:340
  66.9 18.0 %all-to-all-start.2 = ((f32[16,48,128]{2,1,0:T(8,128)}), f32[16,48,128]{2,1,0:T(8,128)S(1)}, u32[]{:S(2)}, u32[]{:S(2)}) async-start(f32[16,48,128]{2,1,0:T(8,128)} %shard_map.94), calls=%async_computation.2 | async-start | bytes 786432 | tf_op jit(solution)/shard_map/all_to_all | solution.py:29
  82.4 16.2 %collective-permute-start.4 = (bf16[4,128,512]{2,1,0:T(8,128)(2,1)}, bf16[4,128,512]{2,1,0:T(8,128)(2,1)S(1)}, u32[]{:S(2)}, u32[]{:S(2)}) collective-permute-start(bf16[4,128,512]{2,1,0:T(8,128)(2,1)} %shard_map.99), channel_id=1, source_target_pairs={{0,1},{1,0},{2,3},{3,2},{4,5},{5,4},{6,7},{7,6},{8,9},{9,8},{10,11... | collective-permute-start | bytes 1572872 | tf_op jit(solution)/shard_map/ppermute | solution.py:25
  85.7 45.5 %all-to-all-start.3 = ((f32[32,16,128]{2,1,0:T(8,128)}), f32[32,16,128]{2,1,0:T(8,128)S(1)}, u32[]{:S(2)}, u32[]{:S(2)}) async-start(f32[32,16,128]{2,1,0:T(8,128)} %get-tuple-element.19), calls=%async_computation.3 | async-start | bytes 524288 | tf_op jit(solution)/shard_map/all_to_all | solution.py:29
  98.6 0.8 copy-start.10
  101.5 29.8 %copy-start.3 = (bf16[1,512,512]{2,1,0:T(8,128)(2,1)S(1)}, bf16[1,512,512]{2,1,0:T(8,128)(2,1)}, u32[]{:S(2)}) copy-start(bf16[1,512,512]{2,1,0:T(8,128)(2,1)} %param.9) | copy-start | bytes 1572868
  101.5 29.8 %copy-start.4 = (bf16[1,512,512]{2,1,0:T(8,128)(2,1)S(1)}, bf16[1,512,512]{2,1,0:T(8,128)(2,1)}, u32[]{:S(2)}) copy-start(bf16[1,512,512]{2,1,0:T(8,128)(2,1)} %param.6) | copy-start | bytes 1572868
  101.5 29.8 %copy-start.6 = (bf16[512,512]{1,0:T(8,128)(2,1)S(1)}, bf16[512,512]{1,0:T(8,128)(2,1)}, u32[]{:S(2)}) copy-start(bf16[512,512]{1,0:T(8,128)(2,1)} %copy-done.5) | copy-start | bytes 1572868
  101.5 16.7 %collective-permute-start.5 = (bf16[2,128,512]{2,1,0:T(8,128)(2,1)}, bf16[2,128,512]{2,1,0:T(8,128)(2,1)S(1)}, u32[]{:S(2)}, u32[]{:S(2)}) collective-permute-start(bf16[2,128,512]{2,1,0:T(8,128)(2,1)} %shard_map.100), channel_id=1, source_target_pairs={{0,4},{4,0},{1,5},{5,1},{2,6},{6,2},{3,7},{7,3},{8,12},{12,8},{9,1... | collective-permute-start | bytes 786440 | tf_op jit(solution)/shard_map/ppermute | solution.py:25
  118.2 0.7 copy-start.11
  121.5 13.4 %collective-permute-start.6 = (bf16[1,128,512]{2,1,0:T(8,128)(2,1)}, bf16[1,128,512]{2,1,0:T(8,128)(2,1)S(1)}, u32[]{:S(2)}, u32[]{:S(2)}) collective-permute-start(bf16[1,128,512]{2,1,0:T(8,128)(2,1)} %get-tuple-element.32), channel_id=1, source_target_pairs={{0,8},{8,0},{1,9},{9,1},{2,10},{10,2},{3,11},{11,3},{4,12},{12,4},... | collective-permute-start | bytes 393224 | tf_op jit(solution)/shard_map/ppermute | solution.py:25

commit v8 on v5

--- a/solution.py
+++ b/solution.py
@@ -29,6 +29,10 @@
     return lax.all_to_all(x, axis, 0, 0, tiled=True)
 
 
+def copy_for_each(x, axis):
+    return exchange(jnp.broadcast_to(x, (lax.axis_size(axis), *x.shape)), axis)
+
+
 def dot(a, b, dims, precision=None):
     return lax.dot_general(
         a, b, (dims, ((), ())), precision=precision, preferred_element_type=f32
@@ -40,7 +44,7 @@
 
 
 def moments(first_ref, q_ref, hbm_ref, out_ref, *, own, rank, replicas):
-    mean = jnp.sum(first_ref[:, :own].astype(f32), axis=0) * (1.0 / replicas)
+    mean = jnp.sum(first_ref[...].astype(f32), axis=0) * (1.0 / replicas)
     q = jnp.concatenate([q_ref[...]] * 4, axis=0)
     p = dot(mean, q, ((1,), (1,)), highest)
     group = lane_group(p.shape, rank)
@@ -96,11 +100,11 @@
 
 
 def key_products(
-    tokens_ref, base_ref, first_ref, its_ref,
+    tokens_ref, base_ref, my_ref, its_ref,
     left_ref, right_ref, kept_ref, full_ref, sent, keep, sems,
 ):
     y0, core = lax.axis_index("y0"), lax.axis_index("core")
-    mine = first_ref[:, its_ref.shape[1] :].astype(f32)
+    mine = my_ref[...].astype(f32)
     other = its_ref[...].astype(f32)
     pairs = jnp.concatenate(
         [
@@ -275,7 +279,7 @@
         cost_estimate=pl.CostEstimate(
             flops=flops, bytes_accessed=flops // 100, transcendentals=0
         ),
-        compiler_params=pltpu.CompilerParams(vmem_limit_bytes=mib << 20),
+        compiler_params=pltpu.CompilerParams(vmem_limit_bytes=(mib << 20) or None),
     )
 
 
@@ -289,6 +293,7 @@
     block = own_tokens.shape[0] // shards
     shape = jax.ShapeDtypeStruct
 
+    my_momentum = copy_for_each(momentum.T, chips)
     half = shape((rows // 2, kv), f32)
     given = pltpu.VMEM((rows, kv), bf16)
     send, pair = in_vmem(
@@ -302,16 +307,8 @@
     )(local_weights[0], outer_base, error_feedback[0])
     send = swap(send, "core")
     pair = (pair + send).astype(bf16)
-    first = exchange(
-        jnp.concatenate(
-            [
-                pair.reshape(replicas // 2, own, kv),
-                jnp.broadcast_to(momentum.T, (replicas // 2, cols, rows)),
-            ],
-            axis=1,
-        ),
-        chips,
-    )
+    pair, my_momentum = lax.optimization_barrier((pair, my_momentum))
+    first = exchange(pair.reshape(replicas // 2, own, kv), chips)
     lanes = 4 * rank
     (second,) = in_vmem(
         functools.partial(moments, own=own, rank=rank, replicas=replicas),
@@ -324,7 +321,7 @@
     )(first, q_start.T)
     second = exchange(second, peers)
 
-    its_momentum = swap(first[:, own:], "core")
+    its_momentum = swap(my_momentum, "core")
 
     part = (shards // 2, block, kv // 2)
     whole = (*part[:2], kv)
@@ -332,7 +329,7 @@
         key_products,
         (shape(part, bf16), shape(part, bf16), shape(whole, f32), shape((rows, kv), bf16)),
         4,
-        16,
+        0,
         2 * tokens.shape[1] * rows * kv,
         (
             pltpu.VMEM(whole, bf16),
@@ -340,7 +337,7 @@
             pltpu.SemaphoreType.DMA((3,)),
         ),
         3,
-    )(own_tokens, outer_base, first, its_momentum)
+    )(own_tokens, outer_base, my_momentum, its_momentum)
     across = ("y2", "y1", "y0")
     left = lax.ppermute(left, across, [(i, i ^ 1) for i in range(8)])
     right = lax.ppermute(

time: 135 us -> 149 us (1.10)
  waiting for transfers between devices: 26.7 us -> 38.1 us
  blocking collectives: 24.7 us -> 15.2 us
  starting transfers between devices: 53.9 us -> 61.1 us
  Pallas kernels: 20.5 us -> 24 us
    all_to_all x3 -> x4, waiting for transfers between devices: 0.01 us -> 12.8 us  [exchange(): return lax.all_to_all(x, axis, 0, 0, tiled=True)]
    all_to_all x1, blocking collectives: 24.7 us -> 15.2 us  [exchange(): return lax.all_to_all(x, axis, 0, 0, tiled=True)]
    all_to_all x3 -> x4, starting transfers between devices: 23.1 us -> 30.4 us  [exchange(): return lax.all_to_all(x, axis, 0, 0, tiled=True)]
    pallas_call x1, Pallas kernels: 1.94 us -> 5.49 us  [on_device(): in_vmem(key_products, (shape(part, bf16), shape(part, bf16), shape(whole,...]
  transfers between devices with their start and end apart: 10 -> 11, of which waited for: 6 -> 6; matrix products, arithmetic and copies ran while one was open for 0% -> 1% of each run, Pallas kernels for 14% -> 15%
where the time goes in v8:
time: 149 us; the launch traced here: 148 us
  starting transfers between devices  61.1 us (41%)
  waiting for transfers between devices  38.1 us (26%)
  Pallas kernels  24 us (16%)
  blocking collectives  15.2 us (10%)
  local copies, waits for them, and re-layouts  6.8 us (5%)
  other arithmetic  1.71 us (1%)
    all_to_all x4, starting transfers between devices, exchange(): return lax.all_to_all(x, axis, 0, 0, tiled=True)  30.4 us
    ppermute x5, starting transfers between devices, swap(): return lax.ppermute(x, axis, [(0, 1), (1, 0)])  22.7 us
    ppermute x5, waiting for transfers between devices, swap(): return lax.ppermute(x, axis, [(0, 1), (1, 0)])  15.6 us
    all_to_all x1, blocking collectives, exchange(): return lax.all_to_all(x, axis, 0, 0, tiled=True)  15.2 us
    all_to_all x4, waiting for transfers between devices, exchange(): return lax.all_to_all(x, axis, 0, 0, tiled=True)  12.8 us
    ppermute x1, waiting for transfers between devices, on_device(): lax.ppermute(right, across, [(i, (i + 1 if i % 2 else i - 1) % 8) for i i...  8.12 us
    pallas_call x3, Pallas kernels, fold_call(): pl.pallas_call(functools.partial(fold, axis=axis, n=n), out_shape=(shape(...  7.2 us
    pallas_call x1, Pallas kernels, on_device(): in_vmem(key_products, (shape(part, bf16), shape(part, bf16), shape(whole,...  5.49 us
  transfers between devices with their start and end apart: 11, of which 6 were waited for; matrix products, arithmetic and copies ran while one was open for 1% of the time, Pallas kernels for 15%

profile of v8, /device:TPU:1, one launch (start us, length us, event | category | flops | bytes accessed | tf_op | source)
XLA Modules:
  0.0 147.8 jit_solution(3248840504418131898)
XLA Ops:
  4.1 8.7 %collective-permute-start = (f32[256,512]{1,0:T(8,128)S(1)}, f32[256,512]{1,0:T(8,128)S(1)}, u32[]{:S(2)}, u32[]{:S(2)}) collective-permute-start(f32[256,512]{1,0:T(8,128)S(1)} %get-tuple-element.28), channel_id=1, source_target_pairs={{0,16},{16,0},{1,17},{17,1},{2,18},{18,2},{3,19},{19,3},{4,20},{20... | collective-permute-start | bytes 1572872 | tf_op jit(solution)/shard_map/ppermute | solution.py:25
  14.3 7.3 %all-to-all-start = ((bf16[16,16,512]{2,1,0:T(8,128)(2,1)}), bf16[16,16,512]{2,1,0:T(8,128)(2,1)S(1)}, u32[]{:S(2)}, u32[]{:S(2)}) async-start(bf16[16,16,512]{2,1,0:T(8,128)(2,1)} %broadcast_in_dim.9), calls=%async_computation | async-start | bytes 524288 | tf_op jit(solution)/shard_map/all_to_all | solution.py:29
  21.7 12.8 %all-to-all-done.my_ref = bf16[16,16,512]{2,1,0:T(8,128)(2,1)S(1)} async-done(((bf16[16,16,512]{2,1,0:T(8,128)(2,1)}), bf16[16,16,512]{2,1,0:T(8,128)(2,1)S(1)}, u32[]{:S(2)}, u32[]{:S(2)}) %all-to-all-start) | async-done | bytes 262176 | tf_op jit(solution)/shard_map/all_to_all | solution.py:29
  34.4 15.2 %all_to_all.25.first_ref = bf16[16,16,512]{2,1,0:T(8,128)(2,1)S(1)} all-to-all(bf16[16,16,512]{2,1,0:T(8,128)(2,1)S(1)} %bitcast.33), channel_id=1, replica_groups=mesh['z'=8,'xh'=2,'core'=2,'y2'=2,'y1'=2,'y0'=2,'xl'=2] {'z','xh'}, dimensions={0} | all-to-all | bytes 524288 | tf_op jit(solution)/shard_map/all_to_all | solution.py:29
  49.6 1.9 %shard_map.94 = f32[32,16,128]{2,1,0:T(8,128)} custom-call(bf16[16,16,512]{2,1,0:T(8,128)(2,1)S(1)} %all_to_all.25.first_ref, f32[32,512]{1,0:T(8,128)S(1)} %bitcast.31), custom_call_target="tpu_custom_call" | custom-call | flops 40000000 | bytes 400000 | tf_op jit(solution)/shard_map/pallas_call | solution.py:313
  51.5 6.2 %all-to-all-start.2 = ((f32[32,16,128]{2,1,0:T(8,128)}), f32[32,16,128]{2,1,0:T(8,128)S(1)}, u32[]{:S(2)}, u32[]{:S(2)}) async-start(f32[32,16,128]{2,1,0:T(8,128)} %shard_map.94), calls=%async_computation.2 | async-start | bytes 524288 | tf_op jit(solution)/shard_map/all_to_all | solution.py:29
  57.7 2.3 %collective-permute-start.1 = (bf16[16,16,512]{2,1,0:T(8,128)(2,1)S(1)}, bf16[16,16,512]{2,1,0:T(8,128)(2,1)S(1)}, u32[]{:S(2)}, u32[]{:S(2)}) collective-permute-start(bf16[16,16,512]{2,1,0:T(8,128)(2,1)S(1)} %all-to-all-done.my_ref), channel_id=1, source_target_pairs={{0,16},{16,0},{1,17},{17,1},{2,18},{18,2},{3,19},{19,3},{4,20},{20... | collective-permute-start | bytes 786440 | tf_op jit(solution)/shard_map/ppermute | solution.py:25
  62.0 5.5 %shard_map.98 = (bf16[8,128,256]{2,1,0:T(8,128)(2,1)}, bf16[8,128,256]{2,1,0:T(8,128)(2,1)}, f32[8,128,512]{2,1,0:T(8,128)}, bf16[512,512]{1,0:T(8,128)(2,1)}) custom-call(bf16[2048,512]{1,0:T(8,128)(2,1)} %bitcast.23, bf16[512,512]{1,0:T(8,128)(2,1)} %base_ref.3, bf16[16,16,512]{2,1,0:T(8,128)(2,1)} %copy-done.14, bf16[16,16,512]{2,1,0:T(8,128)(2,1)} %copy-done.15), custom_call_target="tpu_custom_call" | custom-call | flops 1073741824 | bytes 10737418 | tf_op jit(solution)/shard_map/pallas_call | solution.py:328
  67.5 3.2 %collective-permute-start.2 = (bf16[8,128,256]{2,1,0:T(8,128)(2,1)}, bf16[8,128,256]{2,1,0:T(8,128)(2,1)S(1)}, u32[]{:S(2)}, u32[]{:S(2)}) collective-permute-start(bf16[8,128,256]{2,1,0:T(8,128)(2,1)} %get-tuple-element.40), channel_id=1, source_target_pairs={{0,2},{2,0},{4,6},{6,4},{8,10},{10,8},{12,14},{14,12},{1,3},{3,1},... | collective-permute-start | bytes 1572872 | tf_op jit(solution)/shard_map/ppermute | solution.py:342
  70.7 4.9 %collective-permute-start.3 = (bf16[8,128,256]{2,1,0:T(8,128)(2,1)}, bf16[8,128,256]{2,1,0:T(8,128)(2,1)S(1)}, u32[]{:S(2)}, u32[]{:S(2)}) collective-permute-start(bf16[8,128,256]{2,1,0:T(8,128)(2,1)} %get-tuple-element.41), channel_id=1, source_target_pairs={{0,14},{2,4},{4,2},{6,8},{8,6},{10,12},{12,10},{14,0},{1,15},{3,5}... | collective-permute-start | bytes 1572872 | tf_op jit(solution)/shard_map/ppermute | solution.py:343
  75.6 2.1 %shard_map.95 = f32[16,48,128]{2,1,0:T(8,128)} custom-call(f32[32,16,128]{2,1,0:T(8,128)S(1)} %all-to-all-done.2.second_ref, bf16[2048,512]{1,0:T(8,128)(2,1)S(1)} %bitcast.24), custom_call_target="tpu_custom_call" | custom-call | flops 500000000 | bytes 5000000 | tf_op jit(solution)/shard_map/pallas_call | solution.py:358
  77.7 3.6 %all-to-all-start.3 = ((f32[16,48,128]{2,1,0:T(8,128)}), f32[16,48,128]{2,1,0:T(8,128)S(1)}, u32[]{:S(2)}, u32[]{:S(2)}) async-start(f32[16,48,128]{2,1,0:T(8,128)} %shard_map.95), calls=%async_computation.3 | async-start | bytes 786432 | tf_op jit(solution)/shard_map/all_to_all | solution.py:29
  82.8 8.1 %collective-permute-done.3 = bf16[8,128,256]{2,1,0:T(8,128)(2,1)S(1)} collective-permute-done((bf16[8,128,256]{2,1,0:T(8,128)(2,1)}, bf16[8,128,256]{2,1,0:T(8,128)(2,1)S(1)}, u32[]{:S(2)}, u32[]{:S(2)}) %collective-permute-start.3) | collective-permute-done | bytes 524320 | tf_op jit(solution)/shard_map/ppermute | solution.py:343
  91.8 3.0 %shard_map.100 = (bf16[4,128,512]{2,1,0:T(8,128)(2,1)}, f32[4,128,512]{2,1,0:T(8,128)}) custom-call(bf16[4,2,128,256]{3,2,1,0:T(8,128)(2,1)} %bitcast.36, bf16[4,2,128,256]{3,2,1,0:T(8,128)(2,1)} %bitcast.37, f32[4,2,128,512]{3,2,1,0:T(8,128)} %bitcast.32), custom_call_target="tpu_custom_call" | custom-call | flops 524288 | bytes 3145728 | tf_op jit(solution)/shard_map/pallas_call | solution.py:185
  94.8 2.3 %collective-permute-start.4 = (bf16[4,128,512]{2,1,0:T(8,128)(2,1)}, bf16[4,128,512]{2,1,0:T(8,128)(2,1)}, u32[]{:S(2)}, u32[]{:S(2)}) collective-permute-start(bf16[4,128,512]{2,1,0:T(8,128)(2,1)} %get-tuple-element.43), channel_id=1, source_target_pairs={{0,1},{1,0},{2,3},{3,2},{4,5},{5,4},{6,7},{7,6},{8,9},{9,8},{10,11... | collective-permute-start | bytes 1572872 | tf_op jit(solution)/shard_map/ppermute | solution.py:25
  97.9 13.4 %all-to-all-start.4 = ((f32[32,16,128]{2,1,0:T(8,128)}), f32[32,16,128]{2,1,0:T(8,128)S(1)}, u32[]{:S(2)}, u32[]{:S(2)}) async-start(f32[32,16,128]{2,1,0:T(8,128)} %get-tuple-element.30), calls=%async_computation.4 | async-start | bytes 524288 | tf_op jit(solution)/shard_map/all_to_all | solution.py:29
  111.2 2.3 %shard_map.101 = (bf16[2,128,512]{2,1,0:T(8,128)(2,1)}, f32[2,128,512]{2,1,0:T(8,128)}) custom-call(bf16[2,2,128,512]{3,2,1,0:T(8,128)(2,1)} %bitcast.11.refs_0_, f32[2,2,128,512]{3,2,1,0:T(8,128)} %bitcast.34), custom_call_target="tpu_custom_call" | custom-call | flops 262144 | bytes 1572864 | tf_op jit(solution)/shard_map/pallas_call | solution.py:185
  113.5 2.7 %collective-permute-start.5 = (bf16[2,128,512]{2,1,0:T(8,128)(2,1)}, bf16[2,128,512]{2,1,0:T(8,128)(2,1)S(1)}, u32[]{:S(2)}, u32[]{:S(2)}) collective-permute-start(bf16[2,128,512]{2,1,0:T(8,128)(2,1)} %get-tuple-element.45), channel_id=1, source_target_pairs={{0,4},{4,0},{1,5},{5,1},{2,6},{6,2},{3,7},{7,3},{8,12},{12,8},{9,1... | collective-permute-start | bytes 786440 | tf_op jit(solution)/shard_map/ppermute | solution.py:25
  116.2 13.7 %collective-permute-done.5 = bf16[2,128,512]{2,1,0:T(8,128)(2,1)S(1)} collective-permute-done((bf16[2,128,512]{2,1,0:T(8,128)(2,1)}, bf16[2,128,512]{2,1,0:T(8,128)(2,1)S(1)}, u32[]{:S(2)}, u32[]{:S(2)}) %collective-permute-start.5) | collective-permute-done | bytes 262176 | tf_op jit(solution)/shard_map/ppermute | solution.py:25
  130.6 1.9 %shard_map.102 = (bf16[1,128,512]{2,1,0:T(8,128)(2,1)}, f32[1,128,512]{2,1,0:T(8,128)}) custom-call(bf16[1,2,128,512]{3,2,1,0:T(8,128)(2,1)} %bitcast.38, f32[1,2,128,512]{3,2,1,0:T(8,128)} %bitcast.35), custom_call_target="tpu_custom_call" | custom-call | flops 131072 | bytes 786432 | tf_op jit(solution)/shard_map/pallas_call | solution.py:185
  132.6 6.7 %collective-permute-start.6 = (bf16[1,128,512]{2,1,0:T(8,128)(2,1)}, bf16[1,128,512]{2,1,0:T(8,128)(2,1)}, u32[]{:S(2)}, u32[]{:S(2)}) collective-permute-start(bf16[1,128,512]{2,1,0:T(8,128)(2,1)} %get-tuple-element.48), channel_id=1, source_target_pairs={{0,8},{8,0},{1,9},{9,1},{2,10},{10,2},{3,11},{11,3},{4,12},{12,4},... | collective-permute-start | bytes 393224 | tf_op jit(solution)/shard_map/ppermute | solution.py:25
  139.3 3.2 %shard_map.97 = (f32[512,128]{1,0:T(8,128)S(1)}, f32[128,128]{1,0:T(8,128)S(1)}, f32[128,128]{1,0:T(8,128)S(1)}) custom-call(f32[48,128]{1,0:T(8,128)S(1)} %get-tuple-element.31.total_ref, f32[32,16,128]{2,1,0:T(8,128)S(1)} %all-to-all-done.2.second_ref), custom_call_target="tpu_custom_call" | custom-call | flops 100000000 | bytes 1000000 | tf_op jit(solution)/shard_map/pallas_call | solution.py:378
  142.5 3.1 %shard_map.99 = (bf16[512,512]{1,0:T(8,128)(2,1)}, bf16[16,512]{1,0:T(8,128)(2,1)}, bf16[512,512]{1,0:T(8,128)(2,1)}, f32[128,512]{1,0:T(8,128)S(1)}) custom-call(f32[32,16,128]{2,1,0:T(8,128)S(1)} %all-to-all-done.4.fourth_ref, f32[128,128]{1,0:T(8,128)S(1)} %get-tuple-element.32.inverse_ref, f32[512,128]{1,0:T(8,128)S(1)} %get-tuple-element.33.basis_ref, ...), custom_call_target="tpu_custom_call" | custom-call | flops 400000000 | bytes 4000000 | tf_op jit(solution)/shard_map/pallas_call | solution.py:389
  146.2 1.6 %fusion.1 = bf16[1,128,512]{2,1,0:T(8,128)(2,1)} fusion(f32[128,512]{1,0:T(8,128)S(1)} %get-tuple-element.49, f32[1,128,512]{2,1,0:T(8,128)S(1)} %copy-done.12, bf16[1,128,512]{2,1,0:T(8,128)(2,1)} %collective-permute-done.6), kind=kLoop, calls=%fused_computation.3 | loop fusion | flops 262144 | bytes 786432 | tf_op jit(solution)/shard_map/broadcast_in_dim | solution.py:413
  (44 shorter events, 11.4 us)
Async XLA Ops:
  0.6 1.0 copy-start.1
  1.7 1.0 copy-start.3
  2.7 1.0 copy-start.5
  3.8 45.8 %copy-start.9 = (f32[512,32]{0,1:T(8,128)S(1)}, f32[512,32]{0,1:T(8,128)}, u32[]{:S(2)}) copy-start(f32[512,32]{0,1:T(8,128)} %param.10) | copy-start | bytes 196612
  4.1 17.5 %collective-permute-start = (f32[256,512]{1,0:T(8,128)S(1)}, f32[256,512]{1,0:T(8,128)S(1)}, u32[]{:S(2)}, u32[]{:S(2)}) collective-permute-start(f32[256,512]{1,0:T(8,128)S(1)} %get-tuple-element.28), channel_id=1, source_target_pairs={{0,16},{16,0},{1,17},{17,1},{2,18},{18,2},{3,19},{19,3},{4,20},{20... | collective-permute-start | bytes 1572872 | tf_op jit(solution)/shard_map/ppermute | solution.py:25
  14.3 20.1 %all-to-all-start = ((bf16[16,16,512]{2,1,0:T(8,128)(2,1)}), bf16[16,16,512]{2,1,0:T(8,128)(2,1)S(1)}, u32[]{:S(2)}, u32[]{:S(2)}) async-start(bf16[16,16,512]{2,1,0:T(8,128)(2,1)} %broadcast_in_dim.9), calls=%async_computation | async-start | bytes 524288 | tf_op jit(solution)/shard_map/all_to_all | solution.py:29
  34.4 26.9 %copy-start.14 = (bf16[16,16,512]{2,1,0:T(8,128)(2,1)}, bf16[16,16,512]{2,1,0:T(8,128)(2,1)S(1)}, u32[]{:S(2)}) copy-start(bf16[16,16,512]{2,1,0:T(8,128)(2,1)S(1)} %all-to-all-done.my_ref) | copy-start | bytes 786436
  51.5 24.1 %all-to-all-start.2 = ((f32[32,16,128]{2,1,0:T(8,128)}), f32[32,16,128]{2,1,0:T(8,128)S(1)}, u32[]{:S(2)}, u32[]{:S(2)}) async-start(f32[32,16,128]{2,1,0:T(8,128)} %shard_map.94), calls=%async_computation.2 | async-start | bytes 524288 | tf_op jit(solution)/shard_map/all_to_all | solution.py:29
  57.7 17.9 %copy-start = (bf16[1,2048,512]{2,1,0:T(8,128)(2,1)S(1)}, bf16[1,2048,512]{2,1,0:T(8,128)(2,1)}, u32[]{:S(2)}) copy-start(bf16[1,2048,512]{2,1,0:T(8,128)(2,1)} %param.11) | copy-start | bytes 6291460
  57.7 3.6 %collective-permute-start.1 = (bf16[16,16,512]{2,1,0:T(8,128)(2,1)S(1)}, bf16[16,16,512]{2,1,0:T(8,128)(2,1)S(1)}, u32[]{:S(2)}, u32[]{:S(2)}) collective-permute-start(bf16[16,16,512]{2,1,0:T(8,128)(2,1)S(1)} %all-to-all-done.my_ref), channel_id=1, source_target_pairs={{0,16},{16,0},{1,17},{17,1},{2,18},{18,2},{3,19},{19,3},{4,20},{20... | collective-permute-start | bytes 786440 | tf_op jit(solution)/shard_map/ppermute | solution.py:25
  67.5 15.3 %collective-permute-start.2 = (bf16[8,128,256]{2,1,0:T(8,128)(2,1)}, bf16[8,128,256]{2,1,0:T(8,128)(2,1)S(1)}, u32[]{:S(2)}, u32[]{:S(2)}) collective-permute-start(bf16[8,128,256]{2,1,0:T(8,128)(2,1)} %get-tuple-element.40), channel_id=1, source_target_pairs={{0,2},{2,0},{4,6},{6,4},{8,10},{10,8},{12,14},{14,12},{1,3},{3,1},... | collective-permute-start | bytes 1572872 | tf_op jit(solution)/shard_map/ppermute | solution.py:342
  70.7 20.3 %collective-permute-start.3 = (bf16[8,128,256]{2,1,0:T(8,128)(2,1)}, bf16[8,128,256]{2,1,0:T(8,128)(2,1)S(1)}, u32[]{:S(2)}, u32[]{:S(2)}) collective-permute-start(bf16[8,128,256]{2,1,0:T(8,128)(2,1)} %get-tuple-element.41), channel_id=1, source_target_pairs={{0,14},{2,4},{4,2},{6,8},{8,6},{10,12},{12,10},{14,0},{1,15},{3,5}... | collective-permute-start | bytes 1572872 | tf_op jit(solution)/shard_map/ppermute | solution.py:343
  77.7 19.4 %all-to-all-start.3 = ((f32[16,48,128]{2,1,0:T(8,128)}), f32[16,48,128]{2,1,0:T(8,128)S(1)}, u32[]{:S(2)}, u32[]{:S(2)}) async-start(f32[16,48,128]{2,1,0:T(8,128)} %shard_map.95), calls=%async_computation.3 | async-start | bytes 786432 | tf_op jit(solution)/shard_map/all_to_all | solution.py:29
  82.8 8.1 %copy-start.10 = (bf16[8,128,256]{2,1,0:T(8,128)(2,1)}, bf16[8,128,256]{2,1,0:T(8,128)(2,1)S(1)}, u32[]{:S(2)}) copy-start(bf16[8,128,256]{2,1,0:T(8,128)(2,1)S(1)} %collective-permute-done.2) | copy-start | bytes 1572868
  94.8 47.7 %copy-start.2 = (bf16[1,512,512]{2,1,0:T(8,128)(2,1)S(1)}, bf16[1,512,512]{2,1,0:T(8,128)(2,1)}, u32[]{:S(2)}) copy-start(bf16[1,512,512]{2,1,0:T(8,128)(2,1)} %param.6) | copy-start | bytes 1572868
  94.8 47.7 %copy-start.4 = (bf16[512,512]{1,0:T(8,128)(2,1)S(1)}, bf16[512,512]{1,0:T(8,128)(2,1)}, u32[]{:S(2)}) copy-start(bf16[512,512]{1,0:T(8,128)(2,1)} %base_ref.3) | copy-start | bytes 1572868
  94.8 47.7 %copy-start.6 = (bf16[1,512,512]{2,1,0:T(8,128)(2,1)S(1)}, bf16[1,512,512]{2,1,0:T(8,128)(2,1)}, u32[]{:S(2)}) copy-start(bf16[1,512,512]{2,1,0:T(8,128)(2,1)} %param.9) | copy-start | bytes 1572868
  94.8 47.7 %copy-start.7 = (bf16[512,512]{1,0:T(8,128)(2,1)S(1)}, bf16[512,512]{1,0:T(8,128)(2,1)}, u32[]{:S(2)}) copy-start(bf16[512,512]{1,0:T(8,128)(2,1)} %get-tuple-element.36.full_ref) | copy-start | bytes 1572868
  94.8 47.7 %copy-start.8 = (bf16[512,16]{0,1:T(8,128)(2,1)S(1)}, bf16[512,16]{0,1:T(8,128)(2,1)}, u32[]{:S(2)}) copy-start(bf16[512,16]{0,1:T(8,128)(2,1)} %param.8) | copy-start | bytes 49156
  94.8 16.4 %collective-permute-start.4 = (bf16[4,128,512]{2,1,0:T(8,128)(2,1)}, bf16[4,128,512]{2,1,0:T(8,128)(2,1)}, u32[]{:S(2)}, u32[]{:S(2)}) collective-permute-start(bf16[4,128,512]{2,1,0:T(8,128)(2,1)} %get-tuple-element.43), channel_id=1, source_target_pairs={{0,1},{1,0},{2,3},{3,2},{4,5},{5,4},{6,7},{7,6},{8,9},{9,8},{10,11... | collective-permute-start | bytes 1572872 | tf_op jit(solution)/shard_map/ppermute | solution.py:25
  97.9 44.6 %all-to-all-start.4 = ((f32[32,16,128]{2,1,0:T(8,128)}), f32[32,16,128]{2,1,0:T(8,128)S(1)}, u32[]{:S(2)}, u32[]{:S(2)}) async-start(f32[32,16,128]{2,1,0:T(8,128)} %get-tuple-element.30), calls=%async_computation.4 | async-start | bytes 524288 | tf_op jit(solution)/shard_map/all_to_all | solution.py:29
  113.5 16.4 %collective-permute-start.5 = (bf16[2,128,512]{2,1,0:T(8,128)(2,1)}, bf16[2,128,512]{2,1,0:T(8,128)(2,1)S(1)}, u32[]{:S(2)}, u32[]{:S(2)}) collective-permute-start(bf16[2,128,512]{2,1,0:T(8,128)(2,1)} %get-tuple-element.45), channel_id=1, source_target_pairs={{0,4},{4,0},{1,5},{5,1},{2,6},{6,2},{3,7},{7,3},{8,12},{12,8},{9,1... | collective-permute-start | bytes 786440 | tf_op jit(solution)/shard_map/ppermute | solution.py:25
  132.6 13.7 %copy-start.12 = (f32[1,128,512]{2,1,0:T(8,128)S(1)}, f32[1,128,512]{2,1,0:T(8,128)}, u32[]{:S(2)}) copy-start(f32[1,128,512]{2,1,0:T(8,128)} %get-tuple-element.47) | copy-start | bytes 786436
  132.6 13.6 %collective-permute-start.6 = (bf16[1,128,512]{2,1,0:T(8,128)(2,1)}, bf16[1,128,512]{2,1,0:T(8,128)(2,1)}, u32[]{:S(2)}, u32[]{:S(2)}) collective-permute-start(bf16[1,128,512]{2,1,0:T(8,128)(2,1)} %get-tuple-element.48), channel_id=1, source_target_pairs={{0,8},{8,0},{1,9},{9,1},{2,10},{10,2},{3,11},{11,3},{4,12},{12,4},... | collective-permute-start | bytes 393224 | tf_op jit(solution)/shard_map/ppermute | solution.py:25
  (3 other events, 2.2 us)
